TPU v7x, 128 devices: a whole 4x4x4 slice. The times are simulated.
128 devices in a mesh: dp: 4 (over y), vocab: 32 (over z, x, core).
Axes of the slice: x: 4, y: 4, z: 4, core: 2. Of those that a mesh axis runs over, the one named last changes fastest.
Arguments:
- input_ids: int32 [1024], P('dp'), may hold values from 0 to 255999
- target_ids: int32 [1024], P('dp'), may hold values from 0 to 255999
- loss_mask: int32 [1024], P('dp'), may hold values 0 or 1
- final_hidden: bfloat16 [1024, 3584], P('dp'), may hold values from -5 to 5, as said below
- norm_gain: float32 [3584], replicated, may hold values from 0.25 to 1.75
- embed_cotangent: bfloat16 [1024, 3584], P('dp'), may hold values from -0.059814453 to 0.059814453
- table: bfloat16 [256000, 3584], P(('dp', 'vocab')), may hold values from -0.08351914 to 0.08351914, as said below
Outputs:
- embedded: bfloat16 [1024, 3584], P('dp')
- loss: float32 [], replicated
- grad_hidden: bfloat16 [1024, 3584], P('dp')
- gain_grad: float32 [3584], replicated
- table_grad: bfloat16 [256000, 3584], P(('dp', 'vocab'))
Inputs may be any that keep to these rules, and one draw needn't show every extreme that they name: Every entry of table lies within -5 / sqrt(3584) and 5 / sqrt(3584). Every entry of final_hidden lies within -5 and 5.
All inputs are finite; a program needn't handle non-finite values.
Results may differ from a plain program's by a relative error of at most 0.003.
Values may be sent and summed in bfloat16 or wider, within the bound.
A program may use at most 256 MiB of HBM per device.

v0:
```python
import functools
import math

import jax
import jax.numpy as jnp
from jax import lax
from jax.sharding import Mesh
from jax.sharding import PartitionSpec as P

SOFTCAP = 30
DP_VOCAB = ("dp", "vocab_0", "vocab_1", "vocab_2")
VOCAB = ("vocab_0", "vocab_1", "vocab_2")


EPSILON = 1e-06


def laid_out(parts, dim):
    lengths = list(parts.shape[1:])
    lengths[dim] *= parts.shape[0]
    return jnp.moveaxis(parts, 0, dim).reshape(lengths)


def gather_together(arrays, axis, dims):
    flat = jnp.concatenate([a.reshape(-1) for a in arrays])
    lines, at, finished = lax.all_gather(flat, axis), 0, []
    for a, dim in zip(arrays, dims):
        parts = lines[:, at : at + a.size].reshape(-1, *a.shape)
        finished.append(laid_out(parts, dim))
        at += a.size
    return tuple(finished)


def filled_up(lines, count):
    spare = -lines.shape[0] % count
    if not spare:
        return lines
    return jnp.concatenate([lines, jnp.zeros((spare, *lines.shape[1:]), lines.dtype)])


def sum_in_two_steps(array, axis):
    lines = array.reshape(-1, *array.shape[1:][-1:])
    padded = filled_up(lines, lax.axis_size(axis))
    own = lax.psum_scatter(padded, axis, scatter_dimension=0, tiled=True)
    whole = lax.all_gather(own, axis, axis=0, tiled=True)
    return whole[: len(lines)].reshape(array.shape)


def packed_total(arrays, axis):
    ends = [0]
    for a in arrays:
        ends.append(ends[-1] + a.size)
    so_far = lax.psum(jnp.concatenate([a.ravel() for a in arrays]), axis)
    return tuple(so_far[b:e].reshape(a.shape) for a, b, e in zip(arrays, ends, ends[1:]))


def over_axes(array, axes):
    return functools.reduce(lax.psum, axes, array)


def norm_backward(upstream, widened, inv_rms, norm_gain):
    scaled_up = upstream * norm_gain
    mean_dot = jnp.mean(scaled_up * widened, axis=1, keepdims=True)
    gradient = inv_rms * scaled_up - widened * (inv_rms * inv_rms * inv_rms) * mean_dot
    gain_part = jnp.sum(upstream * widened * inv_rms, axis=0)
    return (gradient.astype(jnp.bfloat16), gain_part)


def body(input_ids, target_ids, loss_mask, final_hidden, norm_gain, embed_cotangent, table):
    row_count = table.shape[0]
    embed_scale = math.sqrt(table.shape[1])
    owner = lax.axis_index(DP_VOCAB)
    first_row = owner * row_count
    every_id, every_target, every_mask = (
        lax.all_gather(input_ids, "dp", axis=0, tiled=True),
        lax.all_gather(target_ids, "dp", axis=0, tiled=True),
        lax.all_gather(loss_mask, "dp", axis=0, tiled=True),
    )
    token_total = every_id.shape[0]
    per_group = token_total // lax.axis_size("dp")
    share_rows = token_total // lax.axis_size(DP_VOCAB)
    widened = final_hidden.astype(jnp.float32)
    inv_rms = lax.rsqrt(jnp.mean(widened * widened, axis=1, keepdims=True) + EPSILON)
    normed = (widened * inv_rms * norm_gain).astype(jnp.bfloat16)
    normed_all, cotangent_all = gather_together((normed, embed_cotangent), "dp", (0, 0))

    def lookup_term():
        wanted = lax.slice_in_dim(every_id, 0, per_group * lax.axis_size("dp"), axis=0) - first_row
        inside = (wanted >= 0) & (wanted < row_count)
        picked = jnp.take(table, jnp.clip(wanted, 0, row_count - 1), axis=0)
        return jnp.where(inside[:, None], picked.astype(jnp.float32), 0.0)

    group_rows = lax.psum_scatter(
        lookup_term().astype(jnp.bfloat16), "dp", scatter_dimension=0, tiled=True
    ).astype(jnp.float32)
    found = sum_in_two_steps(group_rows.astype(jnp.bfloat16), VOCAB).astype(jnp.float32)
    embedded = (found * embed_scale).astype(jnp.bfloat16)
    raw_logits = lax.dot_general(
        normed_all, table, (((1,), (1,)), ((), ())), preferred_element_type=jnp.float32
    )
    capped = SOFTCAP * jnp.tanh(raw_logits / SOFTCAP)
    exp_logits = jnp.exp(capped)
    local_targets = every_target - first_row
    target_hit = lax.broadcasted_iota(jnp.int32, capped.shape, 1) == local_targets[:, None]
    token_weight = every_mask.astype(jnp.float32)
    picked_sum = jnp.sum(token_weight * jnp.sum(jnp.where(target_hit, capped, 0.0), axis=1))
    sum_exp, target_sum = packed_total((jnp.sum(exp_logits, axis=1), picked_sum), DP_VOCAB)
    loss = (jnp.sum(token_weight * jnp.log(sum_exp)) - target_sum) / jnp.maximum(
        jnp.sum(token_weight), 1.0
    )
    slope = (
        token_weight[:, None]
        * (exp_logits / sum_exp[:, None] - target_hit.astype(jnp.float32))
        * (1.0 - (capped / SOFTCAP) ** 2)
    )
    slope_low = slope.astype(jnp.bfloat16)
    head_part = lax.dot_general(
        slope_low, normed_all, (((0,), (0,)), ((), ())), preferred_element_type=jnp.float32
    )
    local_ids = every_id - first_row
    owned = (local_ids >= 0) & (local_ids < row_count)
    segment_ids = jnp.where(owned, local_ids, row_count)
    embed_part = (
        jax.ops.segment_sum(
            cotangent_all.astype(jnp.float32), segment_ids, num_segments=row_count + 1
        )[:row_count]
        * embed_scale
    )
    table_grad = (head_part + embed_part).astype(jnp.bfloat16)

    def upstream_term():
        block = lax.slice_in_dim(slope_low, 0, per_group * lax.axis_size("dp"), axis=0)
        return jnp.dot(block, table, preferred_element_type=jnp.float32)

    group_part = lax.psum_scatter(upstream_term(), "dp", scatter_dimension=0, tiled=True)
    upstream = lax.psum_scatter(group_part, VOCAB, scatter_dimension=0, tiled=True)
    offset_rows = lax.axis_index(VOCAB) * share_rows
    widened_share = lax.dynamic_slice_in_dim(widened, offset_rows, share_rows, 0)
    inv_share = lax.dynamic_slice_in_dim(inv_rms, offset_rows, share_rows, 0)
    gradient_share, gain_part = norm_backward(upstream, widened_share, inv_share, norm_gain)
    gain_grad = over_axes(gain_part, DP_VOCAB)
    grad_hidden = lax.all_gather(gradient_share, VOCAB, axis=0, tiled=True)
    return (embedded, loss, grad_hidden, gain_grad, table_grad)


def solution(mesh):
    finer = Mesh(
        mesh.devices.reshape(mesh.shape["dp"], 4, 4, 2), ("dp", "vocab_0", "vocab_1", "vocab_2")
    )
    placed = (P("dp"), P("dp"), P("dp"), P("dp", None), P(), P("dp", None), P(DP_VOCAB, None))
    return jax.shard_map(
        body,
        mesh=finer,
        in_specs=placed,
        out_specs=(P("dp", None), P(), P("dp", None), P(), P(DP_VOCAB, None)),
        check_vma=False,
    )
```

profile of v0, /device:TPU:1, one launch (start us, length us, event | category | flops | bytes accessed | tf_op | source)
XLA Modules:
  0.0 777.7 jit_solution(10020674517719600696)
XLA Ops:
  7.2 0.0 reduce-scatter.5.cloned.1.call-start
  7.2 9.0 %all-gather.1 = s32[4,1,256]{2,1,0:T(1,128)S(1)} all-gather(s32[1,1,256]{2,1,0:T(1,128)} %bitcast.25), channel_id=1, replica_groups=mesh['dp'=4,'vocab_0'=4,'vocab_1'=4,'vocab_2'=2] {'dp'}, dimensions={0}, use_global_device_ids=true | all-gather | bytes 5120 | tf_op jit(solution)/shard_map/all_gather | solution.py:75
  16.3 20.7 %gather_fusion = bf16[1024,3584]{1,0:T(8,128)(2,1)} fusion(bf16[2000,3584]{1,0:T(8,128)(2,1)} %param.13, s32[1024]{0:T(1024)S(1)} %get-tuple-element.16), kind=kCustom, calls=%fused_computation | custom fusion | bytes 14684160 | tf_op jit(solution)/shard_map/jit(_take)/gather | solution.py:90
  36.9 0.0 copy-start
  36.9 11.5 %select_convert_fusion = bf16[1024,3584]{1,0:T(8,128)(2,1)} fusion(bf16[1024,3584]{1,0:T(8,128)(2,1)} %gather_fusion, pred[1024]{0:T(1024)(128)(4,1)S(1)} %get-tuple-element.18, pred[1024]{0:T(1024)(128)(4,1)S(1)} %get-tuple-element.17), kind=kLoop, calls=%fused_computation.5 | loop fusion | flops 14680064 | bytes 14682112 | tf_op jit(solution)/shard_map/convert_element_type | solution.py:94
  48.4 0.0 copy-start.1
  48.4 0.0 reduce-scatter.5.cloned.1.call-update
  48.5 0.3 all-gather.12.cloned.1.call-start
  48.7 0.0 copy-done
  48.7 0.4 multiply_reduce_fusion
  49.2 0.0 copy-done.1
  49.2 1.7 multiply_convert_fusion.1
  50.9 4.6 reshape.61
  55.6 0.0 copy-start.2
  55.6 0.0 copy-start.3
  55.6 4.7 reshape.62
  60.2 5.0 pad_maximum_fusion
  65.2 0.0 all-gather.12.cloned.1.call-update
  65.3 0.0 reduce-scatter.7.cloned.1.call-start
  65.3 0.0 copy-done.2
  65.3 6.1 all-gather.2
  71.5 0.0 copy-done.3
  71.5 7.6 all-gather.3
  79.0 44.1 %reduce-scatter.5.cloned.1.call-done = bf16[256,3584]{1,0:T(8,128)(2,1)} async-done(((bf16[1024,3584]{1,0:T(8,128)(2,1)}), bf16[256,3584]{1,0:T(8,128)(2,1)}) %reduce-scatter.5.cloned.1.call-update) | async-done | bytes 1835024 | tf_op jit(solution)/shard_map/reduce_scatter | solution.py:93
  123.1 0.0 reduce-scatter.7.cloned.1.call-update
  123.1 0.0 reduce-scatter.9.cloned.1.call-start
  123.2 137.5 %all-gather.12.cloned.1.call-done = bf16[7340032]{0:T(1024)(128)(2,1)} async-done(((bf16[1835008]{0:T(1024)(128)(2,1)}), bf16[7340032]{0:T(1024)(128)(2,1)}) %all-gather.12.cloned.1.call-update) | async-done | bytes 14680080 | tf_op jit(solution)/shard_map/all_gather | solution.py:26
  260.6 17.6 %reshape.82 = bf16[4,1835008]{1,0:T(4,128)(2,1)} reshape(bf16[7340032]{0:T(1024)(128)(2,1)} %all-gather.12.cloned.1.call-done) | data formatting | bytes 29360128 | tf_op jit(solution)/shard_map/all_gather | solution.py:26
  278.3 15.0 %slice_convert_fusion = (f32[4,917504]{1,0:T(4,128)}, bf16[4,917504]{1,0:T(4,128)(2,1)}) fusion(bf16[4,1835008]{1,0:T(4,128)(2,1)} %reshape.82), kind=kLoop, calls=%fused_computation.13 | loop fusion | flops 3670016 | bytes 36700160 | tf_op jit(solution)/shard_map/convert_element_type | solution.py:125
  293.2 12.9 %reshape_reshape.4 = bf16[1024,3584]{1,0:T(8,128)(2,1)} reshape(bf16[4,917504]{1,0:T(4,128)(2,1)} %get-tuple-element.12) | data formatting | bytes 14680064 | tf_op jit(solution)/shard_map/reshape;reshape | solution.py:21
  306.1 23.0 %exponential_reduce_fusion = (f32[1024]{0:T(1024)S(1)}, f32[1024]{0:T(1024)S(1)}, f32[1024,2000]{0,1:T(8,128)}) fusion(s32[1024]{0:T(1024)S(1)} %bitcast.22, bf16[1024,3584]{1,0:T(8,128)(2,1)} %reshape_reshape.4, bf16[2000,3584]{1,0:T(8,128)(2,1)} %param.13), kind=kOutput, calls=%fused_computation.12 | convolution fusion | flops 14692349952 | bytes 29880320 | tf_op jit(solution)/shard_map/dot_general | solution.py:98
  329.1 0.6 multiply_reduce_fusion.4
  329.7 0.6 pad_maximum_fusion.1
  330.4 66.1 %psum.35 = f32[1025]{0:T(1024)S(1)} all-reduce(f32[1025]{0:T(1024)S(1)} %pad_maximum_fusion.1), channel_id=1, replica_groups=mesh['dp'=4,'vocab_0'=4,'vocab_1'=4,'vocab_2'=2] {'dp','vocab_0','vocab_..., use_global_device_ids=true, to_apply=%region_6.7 | all-reduce | flops 1025 | bytes 8200 | tf_op jit(solution)/shard_map/psum | solution.py:53
  396.4 0.6 fusion.7
  397.0 29.1 %fusion.6 = f32[1024,3584]{1,0:T(8,128)} fusion(bf16[2000,3584]{1,0:T(8,128)(2,1)} %param.13, f32[1024,2000]{0,1:T(8,128)} %get-tuple-element.19, f32[1024]{0:T(1024)S(1)} %get-tuple-element.13, f32[1024]{0:T(1024)S(1)} %bitcast.18, s32[1024]{0:T(1024)S(1)} %bitcast.23), kind=kOutput, calls=%fused_computation.36 | convolution fusion | flops 14702592000 | bytes 37220352 | tf_op jit(solution)/shard_map/dot_general | solution.py:133
  426.2 0.0 reduce-scatter.9.cloned.1.call-update
  426.2 0.0 all-gather.8.cloned.1.call-start
  426.2 0.0 reduce-scatter.7.cloned.1.call-done
  426.2 0.5 all-gather.8.cloned.1.call-update
  426.8 0.0 reduce-scatter.11.cloned.1.call-start
  426.8 127.8 %reduce-scatter.9.cloned.1.call-done = f32[256,3584]{1,0:T(8,128)} async-done(((f32[1024,3584]{1,0:T(8,128)}), f32[256,3584]{1,0:T(8,128)}) %reduce-scatter.9.cloned.1.call-update) | async-done | bytes 3670032 | tf_op jit(solution)/shard_map/reduce_scatter | solution.py:135
  554.6 0.0 reduce-scatter.11.cloned.1.call-update
  554.6 0.4 all-gather.10.cloned.1.call-start
  555.1 2.3 convert_element_type.46
  557.3 0.6 convert_reduce_fusion
  558.6 0.1 fusion.5
  558.7 41.6 %all-gather.8.cloned.1.call-done = bf16[256,3584]{1,0:T(8,128)(2,1)} async-done(((bf16[8,3584]{1,0:T(8,128)(2,1)}), bf16[256,3584]{1,0:T(8,128)(2,1)}) %all-gather.8.cloned.1.call-update) | async-done | bytes 1835024 | tf_op jit(solution)/shard_map/all_gather | solution.py:45
  600.3 3.0 multiply_convert_fusion.2
  603.4 0.5 slice.24
  603.9 28.9 %reshape.78 = f32[1024,3584]{1,0:T(8,128)} reshape(f32[4,917504]{1,0:T(4,128)} %get-tuple-element.11) | data formatting | bytes 29360128 | tf_op jit(solution)/shard_map/convert_element_type | solution.py:125
  634.1 35.3 %scatter_custom_fusion = f32[2001,3584]{1,0:T(8,128)} fusion(s32[1024]{0:T(1024)S(1)} %get-tuple-element.15, f32[1024,3584]{1,0:T(8,128)} %reshape.78, f32[]{:T(128)} %constant.28.clone.1), kind=kCustom, calls=%fused_computation.6 | custom fusion | flops 3670016 | bytes 28686848 | tf_op jit(solution)/shard_map/scatter-add | solution.py:124
  669.4 13.1 %reduce-scatter.11.cloned.1.call-done = f32[8,3584]{1,0:T(8,128)} async-done(((f32[256,3584]{1,0:T(8,128)}), f32[8,3584]{1,0:T(8,128)}) %reduce-scatter.11.cloned.1.call-update) | async-done | bytes 114704 | tf_op jit(solution)/shard_map/reduce_scatter | solution.py:136
  682.5 1.2 multiply_reduce_fusion.1
  683.7 1.7 subtract_convert_fusion
  685.3 0.0 all-gather.10.cloned.1.call-update
  685.4 26.8 %fusion.1 = bf16[2000,3584]{1,0:T(8,128)(2,1)} fusion(f32[2001,3584]{1,0:T(8,128)} %scatter_custom_fusion, bf16[1024,3584]{1,0:T(8,128)(2,1)} %reshape_reshape.4, f32[1024,2000]{0,1:T(8,128)} %get-tuple-element.19, f32[1024]{0:T(1024)S(1)} %get-tuple-element.13, f32[1024]{0:T(1024)S(1)} %bitcast.19, s32[1024]{0:T(1024)S(1)} %bitcast.24), kind=kOutput, calls=%fused_computation.4 | convolution fusion | flops 14724096000 | bytes 58552320 | tf_op jit(solution)/shard_map/dot_general | solution.py:117
  712.2 13.8 %psum.36 = f32[3584]{0:T(1024)S(1)} all-reduce(f32[3584]{0:T(1024)S(1)} %get-tuple-element.7), channel_id=1, replica_groups=mesh['dp'=4,'vocab_0'=4,'vocab_1'=4,'vocab_2'=2] {'dp'}, use_global_device_ids=true, to_apply=%region_13.14 | all-reduce | flops 3584 | bytes 28672 | tf_op jit(solution)/shard_map/psum | solution.py:58
  726.0 11.6 %psum.37 = f32[3584]{0:T(1024)S(1)} all-reduce(f32[3584]{0:T(1024)S(1)} %psum.36), channel_id=1, replica_groups=mesh['dp'=4,'vocab_0'=4,'vocab_1'=4,'vocab_2'=2] {'vocab_0'}, use_global_device_ids=true, to_apply=%region_14.15 | all-reduce | flops 3584 | bytes 28672 | tf_op jit(solution)/shard_map/psum | solution.py:58
  737.6 12.5 %psum.38 = f32[3584]{0:T(1024)S(1)} all-reduce(f32[3584]{0:T(1024)S(1)} %psum.37), channel_id=1, replica_groups=mesh['dp'=4,'vocab_0'=4,'vocab_1'=4,'vocab_2'=2] {'vocab_1'}, use_global_device_ids=true, to_apply=%region_15.16 | all-reduce | flops 3584 | bytes 28672 | tf_op jit(solution)/shard_map/psum | solution.py:58
  750.1 16.6 %psum.39 = f32[3584]{0:T(1024)} all-reduce(f32[3584]{0:T(1024)S(1)} %psum.38), channel_id=1, replica_groups=mesh['dp'=4,'vocab_0'=4,'vocab_1'=4,'vocab_2'=2] {'vocab_2'}, use_global_device_ids=true, to_apply=%region_16.17 | all-reduce | flops 3584 | bytes 28672 | tf_op jit(solution)/shard_map/psum | solution.py:58
  766.7 0.0 all-gather.10.cloned.1.call-done
  766.7 2.8 copy.13
  (7 shorter events, 0.0 us)
Async XLA Ops:
  7.2 115.9 %reduce-scatter.5.cloned.1.call-start = ((), (), s32[]{:S(2)}) async-start(), calls=%async_computation.4 | async-start | bytes 9175040 | tf_op jit(solution)/shard_map/reduce_scatter | solution.py:93
  36.9 11.8 %copy-start = (bf16[256,3584]{1,0:T(8,128)(2,1)S(1)}, bf16[256,3584]{1,0:T(8,128)(2,1)}, u32[]{:S(2)}) copy-start(bf16[256,3584]{1,0:T(8,128)(2,1)} %param.10) | copy-start | bytes 5505028
  48.4 0.8 copy-start.1
  48.5 212.2 %all-gather.12.cloned.1.call-start = ((), (), s32[]{:S(2)}) async-start(), calls=%async_computation.10 | async-start | bytes 18350080 | tf_op jit(solution)/shard_map/all_gather | solution.py:26
  55.6 9.8 %copy-start.2 = (s32[256]{0:T(256)S(1)}, s32[256]{0:T(256)}, u32[]{:S(2)}) copy-start(s32[256]{0:T(256)} %param.9) | copy-start | bytes 3076
  55.6 15.9 %copy-start.3 = (s32[256]{0:T(256)S(1)}, s32[256]{0:T(256)}, u32[]{:S(2)}) copy-start(s32[256]{0:T(256)} %param.8) | copy-start | bytes 3076
  65.3 361.0 %reduce-scatter.7.cloned.1.call-start = ((), (), s32[]{:S(2)}) async-start(), calls=%async_computation.5 | async-start | bytes 1892352 | tf_op jit(solution)/shard_map/reduce_scatter | solution.py:44
  123.1 431.5 %reduce-scatter.9.cloned.1.call-start = ((), (), s32[]{:S(2)}) async-start(), calls=%async_computation.7 | async-start | bytes 18350080 | tf_op jit(solution)/shard_map/reduce_scatter | solution.py:135
  426.2 174.2 %all-gather.8.cloned.1.call-start = ((), (), s32[]{:S(2)}) async-start(), calls=%async_computation.6 | async-start | bytes 1892352 | tf_op jit(solution)/shard_map/all_gather | solution.py:45
  426.8 255.7 %reduce-scatter.11.cloned.1.call-start = ((), (), s32[]{:S(2)}) async-start(), calls=%async_computation.8 | async-start | bytes 3784704 | tf_op jit(solution)/shard_map/reduce_scatter | solution.py:136
  554.6 212.1 %all-gather.10.cloned.1.call-start = ((), (), s32[]{:S(2)}) async-start(), calls=%async_computation.9 | async-start | bytes 1892352 | tf_op jit(solution)/shard_map/all_gather | solution.py:142
Sparse Core Ops, SparseCore 0:
  48.6 74.4 reduce-scatter.4
  124.8 135.8 all-gather.11
  264.2 78.4 reduce-scatter.6
  426.3 128.2 reduce-scatter.8
  556.7 43.5 all-gather.7
  603.9 78.5 reduce-scatter.10
  685.5 44.5 all-gather.9
where the time goes:
time: 785 us; the launch traced here: 778 us
  waiting for transfers between devices  365 us (46%)
  blocking collectives  143 us (18%)
  local copies, waits for them, and re-layouts  92.7 us (12%)
  other arithmetic  79.7 us (10%)
  matrix products  78.9 us (10%)
  between operations  17.6 us (2%)
    all_gather x1, waiting for transfers between devices, gather_together(): lines, at, finished = (lax.all_gather(flat, axis), 0, [])  137 us
    reduce_scatter x1, waiting for transfers between devices, body(): lax.psum_scatter(upstream_term(), 'dp', scatter_dimension=0, tiled=True)  128 us
    psum x1, blocking collectives, packed_total(): so_far = lax.psum(jnp.concatenate([a.ravel() for a in arrays]), axis)  66.1 us
    psum x4, blocking collectives, over_axes(): return functools.reduce(lax.psum, axes, array)  54.5 us
    reduce_scatter x1, waiting for transfers between devices, body(): lax.psum_scatter(lookup_term().astype(jnp.bfloat16), 'dp', scatter_dimens...  44.1 us
    all_gather x1, waiting for transfers between devices, sum_in_two_steps(): whole = lax.all_gather(own, axis, axis=0, tiled=True)  41.6 us
    scatter-add x1, other arithmetic, body(): jax.ops.segment_sum(cotangent_all.astype(jnp.float32), segment_ids, num_s...  35.3 us
    dot_general x1, matrix products, upstream_term(): return jnp.dot(block, table, preferred_element_type=jnp.float32)  29.1 us
  transfers between devices with their start and end apart: 7, of which 5 were waited for; matrix products, arithmetic and copies ran while one was open for 27% of the time, Pallas kernels for 0%

commit v1 on v0

v1 whole, which is shorter than its diff:
```python
import math

import jax
import jax.numpy as jnp
from jax import lax
from jax.experimental import pallas as pl
from jax.experimental.pallas import tpu as pltpu
from jax.sharding import Mesh
from jax.sharding import PartitionSpec as P

SOFTCAP = 30.0
EPSILON = 1e-06
D = 3584
ROWS = 2000
DP_VOCAB = ("dp", "vocab_0", "vocab_1", "vocab_2")
MESH = pl.DeviceIdType.MESH
BF = jnp.bfloat16
F32 = jnp.float32
NT = (((1,), (1,)), ((), ()))
TN = (((0,), (0,)), ((), ()))
NN = (((1,), (0,)), ((), ()))
MT = 400
NV = ROWS // MT
CT = 512
NT_COLS = D // CT
HALF = D // 2
VMEM_LIMIT = 66_500_000
TABLE_BOUND = 5.0 / math.sqrt(D) * 1.01


class Place:
    def __init__(self):
        self.y = lax.axis_index("dp")
        self.z = lax.axis_index("vocab_0")
        self.x = lax.axis_index("vocab_1")
        self.c = lax.axis_index("vocab_2")
        self.o = 1 - self.c
        y, z, x, c = self.y, self.z, self.x, self.c
        self.g = y + (y // 2) * (1 - 2 * (y % 2))
        self.ga = self.g + 1 - 2 * (self.g % 2)
        self.gb = (self.g + 2) % 4
        self.gc = (self.ga + 2) % 4
        self.a = x + c * (z - x)
        self.b = z + c * (x - z)
        self.bits = [
            (self.a + self.a // 2) % 2,
            self.a // 2,
            (self.b + self.b // 2) % 2,
            self.b // 2,
        ]
        self.r = self.bits[0] + 2 * self.bits[1] + 4 * self.bits[2] + 8 * self.bits[3]
        self.y_a = {"dp": y + 1 - 2 * (y % 2)}
        self.y_b = {"dp": 3 - y}
        self.core = {"vocab_2": self.o}
        self.mirror = {"vocab_0": x, "vocab_1": z, "vocab_2": self.o}
        self.plane = [self._in_plane(e) for e in range(4)]
        self.ring = {
            name: [{name: (i + off) % 4} for off in (1, 2, 3)]
            for name, i in (("vocab_1", x), ("vocab_0", z), ("dp", y))
        }
        self.ring_at = {"vocab_1": x, "vocab_0": z, "dp": y}
        self.cols = pl.ds(pl.multiple_of(c * HALF, 128), HALF)

    def _in_plane(self, e):
        a, b = self.a, self.b
        if e == 0:
            a = a + 1 - 2 * (a % 2)
        elif e == 1:
            a = 3 - a
        elif e == 2:
            b = b + 1 - 2 * (b % 2)
        else:
            b = 3 - b
        return {"vocab_1": a + self.c * (b - a), "vocab_0": b + self.c * (a - b)}

    def meet(self, mirror=False):
        peers = [self.core] + [d for name in self.ring for d in self.ring[name]]
        if mirror:
            peers.append(self.mirror)
        barrier = pltpu.get_barrier_semaphore()
        for peer in peers:
            pl.semaphore_signal(barrier, inc=1, device_id=peer, device_id_type=MESH)
        return lambda: pl.semaphore_wait(barrier, len(peers))


class Post:
    def __init__(self, send_sems, recv_sems):
        self.sems = (send_sems, recv_sems)
        self.used = 0
        self.open = []

    def send(self, src, dst, peer):
        copy = pltpu.make_async_remote_copy(
            src_ref=src,
            dst_ref=dst,
            send_sem=self.sems[0].at[self.used],
            recv_sem=self.sems[1].at[self.used],
            device_id=peer,
            device_id_type=MESH,
        )
        self.used += 1
        copy.start()
        self.open.append(copy)
        return copy

    def sent(self, copy):
        copy.wait_send()
        self.open = [c for c in self.open if c is not copy]

    def close(self):
        for copy in self.open:
            copy.wait_send()
        self.open = []


class Agenda:
    def __init__(self):
        self.now = 0.0
        self.todo = []
        self.count = 0

    def add(self, after, step):
        self.todo.append((self.now + after, self.count, step))
        self.count += 1

    def run(self, until=None):
        while self.todo:
            self.todo.sort(key=lambda item: item[:2])
            if until is not None and self.todo[0][0] > until:
                return
            when, _, step = self.todo.pop(0)
            self.now = max(self.now, when)
            step()

    def compute(self, cost, work):
        self.run(self.now)
        work()
        self.now += cost
        self.run(self.now)


def pick(dims, fixed):
    return tuple(fixed.get(d, slice(None)) for d in dims)


class Scatter:
    def __init__(self, place, post, agenda, tile, bufs, last):
        self.place, self.post, self.agenda = place, post, agenda
        self.bufs, self.last = bufs, last
        self.order = [(tile + i) % 4 for i in range(4)]
        self.dims = [3, 2, 1, 0]

    def start(self, held):
        self._send(held, 0)

    def _send(self, held, step):
        e = self.order[step]
        bit = self.place.bits[e]
        out = (slice(None),) + pick(self.dims, {e: 1 - bit})
        keep = (slice(None),) + pick(self.dims, {e: bit})
        target = self.bufs[step]
        copy = self.post.send(held.at[out], target, self.place.plane[e])
        wait = (5.5, 4.0, 3.2, 3.0)[step]

        def arrived():
            copy.wait_recv()
            if step < 3:
                target[...] = held[keep] + target[...]
                self.dims.remove(e)
                self._send(target, step + 1)
            else:
                self.last(held[keep] + target[...])

        self.agenda.add(wait, arrived)


def columns(table, j):
    at = j * CT // 2
    return jnp.concatenate([table[:, at : at + 256], table[:, HALF + at : HALF + at + 256]], axis=1)


def y_scatter(place, post, full, mid, end):
    low = place.g % 2
    high = place.g // 2
    copy = post.send(full.at[:, 1 - low], mid, place.y_a)
    copy.wait_recv()
    mid[...] = full[:, low] + mid[...]
    copy = post.send(mid.at[1 - high], end, place.y_b)
    copy.wait_recv()
    return mid[high] + end[...]


def head_kernel(
    meta, hidden, gain, table_hbm,
    capped_hbm, normed_hbm, stats_out, metas_out, found_out,
    table, normed, metas, onehot, cap_tiles, stage, rc, r1, r2, r3, r4, found, y_mid, y_end, stats, ring_in,
    local_sems, send_sems, recv_sems,
):
    place = Place()
    post = Post(send_sems, recv_sems)
    agenda = Agenda()
    first_row = (((place.y * 4 + place.z) * 4 + place.x) * 2 + place.c) * ROWS
    entered = place.meet()
    loads = []
    for i in range(NV):
        rows = pl.ds(i * MT, MT)
        load = pltpu.make_async_copy(table_hbm.at[rows], table.at[rows], local_sems.at[i])
        load.start()
        loads.append(load)

    g = place.g
    own = normed.at[g]

    def normalise(i, carry):
        rows = pl.ds(pl.multiple_of(i * 16, 16), 16)
        wide = hidden[rows, :].astype(F32)
        inv = lax.rsqrt(jnp.mean(wide * wide, axis=1, keepdims=True) + EPSILON)
        own[rows, :] = (wide * inv * gain[...]).astype(BF)
        return carry

    metas[g] = meta[...]
    lax.fori_loop(0, 16, normalise, 0)
    entered()

    low, high = pl.ds(0, 128), pl.ds(128, 128)
    meta_in = [
        post.send(metas.at[g], metas.at[g], peer) for peer in (place.y_a, place.y_b)
    ]

    def ship(block, rows, peer):
        part = normed.at[block, rows, place.cols]
        return post.send(part, part, peer)

    a_low = ship(g, low, place.y_a)
    b_high = ship(g, high, place.y_b)
    a_high = ship(g, high, place.y_a)
    b_low = ship(g, low, place.y_b)
    for copy in meta_in:
        copy.wait_recv()
    copy = post.send(metas.at[place.ga], metas.at[place.ga], place.y_b)
    copy.wait_recv()

    swaps = {}
    relays = {}

    def relay_low():
        a_low.wait_recv()
        relays["low"] = ship(place.ga, low, place.y_b)
        agenda.add(11, lambda: arrive("c_low", relays["low"], place.gc, low))

    def relay_high():
        b_high.wait_recv()
        relays["high"] = ship(place.gb, high, place.y_a)
        agenda.add(11, lambda: arrive("c_high", relays["high"], place.gc, high))

    def arrive(name, copy, block, rows):
        copy.wait_recv()
        swaps[name] = ship(block, rows, place.core)

    def arrive_a():
        a_high.wait_recv()
        swaps["a"] = ship(place.ga, pl.ds(0, 256), place.core)

    def arrive_b():
        b_low.wait_recv()
        swaps["b"] = ship(place.gb, pl.ds(0, 256), place.core)

    agenda.add(11.5, relay_low)
    agenda.add(11.5, relay_high)
    agenda.add(21.5, arrive_a)
    agenda.add(21.5, arrive_b)

    stats[...] = jnp.zeros_like(stats)
    stores = {}

    def forward(block, side, wait_loads=False):
        def tile(i, carry):
            rows = pl.ds(pl.multiple_of(i * MT, 16), MT)
            logits = lax.dot_general(
                table[rows, :], normed[block], NT, preferred_element_type=F32
            )
            capped = SOFTCAP * jnp.tanh(logits / SOFTCAP)
            ids = lax.broadcasted_iota(jnp.int32, capped.shape, 0) + (first_row + i * MT)
            hit = ids == metas[block, 1:2, :]
            total = jnp.sum(jnp.exp(capped), axis=0, keepdims=True)
            picked = jnp.sum(jnp.where(hit, capped, 0.0), axis=0, keepdims=True)
            stats[block, 0:1, :] += total
            stats[block, 1:2, :] += picked
            cap_tiles[side, rows, :] = capped
            return carry

        if wait_loads:
            for i in range(NV):
                loads[i].wait()
        if side in stores:
            stores.pop(side).wait()
        lax.fori_loop(0, NV, tile, 0)
        copy = pltpu.make_async_copy(cap_tiles.at[side], capped_hbm.at[block], local_sems.at[NV + side])
        copy.start()
        stores[side] = copy

    agenda.compute(5.2, lambda: forward(g, 0, True))

    def mark(i, carry):
        rows = pl.ds(pl.multiple_of(i * 16, 16), 16)
        ids = lax.broadcasted_iota(jnp.int32, (16, 256), 0) + (first_row + i * 16)
        for k in range(4):
            same = ids == metas[k, 0:1, :]
            onehot[rows, k * 256 : (k + 1) * 256] = jnp.where(same, 1.0, 0.0).astype(BF)
        return carry

    agenda.compute(1.5, lambda: lax.fori_loop(0, ROWS // 16, mark, 0))

    crossing = {}

    def look_up(j):
        slot = j % 2
        if j >= 2:
            post.sent(crossing[j - 2])
        product = lax.dot_general(
            onehot[...], columns(table, j), TN, preferred_element_type=F32
        ).astype(BF)
        shape = (4, 2, 2, 2, 2, 16, CT // 2)
        stage[slot, 0] = product[:, : CT // 2].reshape(shape)
        stage[slot, 1] = product[:, CT // 2 :].reshape(shape)
        crossing[j] = post.send(stage.at[slot, place.o], rc.at[j], place.core)

    def merge_up(j):
        crossing[j].wait_recv()
        rc[j] = stage[j % 2, place.c] + rc[j]

        def last(value):
            found[:, :, :, j * 256 : (j + 1) * 256] = value.reshape(2, 2, 16, 256)

        Scatter(
            place, post, agenda, j, [r1.at[j], r2.at[j], r3.at[j], r4.at[j]], last
        ).start(rc.at[j])

    def look(j):
        agenda.compute(2.5, lambda: look_up(j))
        agenda.add(0.0 if j == NT_COLS - 1 else 1.5, lambda: merge_up(j))
        if j >= 1:
            agenda.run(agenda.now + 0.0)

    looked = [0]

    def look_while(limit):
        while looked[0] < limit:
            j = looked[0]
            looked[0] += 1
            look(j)

    look_while(5)

    def need(name, work):
        while name not in swaps:
            agenda.run(agenda.todo[0][0] if agenda.todo else None)
        swaps[name].wait_recv()
        work()

    agenda.compute(5.2, lambda: need("a", lambda: forward(place.ga, 1)))
    agenda.compute(5.2, lambda: need("b", lambda: forward(place.gb, 0)))

    def both():
        need("c_low", lambda: None)
        need("c_high", lambda: forward(place.gc, 1))

    agenda.compute(5.2, both)


    def ring_start(name, base, peers, at):
        ring_in[base + at] = stats[...]
        return [
            post.send(ring_in.at[base + at], ring_in.at[base + at], peer) for peer in peers
        ]

    def ring_end(copies, base, count):
        for copy in copies:
            copy.wait_recv()
        total = ring_in[base]
        for i in range(1, count):
            total = total + ring_in[base + i]
        stats[...] = total

    core_copies = ring_start("core", 0, [place.core], place.c)
    base, copies, count = 0, core_copies, 2
    plan = [("vocab_1", 2), ("vocab_0", 6), ("dp", 10)]
    for name, nxt in plan:
        look_one = looked[0] < NT_COLS
        if look_one and base != 0:
            look_while(looked[0] + 1)
        ring_end(copies, base, count)
        copies = ring_start(name, nxt, place.ring[name], place.ring_at[name])
        base, count = nxt, 4
    look_while(NT_COLS)
    agenda.run()
    value = y_scatter(place, post, found, y_mid, y_end)
    found_out[...] = (value.astype(F32) * math.sqrt(D)).astype(BF)
    ring_end(copies, base, count)
    stats_out[...] = stats[...]
    metas_out[...] = metas[...]
    out = pltpu.make_async_copy(normed, normed_hbm, local_sems.at[0])
    out.start()
    for copy in stores.values():
        copy.wait()
    post.close()
    out.wait()


def back_kernel(
    capped_hbm, stats, metas, hidden, gain, cotangent, found, table_hbm,
    slope_hbm, cot_hbm, embed_hbm, grad_hbm, gain_out, loss_out,
    table, slope, cap_tiles, scale_rows, stage, rc, q0, r1, r2, r3, r4, up, y_mid, y_end,
    sums, grad, embed, ring_in, local_sems, send_sems, recv_sems,
):
    place = Place()
    post = Post(send_sems, recv_sems)
    agenda = Agenda()
    first_row = (((place.y * 4 + place.z) * 4 + place.x) * 2 + place.c) * ROWS
    g = place.g
    entered = place.meet(mirror=True)

    def cap_load(i):
        return pltpu.make_async_copy(
            capped_hbm.at[:, pl.ds(i * MT, MT)], cap_tiles.at[i % 2], local_sems.at[i % 2]
        )

    cap_load(0).start()
    cap_load(1).start()

    def table_load(j, h):
        cols = pl.ds(h * HALF + j * 256, 256)
        return pltpu.make_async_copy(
            table_hbm.at[:, cols], table.at[:, cols], local_sems.at[2 + 2 * j + h]
        )

    for j in range(NT_COLS):
        table_load(j, 0).start()
        table_load(j, 1).start()
    own_cot = pltpu.make_async_copy(cotangent, cot_hbm.at[g], local_sems.at[2 + 2 * NT_COLS])
    own_cot.start()

    def line(k, row):
        return metas[k, row : row + 1, :]

    weights = [line(k, 2).astype(F32) for k in range(4)]
    totals = [stats[k, 0:1, :] for k in range(4)]
    targets = [stats[k, 1:2, :] for k in range(4)]
    entered()

    low, high, whole = pl.ds(0, 128), pl.ds(128, 128), pl.ds(0, 256)

    def ship(src, block, rows, peer):
        return post.send(src, cot_hbm.at[block, rows, place.cols], peer)

    a_low = ship(cotangent.at[low, place.cols], g, low, place.y_a)
    b_high = ship(cotangent.at[high, place.cols], g, high, place.y_b)
    a_high = ship(cotangent.at[high, place.cols], g, high, place.y_a)
    b_low = ship(cotangent.at[low, place.cols], g, low, place.y_b)
    swaps = []

    def relay(copy, block, rows, peer, at):
        copy.wait_recv()
        part = cot_hbm.at[block, rows, place.cols]
        onward = post.send(part, part, peer)
        agenda.add(at, lambda: swap(onward, place.gc, rows))

    def swap(copy, block, rows):
        copy.wait_recv()
        part = cot_hbm.at[block, rows, place.cols]
        swaps.append(post.send(part, part, place.core))

    def swap_a():
        a_high.wait_recv()
        part = cot_hbm.at[place.ga, whole, place.cols]
        swaps.append(post.send(part, part, place.core))

    def swap_b():
        b_low.wait_recv()
        part = cot_hbm.at[place.gb, whole, place.cols]
        swaps.append(post.send(part, part, place.core))

    agenda.add(13.0, lambda: relay(a_low, place.ga, low, place.y_b, 12.0))
    agenda.add(13.0, lambda: relay(b_high, place.gb, high, place.y_a, 12.0))
    agenda.add(23.0, swap_a)
    agenda.add(23.0, swap_b)

    def doubling(buf, order, cols, base_wait, then):
        free = []

        def step(n):
            e = order[n]
            at = pick([3, 2, 1, 0], {d: place.bits[d] for d in range(4) if d not in free})
            part = buf.at[at + (slice(None), cols)]
            copy = post.send(part, part, place.plane[e])
            free.append(e)

            def arrived():
                copy.wait_recv()
                if n < 3:
                    step(n + 1)
                else:
                    then()

            agenda.add(base_wait + 0.4 * (1 << n), arrived)

        step(0)

    colour = [
        ((0, 1, 2, 3), pl.ds(pl.multiple_of(place.c * HALF, 128), HALF // 2)),
        ((1, 0, 3, 2), pl.ds(pl.multiple_of(place.c * HALF + HALF // 2, 128), HALF // 2)),
    ]
    mine = tuple(place.bits[d] for d in (3, 2, 1, 0))
    gathered = {"embed": 0, "grad": 0}
    final = []

    def gather_all(buf, name, wait):
        def one_done():
            gathered[name] += 1
            if gathered[name] == 2:
                part = buf.at[:, :, :, :, :, place.cols]
                final.append(post.send(part, part, place.core))

        for order, cols in colour:
            doubling(buf, order, cols, wait, one_done)

    embed[mine + (slice(None), place.cols)] = found[...]
    gather_all(embed, "embed", 3.0)

    factors = [w / s for w, s in zip(weights, totals)]

    def slopes(i):
        cap_load(i).wait()

        def slab(n, carry):
            rows = pl.ds(pl.multiple_of(n * 16, 16), 16)
            ids = lax.broadcasted_iota(jnp.int32, (16, 256), 0) + (first_row + i * MT + n * 16)
            for k in range(4):
                capped = cap_tiles[i % 2, k, rows, :]
                hit = jnp.where(ids == line(k, 1), weights[k], 0.0)
                ratio = capped * (1.0 / SOFTCAP)
                value = (jnp.exp(capped) * factors[k] - hit) * (1.0 - ratio * ratio)
                slope[pl.ds(pl.multiple_of(i * MT + n * 16, 16), 16), k * 256 : (k + 1) * 256] = (
                    value.astype(BF)
                )
            return carry

        lax.fori_loop(0, MT // 16, slab, 0)
        if i + 2 < NV:
            cap_load(i + 2).start()

    for i in range(NV):
        agenda.compute(1.2, lambda: slopes(i))
    slope_store = pltpu.make_async_copy(slope, slope_hbm, local_sems.at[0])
    slope_store.start()

    bound = []
    for k in range(4):
        rest = jnp.maximum(1.0 - jnp.exp(targets[k]) / totals[k], 0.0)
        bound.append(TABLE_BOUND * (2.0 * rest + 1e-4))
    for k in range(4):
        up_scale = jnp.broadcast_to(32600.0 / bound[k], (128, 256))
        scale_rows[0, k * 16 : (k + 1) * 16] = up_scale.T.reshape(16, 16, 128)
        down = jnp.broadcast_to(bound[k] * (1.0 / 32600.0), (128, 256))
        scale_rows[1, k * 16 : (k + 1) * 16] = down.T.reshape(16, 16, 128)

    weight_sum = sum(jnp.sum(w) for w in weights)
    loss_sum = sum(
        jnp.sum(w * (jnp.log(s) - t)) for w, s, t in zip(weights, totals, targets)
    )
    loss_out[...] = jnp.full((8, 128), loss_sum / jnp.maximum(weight_sum, 1.0), F32)

    crossing = {}

    def pull(j):
        slot = j % 2
        if j >= 2:
            post.sent(crossing[j - 2])
        table_load(j, 0).wait()
        table_load(j, 1).wait()
        product = lax.dot_general(
            slope[...], columns(table, j), TN, preferred_element_type=F32
        )
        stage[slot, 0] = product[:, : CT // 2].reshape(64, 16, CT // 2)
        stage[slot, 1] = product[:, CT // 2 :].reshape(64, 16, CT // 2)
        crossing[j] = post.send(stage.at[slot, place.o], rc.at[j], place.core)

    def merge(j):
        crossing[j].wait_recv()

        def slab(n, carry):
            for side in range(2):
                cols = slice(side * 128, side * 128 + 128)
                rows = pl.ds(n * 4, 4)
                total = stage[j % 2, place.c, rows, :, cols] + rc[j, rows, :, cols]
                fixed = jnp.round(total * scale_rows[0, rows])
                q0[j, rows, :, cols] = fixed.astype(jnp.int32).astype(jnp.int16)
            return carry

        lax.fori_loop(0, 16, slab, 0)

        def last(value):
            up[:, :, :, j * 256 : (j + 1) * 256] = value.reshape(2, 2, 16, 256)

        held = q0.at[j].reshape(4, 2, 2, 2, 2, 16, 256)
        Scatter(
            place, post, agenda, j, [r1.at[j], r2.at[j], r3.at[j], r4.at[j]], last
        ).start(held)

    def turn(j):
        agenda.compute(2.5, lambda: pull(j))
        agenda.add(1.8, lambda: merge(j))

    for j in range(NT_COLS):
        turn(j)
    agenda.run()

    fixed = y_scatter(place, post, up, y_mid, y_end)
    back = scale_rows[1, g * 16 + place.r]
    upstream = fixed.astype(jnp.int32).astype(F32) * jnp.concatenate([back] * (HALF // 128), axis=1)
    own_rows = pl.ds(pl.multiple_of(place.r * 16, 16), 16)
    wide_all = hidden[own_rows, :].astype(F32)
    inv = lax.rsqrt(jnp.mean(wide_all * wide_all, axis=1, keepdims=True) + EPSILON)
    wide = hidden[own_rows, place.cols].astype(F32)
    scaled_up = upstream * gain[:, place.cols]
    dot = jnp.sum(scaled_up * wide, axis=1, keepdims=True)
    sums[0] = jnp.broadcast_to(dot, (16, 128))
    other = post.send(sums.at[0], sums.at[1], place.mirror)

    part = jnp.sum(upstream * wide * inv, axis=0, keepdims=True)
    lane = jnp.concatenate([part[:, i * 128 : (i + 1) * 128] for i in range(HALF // 128)], axis=0)

    def ring_start(base, name):
        at = base + place.ring_at[name]
        return [post.send(ring_in.at[at], ring_in.at[at], peer) for peer in place.ring[name]]

    ring_in[place.x, 0 : HALF // 128] = lane
    copies = ring_start(0, "vocab_1")

    other.wait_recv()
    mean_dot = (sums[0, :, 0:1] + sums[1, :, 0:1]) * (1.0 / D)
    value = inv * scaled_up - wide * (inv * inv * inv) * mean_dot
    grad[mine + (slice(None), place.cols)] = value.astype(BF)
    gather_all(grad, "grad", 2.4)

    def ring_turn(copies, base, nxt, name):
        for copy in copies:
            copy.wait_recv()
        total = ring_in[base, 0:14]
        for i in range(1, 4):
            total = total + ring_in[base + i, 0:14]
        if name is None:
            ring_in[nxt + place.c, 0:14] = total
            at = ring_in.at[nxt + place.c]
            copy = post.send(at, at, place.core)
            agenda.add(1.5, copy.wait_recv)
            return
        ring_in[nxt + place.ring_at[name], 0:14] = total
        onward = ring_start(nxt, name)
        then = {"vocab_0": (8, "dp"), "dp": (12, None)}[name]
        agenda.add(3.2, lambda: ring_turn(onward, nxt, *then))

    agenda.add(2.5, lambda: ring_turn(copies, 0, 4, "vocab_0"))
    agenda.run()
    for copy in final:
        copy.wait_recv()
    outs = [
        pltpu.make_async_copy(embed, embed_hbm, local_sems.at[1]),
        pltpu.make_async_copy(grad, grad_hbm, local_sems.at[2]),
    ]
    for copy in outs:
        copy.start()
    gain_out[0] = ring_in[12]
    gain_out[1] = ring_in[13]
    for copy in swaps:
        copy.wait_recv()
    own_cot.wait()
    slope_store.wait()
    post.close()
    for copy in outs:
        copy.wait()


def table_kernel(slope, normed, cot, ids, out):
    first = (
        lax.axis_index(DP_VOCAB) * ROWS + pl.program_id(0) * MT
    )
    rows = lax.broadcasted_iota(jnp.int32, (MT, 256), 0) + first
    mark = jnp.concatenate(
        [jnp.where(rows == ids[k, 0:1, :], 1.0, 0.0).astype(BF) for k in range(4)], axis=1
    )
    for h in range(2):
        cols = slice(h * HALF, (h + 1) * HALF)
        head = lax.dot_general(slope[...], normed[:, cols], NN, preferred_element_type=F32)
        part = lax.dot_general(mark, cot[:, cols], NN, preferred_element_type=F32)
        out[:, cols] = (head + part * math.sqrt(D)).astype(BF)


def body(input_ids, target_ids, loss_mask, final_hidden, norm_gain, embed_cotangent, table):
    any_ = pl.BlockSpec(memory_space=pl.ANY)
    vmem = pl.BlockSpec(memory_space=pltpu.VMEM)
    dma = pltpu.SemaphoreType.DMA
    meta = jnp.pad(jnp.stack([input_ids, target_ids, loss_mask]), ((0, 5), (0, 0)))
    gain = norm_gain.reshape(1, D)
    S = jax.ShapeDtypeStruct

    def params(cid):
        return pltpu.CompilerParams(
            collective_id=cid, has_side_effects=True, vmem_limit_bytes=VMEM_LIMIT
        )

    def halving(n, dt):
        shapes = [(n, 4, 2, 2, 2, 16, 256), (n, 4, 2, 2, 16, 256), (n, 4, 2, 16, 256), (n, 4, 16, 256)]
        return [pltpu.VMEM(s, dt) for s in shapes]

    capped, normed, stats, metas, found = pl.pallas_call(
        head_kernel,
        out_shape=(
            S((4, ROWS, 256), F32),
            S((4, 256, D), BF),
            S((4, 2, 256), F32),
            S((4, 8, 256), jnp.int32),
            S((16, HALF), BF),
        ),
        in_specs=[vmem, vmem, vmem, any_],
        out_specs=(any_, any_, vmem, vmem, vmem),
        scratch_shapes=[
            pltpu.VMEM((ROWS, D), BF),
            pltpu.VMEM((4, 256, D), BF),
            pltpu.VMEM((4, 8, 256), jnp.int32),
            pltpu.VMEM((ROWS, 1024), BF),
            pltpu.VMEM((2, ROWS, 256), F32),
            pltpu.VMEM((2, 2, 4, 2, 2, 2, 2, 16, 256), BF),
            pltpu.VMEM((NT_COLS, 4, 2, 2, 2, 2, 16, 256), BF),
            *halving(NT_COLS, BF),
            pltpu.VMEM((2, 2, 16, HALF), BF),
            pltpu.VMEM((2, 16, HALF), BF),
            pltpu.VMEM((16, HALF), BF),
            pltpu.VMEM((4, 2, 256), F32),
            pltpu.VMEM((14, 4, 2, 256), F32),
            dma((NV + 2,)),
            dma((64,)),
            dma((64,)),
        ],
        compiler_params=params(0),
        name="head",
    )(meta, final_hidden, gain, table)

    slope, cot, embed, grad, gain_parts, loss = pl.pallas_call(
        back_kernel,
        out_shape=(
            S((ROWS, 1024), BF),
            S((4, 256, D), BF),
            S((2, 2, 2, 2, 16, D), BF),
            S((2, 2, 2, 2, 16, D), BF),
            S((2, 16, 128), F32),
            S((8, 128), F32),
        ),
        in_specs=[any_, vmem, vmem, vmem, vmem, vmem, vmem, any_],
        out_specs=(any_, any_, any_, any_, vmem, vmem),
        scratch_shapes=[
            pltpu.VMEM((ROWS, D), BF),
            pltpu.VMEM((ROWS, 1024), BF),
            pltpu.VMEM((2, 4, MT, 256), F32),
            pltpu.VMEM((2, 64, 16, 128), F32),
            pltpu.VMEM((2, 2, 64, 16, 256), F32),
            pltpu.VMEM((NT_COLS, 64, 16, 256), F32),
            pltpu.VMEM((NT_COLS, 64, 16, 256), jnp.int16),
            *halving(NT_COLS, jnp.int16),
            pltpu.VMEM((2, 2, 16, HALF), jnp.int16),
            pltpu.VMEM((2, 16, HALF), jnp.int16),
            pltpu.VMEM((16, HALF), jnp.int16),
            pltpu.VMEM((2, 16, 128), F32),
            pltpu.VMEM((2, 2, 2, 2, 16, D), BF),
            pltpu.VMEM((2, 2, 2, 2, 16, D), BF),
            pltpu.VMEM((14, 16, 128), F32),
            dma((3 + 2 * NT_COLS,)),
            dma((96,)),
            dma((96,)),
        ],
        compiler_params=params(1),
        name="back",
    )(capped, stats, metas, final_hidden, gain, embed_cotangent, found, table)

    table_grad = pl.pallas_call(
        table_kernel,
        grid=(NV,),
        out_shape=S((ROWS, D), BF),
        in_specs=[
            pl.BlockSpec((MT, 1024), lambda i: (i, 0)),
            pl.BlockSpec((1024, D), lambda i: (0, 0)),
            pl.BlockSpec((1024, D), lambda i: (0, 0)),
            pl.BlockSpec((4, 8, 256), lambda i: (0, 0, 0)),
        ],
        out_specs=pl.BlockSpec((MT, D), lambda i: (i, 0)),
        compiler_params=pltpu.CompilerParams(vmem_limit_bytes=VMEM_LIMIT),
        name="table_grad",
    )(slope, normed.reshape(1024, D), cot.reshape(1024, D), metas)
    return (
        embed.reshape(256, D),
        loss[0, 0],
        grad.reshape(256, D),
        gain_parts[:, : HALF // 128].reshape(D),
        table_grad,
    )


def solution(mesh):
    finer = Mesh(
        mesh.devices.reshape(mesh.shape["dp"], 4, 4, 2), ("dp", "vocab_0", "vocab_1", "vocab_2")
    )
    placed = (P("dp"), P("dp"), P("dp"), P("dp", None), P(), P("dp", None), P(DP_VOCAB, None))
    return jax.shard_map(
        body,
        mesh=finer,
        in_specs=placed,
        out_specs=(P("dp", None), P(), P("dp", None), P(), P(DP_VOCAB, None)),
        check_vma=False,
    )
```

time: 785 us -> 237 us (0.30)
  waiting for transfers between devices: 365 us -> 0 us
  Pallas kernels: 0 us -> 226 us
  blocking collectives: 143 us -> 0 us
  local copies, waits for them, and re-layouts: 92.7 us -> 8.66 us
  other arithmetic: 79.7 us -> 0.72 us
  matrix products: 78.9 us -> 0 us
  between operations: 17.6 us -> 0.65 us
    pallas_call x0 -> x3, Pallas kernels: none -> 226 us  [the longest x1 100 us: body(): pl.pallas_call(head_kernel, out_shape=(S((4, ROWS, 256), F32), S((4, 256,...]
    reduce_scatter x4 -> x0, waiting for transfers between devices: 185 us -> none  [the longest x1 128 us: body(): lax.psum_scatter(upstream_term(), 'dp', scatter_dimension=0, tiled=True)]
    all_gather x3 -> x0, waiting for transfers between devices: 179 us -> none  [the longest x1 137 us: gather_together(): lines, at, finished = (lax.all_gather(flat, axis), 0, [])]
    psum x5 -> x0, blocking collectives: 121 us -> none  [the longest x1 66.1 us: packed_total(): so_far = lax.psum(jnp.concatenate([a.ravel() for a in arrays]), axis)]
    dot_general x3 -> x0, matrix products: 78.9 us -> none  [the longest x1 29.1 us: upstream_term(): return jnp.dot(block, table, preferred_element_type=jnp.float32)]
    scatter-add x1 -> x0, other arithmetic: 35.3 us -> none  [body(): jax.ops.segment_sum(cotangent_all.astype(jnp.float32), segment_ids, num_s...]
    convert_element_type x7 -> x0, other arithmetic: 35.2 us -> none  [the longest x1 15 us: body(): cotangent_all.astype(jnp.float32)]
    convert_element_type x1 -> x0, local copies, waits for them, and re-layouts: 28.9 us -> none  [body(): cotangent_all.astype(jnp.float32)]
  transfers between devices with their start and end apart: 7 -> 0, of which waited for: 5 -> 0; matrix products, arithmetic and copies ran while one was open for 27% -> 0% of each run, Pallas kernels for 0% -> 0%
where the time goes in v1:
time: 237 us; the launch traced here: 236 us
  Pallas kernels  226 us (95%)
  local copies, waits for them, and re-layouts  8.66 us (4%)
    pallas_call x1, Pallas kernels, body(): pl.pallas_call(head_kernel, out_shape=(S((4, ROWS, 256), F32), S((4, 256,...  100 us
    pallas_call x1, Pallas kernels, body(): pl.pallas_call(back_kernel, out_shape=(S((ROWS, 1024), BF), S((4, 256, D)...  88.5 us
    pallas_call x1, Pallas kernels, body(): pl.pallas_call(table_kernel, grid=(NV,), out_shape=S((ROWS, D), BF), in_s...  37.6 us

profile of v1, /device:TPU:1, one launch (start us, length us, event | category | flops | bytes accessed | tf_op | source)
XLA Modules:
  0.0 236.4 jit_solution(13331968894134303406)
XLA Ops:
  0.6 0.7 pad_add_fusion
  1.4 0.6 pad.4.meta
  2.0 1.3 reshape.28.gain
  3.3 100.3 %head.1 = (f32[4,2000,256]{2,1,0:T(8,128)}, bf16[4,256,3584]{2,1,0:T(8,128)(2,1)}, f32[4,2,256]{2,1,0:T(2,128)}, s32[4,8,256]{2,1,0:T(8,128)}, bf16[16,1792]{1,0:T(8,128)(2,1)}) custom-call(s32[8,256]{1,0:T(8,128)} %pad.4.meta, bf16[256,3584]{1,0:T(8,128)(2,1)} %hidden.3, f32[1,3584]{1,0:T(1,128)} %reshape.28.gain, bf16[2000,3584]{1,0:T(8,128)(2,1)} %table_hbm.3), custom_call_target="tpu_custom_call" | custom-call | tf_op jit(solution)/shard_map/head/pallas_call | solution.py:716
  103.6 88.5 %back.1 = (bf16[2000,1024]{1,0:T(8,128)(2,1)}, bf16[4,256,3584]{2,1,0:T(8,128)(2,1)}, bf16[2,2,2,2,16,3584]{5,4,3,2,1,0:T(8,128)(2,1)}, bf16[2,2,2,2,16,3584]{5,...) custom-call(f32[4,2000,256]{2,1,0:T(8,128)} %get-tuple-element.16.capped_hbm, ...), custom_call_target="tpu_custom_call" | custom-call | tf_op jit(solution)/shard_map/back/pallas_call | solution.py:749
  192.1 1.2 slice.6
  193.3 1.3 reshape.31
  194.6 37.6 %table_grad.1 = bf16[2000,3584]{1,0:T(8,128)(2,1)} custom-call(bf16[2000,1024]{1,0:T(8,128)(2,1)} %get-tuple-element.24.slope, bf16[1024,3584]{1,0:T(8,128)(2,1)} %bitcast.9, bf16[1024,3584]{1,0:T(8,128)(2,1)} %bitcast.10, s32[4,8,256]{2,1,0:T(8,128)} %get-tuple-element.18.metas.ids), custom_call_target="tpu_custom_call" | custom-call | tf_op jit(solution)/shard_map/table_grad/pallas_call | solution.py:785
  232.2 0.0 copy-start
  232.2 3.0 %copy.14 = bf16[256,3584]{1,0:T(8,128)(2,1)} copy(bf16[256,3584]{1,0:T(8,128)(2,1)} %bitcast.12) | data formatting | bytes 3670016
  235.2 0.0 copy-done
  235.2 1.2 copy.15
Async XLA Ops:
  232.2 3.0 %copy-start = (bf16[2,2,2,2,16,3584]{5,4,3,2,1,0:T(8,128)(2,1)S(1)}, bf16[2,2,2,2,16,3584]{5,4,3,2,1,0:T(8,128)(2,1)}, u32[]{:S(2)}) copy-start(bf16[2,2,2,2,16,3584]{5,4,3,2,1,0:T(8,128)(2,1)} %get-tuple-element.22) | copy-start | bytes 5505028

commit v2 on v0

v2 whole, which is shorter than its diff:
```python
import math

import jax
import jax.numpy as jnp
from jax import lax
from jax.experimental import pallas as pl
from jax.experimental.pallas import tpu as pltpu
from jax.sharding import Mesh
from jax.sharding import PartitionSpec as P

SOFTCAP = 30.0
EPSILON = 1e-06
D = 3584
ROWS = 2000
EMBED_SCALE = math.sqrt(D)
DP_VOCAB = ("dp", "vocab_0", "vocab_1", "vocab_2")
MESH = pl.DeviceIdType.MESH
BF = jnp.bfloat16
F32 = jnp.float32
I16 = jnp.int16
NT = (((1,), (1,)), ((), ()))
TN = (((0,), (0,)), ((), ()))
NN = (((1,), (0,)), ((), ()))
MT = 400
MF = 256
NV = ROWS // MT
HALF = D // 2
W = 256
NT_COLS = HALF // W
CHUNK = 32
D_START = 24.0
VMEM_LIMIT = 66_900_000
TABLE_BOUND = 5.0 / math.sqrt(D) * 1.01
UNITS = 24000.0
KNEE = 256.0
FINE = 32.0


def encode(value):
    bent = jnp.clip(value, -KNEE, KNEE)
    return jnp.round(value + bent * (FINE - 1.0)).astype(jnp.int32).astype(I16)


def decode(code):
    wide = code.astype(jnp.int32).astype(F32)
    return wide - jnp.clip(wide, -KNEE * FINE, KNEE * FINE) * (1.0 - 1.0 / FINE)


def gray(i):
    return i + (i // 2) * (1 - 2 * (i % 2))


class Place:
    def __init__(self):
        self.y = y = lax.axis_index("dp")
        self.z = z = lax.axis_index("vocab_0")
        self.x = x = lax.axis_index("vocab_1")
        self.c = c = lax.axis_index("vocab_2")
        self.o = 1 - c
        self.first_row = (((y * 4 + z) * 4 + x) * 2 + c) * ROWS
        self.g = gray(y)
        self.ga = self.g + 1 - 2 * (self.g % 2)
        self.gb = (self.g + 2) % 4
        self.gc = (self.ga + 2) % 4
        self.y_a = {"dp": y + 1 - 2 * (y % 2)}
        self.y_b = {"dp": 3 - y}
        self.core = {"vocab_2": self.o}
        self.a = x + c * (z - x)
        self.b = z + c * (x - z)
        self.a_peers = [self._at((self.a + off) % 4, self.b) for off in (1, 2, 3)]
        self.b_peers = [self._at(self.a, (self.b + off) % 4) for off in (1, 2, 3)]
        self.x_peers = [{"vocab_1": (x + off) % 4} for off in (1, 2, 3)]
        self.z_peers = [{"vocab_0": (z + off) % 4} for off in (1, 2, 3)]
        self.y_peers = [{"dp": (y + off) % 4} for off in (1, 2, 3)]
        self.cols = pl.ds(pl.multiple_of(c * HALF, 128), HALF)
        self.tiles = [self.tile_cols(j) for j in range(NT_COLS)]
        self.a_at = [(self.a + off) % 4 for off in (1, 2, 3)]
        self.b_at = [(self.b + off) % 4 for off in (1, 2, 3)]
        self.y_at = [gray((y + off) % 4) for off in (1, 2, 3)]
        a, b = self.a, self.b
        a0, a1, b0 = (a + a // 2) % 2, a // 2, (b + b // 2) % 2
        self.colour = (a0 + b0) % 2 + 2 * ((a1 + b0) % 2)
        flip_a, flip_b = a + 1 - 2 * (a % 2), b + 1 - 2 * (b % 2)
        self.near = [self._at(flip_a, b), self._at(3 - a, b), self._at(a, flip_b)]

    def _at(self, a, b):
        return {"vocab_1": a + self.c * (b - a), "vocab_0": b + self.c * (a - b)}

    def tile_cols(self, j, core=None):
        core = self.c if core is None else core
        return pl.ds(pl.multiple_of(core * HALF + j * W, 128), W)

    def meet(self):
        peers = [self.core] + self.x_peers + self.z_peers + self.y_peers
        barrier = pltpu.get_barrier_semaphore()
        for peer in peers:
            pl.semaphore_signal(barrier, inc=1, device_id=peer, device_id_type=MESH)
        return lambda: pl.semaphore_wait(barrier, len(peers))


class Sent:
    def __init__(self, sems, at, out_like, in_like, times):
        self.sems, self.at = sems, at
        self.out_like, self.in_like, self.times = out_like, in_like, times

    def wait_send(self):
        for _ in range(self.times):
            like = self.out_like()
            pltpu.make_async_copy(like, like, self.sems[0].at[self.at]).wait()

    def wait_recv(self):
        like = self.in_like()
        pltpu.make_async_copy(like, like, self.sems[1].at[self.at]).wait()


class Post:
    def __init__(self, send_sems, recv_sems):
        self.sems = (send_sems, recv_sems)
        self.used = 0
        self.open = []

    def send(self, src, dst, peer):
        return self.group([(src, dst, peer)], src, dst)

    def group(self, parts, out_like, in_like, times=1):
        for src, dst, peer in parts:
            pltpu.make_async_remote_copy(
                src_ref=src(),
                dst_ref=dst(),
                send_sem=self.sems[0].at[self.used],
                recv_sem=self.sems[1].at[self.used],
                device_id=peer,
                device_id_type=MESH,
            ).start()
        sent = Sent(self.sems, self.used, out_like, in_like, times)
        self.used += 1
        self.open.append(sent)
        return sent

    def sent(self, item):
        item.wait_send()
        self.open = [c for c in self.open if c is not item]

    def close(self):
        for item in self.open:
            item.wait_send()
        self.open = []


class Agenda:
    def __init__(self):
        self.now = 0.0
        self.todo = []
        self.count = 0

    def add(self, after, step):
        self.todo.append((self.now + after, self.count, step))
        self.count += 1

    def run(self, until=None):
        while self.todo:
            self.todo.sort(key=lambda item: item[:2])
            if until is not None and self.todo[0][0] > until:
                return
            when, _, step = self.todo.pop(0)
            self.now = max(self.now, when)
            step()

    def due(self, until):
        return any(item[0] <= until for item in self.todo)

    def compute(self, cost, work):
        self.run(self.now)
        work()
        self.now += cost
        self.run(self.now)


def columns(table, j):
    left = pl.ds(pl.multiple_of(j * W, 128), W)
    right = pl.ds(pl.multiple_of(HALF + j * W, 128), W)
    return jnp.concatenate([table[:, left], table[:, right]], axis=1)


def gather_tile(place, post, agenda, buf, j, sends):
    a, b = place.a, place.b
    cols = place.tiles[j]

    def mine():
        return buf.at[b, a, :, cols]

    first = post.group(
        [(mine, mine, peer) for peer in place.b_peers], mine, lambda: buf.at[0:3, 0, :, cols], 3
    )

    def along_a():
        first.wait_recv()

        def part():
            return buf.at[:, a, :, cols]

        def like():
            return buf.at[:, 0:3, :, cols]

        second = post.group([(part, part, peer) for peer in place.a_peers], like, like)
        sends.append(second)
        agenda.add(4.5, lambda: across(second))

    def across(second):
        second.wait_recv()

        def part():
            return buf.at[:, :, :, cols]

        third = post.send(part, part, place.core)
        sends.append(third)
        agenda.add(2.5, third.wait_recv)

    sends.append(first)
    agenda.add(3.6, along_a)


STEPS = 7
LAG = (1, 4, 6, 8, 10, 12, 13)
TG_TURNS = NT_COLS
TURNS = NT_COLS + LAG[-1]


def main_kernel(
    meta, hidden, gain, table_hbm, cotangent,
    head_hbm, cot_hbm, metas_out, embed_hbm, grad_hbm, gain_out, loss_out, cap_hbm,
    table, normed, metas, marks, stats, stat_in, scale_rows, back_rows, inverses,
    d_stage, d_rc, d_rx, d_rz, d_ry, found,
    stage, snd, rc, sx, rx, acc, sz, rz, acc_z, sy, ry, up,
    gain_in, local_sems, send_sems, recv_sems, flow_send, flow_recv,
):
    place = Place()
    post = Post(send_sems, recv_sems)
    agenda = Agenda()
    first_row = place.first_row
    a, b, c, o, g, y = place.a, place.b, place.c, place.o, place.g, place.y
    blocks = [g, place.ga, place.gb, place.gc]
    entered = place.meet()
    table_load = pltpu.make_async_copy(table_hbm, table, local_sems.at[0])
    table_load.start()
    metas[g] = meta[...]

    def inverse(wide):
        return lax.rsqrt(jnp.mean(wide * wide, axis=1, keepdims=True) + EPSILON)

    def rows_of(block, first, count):
        return pl.ds(pl.multiple_of(block * 256 + first, 16), count)

    quarter = place.colour

    def normalise(i, carry):
        at = ((quarter + i) % 4) * 64
        rows = pl.ds(pl.multiple_of(at, 16), 64)
        wide = hidden[rows, :].astype(F32)
        inv = inverse(wide)
        inverses[rows, :] = jnp.broadcast_to(inv, (64, 128))
        normed[rows_of(g, at, 64), :] = (wide * inv * gain[...]).astype(BF)
        return carry

    normalise(0, 0)
    stats[...] = jnp.zeros_like(stats)
    entered()

    def ship(block, first, count, peer):
        def part():
            return normed.at[rows_of(block, first, count), place.cols]

        return post.send(part, part, peer)

    at_q = quarter * 64
    meta_in = [
        post.send(lambda: metas.at[g], lambda: metas.at[g], peer) for peer in (place.y_a, place.y_b)
    ]
    a_low = ship(g, at_q, 32, place.y_a)
    b_high = ship(g, at_q + 32, 32, place.y_b)
    a_high = ship(g, at_q + 32, 32, place.y_a)
    b_low = ship(g, at_q, 32, place.y_b)
    lax.fori_loop(1, 4, normalise, 0)
    for item in meta_in:
        item.wait_recv()
    meta_c = post.send(lambda: metas.at[place.ga], lambda: metas.at[place.ga], place.y_b)
    spread = {}
    swaps = {}
    relays = []

    def relay():
        a_low.wait_recv()
        relays.append(ship(place.ga, at_q, 32, place.y_b))
        b_high.wait_recv()
        relays.append(ship(place.gb, at_q + 32, 32, place.y_a))

    def spread_block(name, block, items):
        for item in items:
            item.wait_recv()
        spread[name] = [ship(block, at_q, 64, peer) for peer in place.near]

    def swap_block(name, block):
        for item in spread[name]:
            item.wait_recv()
        swaps[name] = ship(block, 0, 256, place.core)

    cot_in = {}
    pieces = 256 // CHUNK

    def piece(n):
        rows_a = pl.ds((n % pieces) * CHUNK, CHUNK)
        rows_b = pl.ds((pieces - 1 - n % pieces) * CHUNK, CHUNK)

        def part(ref, rows, block=None):
            if block is None:
                return lambda: ref.at[rows, place.cols]
            return lambda: ref.at[block, rows, place.cols]

        if n < pieces:
            cot_in["a", n] = post.send(part(cotangent, rows_a), part(cot_hbm, rows_a, g), place.y_a)
            cot_in["b", n] = post.send(part(cotangent, rows_b), part(cot_hbm, rows_b, g), place.y_b)
        else:
            cot_in["b", n - pieces].wait_recv()
            cot_in["a", n - pieces].wait_recv()
            at_a, at_b = part(cot_hbm, rows_b, place.gb), part(cot_hbm, rows_a, place.ga)
            cot_in["a", n] = post.send(at_a, at_a, place.y_a)
            cot_in["b", n] = post.send(at_b, at_b, place.y_b)

    def cot_swap():
        for n in range(pieces // 2, pieces + pieces // 2):
            cot_in["a", n].wait_recv()
            cot_in["b", n].wait_recv()

        def part(block):
            return lambda: cot_hbm.at[block, :, place.cols]

        for n, block in enumerate((place.ga, place.gb, place.gc)):
            cot_in["swap", n] = post.send(part(block), part(block), place.core)

    def cap_store(n):
        return pltpu.make_async_copy(
            stage.at[n, pl.ds(0, ROWS)], cap_hbm.at[n], local_sems.at[1 + n]
        )

    def forward(n):
        block, side = blocks[n], n % 2
        if n >= 2:
            cap_store(side).wait()
        rows = normed[rows_of(block, 0, 256), :]
        total = jnp.zeros((1, 256), F32)
        picked = total
        for at in range(0, ROWS, MF):
            size = min(MF, ROWS - at)
            logits = lax.dot_general(table[at : at + size, :], rows, NT, preferred_element_type=F32)
            capped = SOFTCAP * jnp.tanh(logits * (1.0 / SOFTCAP))
            stage[side, at : at + size] = capped
            ids = lax.broadcasted_iota(jnp.int32, capped.shape, 0) + (first_row + at)
            hit = ids == metas[block, 1:2, :]
            total += jnp.sum(jnp.exp(capped), axis=0, keepdims=True)
            picked += jnp.sum(jnp.where(hit, capped, 0.0), axis=0, keepdims=True)
        stats[block, 0:1, :] = total
        stats[block, 1:2, :] = picked
        if n < 2:
            cap_store(side).start()

    table_load.wait()
    agenda.now = 4.5
    agenda.compute(4.0, lambda: forward(0))

    def mark(i, carry):
        rows = pl.ds(pl.multiple_of(i * MT, 16), MT)
        ids = lax.broadcasted_iota(jnp.int32, (MT, 256), 0) + (first_row + i * MT)
        for k in range(4):
            same = ids == metas[k, 0:1, :]
            marks[rows, k * 256 : (k + 1) * 256] = jnp.where(same, 1.0, 0.0).astype(BF)
        return carry

    meta_c.wait_recv()
    relay()
    agenda.compute(1.2, lambda: lax.fori_loop(0, NV, mark, 0))
    crossing = {}
    shape = (4, 4, 4, 16, W)

    def look_up(j):
        slot = j % 2
        if j >= 2:
            post.sent(crossing[j - 2])
        product = lax.dot_general(
            marks[...], columns(table, j), TN, preferred_element_type=F32
        ).astype(BF)
        d_stage[slot, 0:1024] = product[:, :W]
        d_stage[slot, 1024:2048] = product[:, W:]

        def there():
            return d_stage.at[slot, pl.ds(pl.multiple_of(o * 1024, 16), 1024)].reshape(*shape)

        crossing[j] = post.send(there, lambda: d_rc.at[j], place.core)

    def d_merge(j):
        crossing[j].wait_recv()
        here = d_stage[j % 2, pl.ds(pl.multiple_of(c * 1024, 16), 1024), :]
        d_rc[j] = here.reshape(*shape) + d_rc[j]
        agenda.add(max(0.0, D_START - agenda.now), lambda: d_along_a(j))

    def d_along_a(j):
        parts = [
            (lambda n=n: d_rc.at[j, :, :, place.a_at[n]], lambda n=n: d_rx.at[j, n], peer)
            for n, peer in enumerate(place.a_peers)
        ]
        item = post.group(parts, lambda: d_rx.at[j], lambda: d_rx.at[j])
        agenda.add(7.0, lambda: d_along_b(j, item))

    def d_along_b(j, item):
        item.wait_recv()
        d_rc[j, :, :, a] = (d_rc[j, :, :, a] + d_rx[j, 0]) + (d_rx[j, 1] + d_rx[j, 2])
        parts = [
            (lambda n=n: d_rc.at[j, :, place.b_at[n], a], lambda n=n: d_rz.at[j, n], peer)
            for n, peer in enumerate(place.b_peers)
        ]
        item = post.group(parts, lambda: d_rz.at[j], lambda: d_rz.at[j])
        agenda.add(5.0, lambda: d_along_y(j, item))

    def d_along_y(j, item):
        item.wait_recv()
        d_rc[j, :, b, a] = (d_rc[j, :, b, a] + d_rz[j, 0]) + (d_rz[j, 1] + d_rz[j, 2])
        parts = [
            (lambda n=n: d_rc.at[j, place.y_at[n], b, a], lambda n=n: d_ry.at[j, n], peer)
            for n, peer in enumerate(place.y_peers)
        ]
        item = post.group(parts, lambda: d_ry.at[j], lambda: d_ry.at[j])
        agenda.add(6.0, lambda: d_end(j, item))

    def d_end(j, item):
        item.wait_recv()
        row = (d_rc[j, g, b, a] + d_ry[j, 0]) + (d_ry[j, 1] + d_ry[j, 2])
        found[b, a, :, place.tiles[j]] = (row.astype(F32) * EMBED_SCALE).astype(BF)
        gather_tile(place, post, agenda, found, j, found_sends)

    looked = [0]
    found_sends = []

    def look():
        j = looked[0]
        looked[0] += 1
        agenda.compute(2.4, lambda: look_up(j))
        agenda.add(2.2, lambda: d_merge(j))

    look()
    spread_block("a", place.ga, [a_low_rest for a_low_rest in (a_high,)])
    spread_block("b", place.gb, [b_low])
    look()
    spread_block("c", place.gc, relays)
    for _ in range(2):
        look()
    swap_block("a", place.ga)
    swap_block("b", place.gb)
    agenda.now = max(agenda.now, 23.0)
    swaps["a"].wait_recv()
    agenda.compute(4.0, lambda: forward(1))
    swap_block("c", place.gc)
    piece(0)
    swaps["b"].wait_recv()
    agenda.compute(4.0, lambda: forward(2))
    piece(1)
    swaps["c"].wait_recv()
    agenda.compute(4.0, lambda: forward(3))

    def ring_start(base, peers, at):
        stat_in[base + at] = stats[...]

        def part():
            return stat_in.at[base + at]

        def like():
            return stat_in.at[pl.ds(0, len(peers))]

        return post.group([(part, part, peer) for peer in peers], like, like)

    def ring_end(item, base, count):
        item.wait_recv()
        total = stat_in[base]
        for i in range(1, count):
            total = total + stat_in[base + i]
        stats[...] = total

    item, base, count = ring_start(0, [place.core], c), 0, 2
    for peers, at in ((place.x_peers, place.x), (place.z_peers, place.z), (place.y_peers, y)):
        if base:
            look()
        ring_end(item, base, count)
        base = base + 4
        item, count = ring_start(base, peers, at), 4
    while looked[0] < NT_COLS:
        look()
    agenda.run(agenda.now + 1.5)
    ring_end(item, base, count)
    piece(2)

    def cap_load(n):
        return pltpu.make_async_copy(
            cap_hbm.at[n], stage.at[n, pl.ds(0, ROWS)], local_sems.at[1 + n]
        )

    def slopes(n):
        block, side = blocks[n], n % 2
        if n < 2:
            cap_load(n).wait()
        weight = metas[block, 2:3, :].astype(F32)
        factor = weight / stats[block, 0:1, :]
        target = metas[block, 1:2, :]
        lanes = pl.ds(pl.multiple_of(block * 256, 128), 256)

        def slab(i, carry):
            rows = pl.ds(pl.multiple_of(i * MT, 16), MT)
            ids = lax.broadcasted_iota(jnp.int32, (MT, 256), 0) + (first_row + i * MT)
            capped = stage[side, rows, :]
            hit = jnp.where(ids == target, weight, 0.0)
            ratio = capped * (1.0 / SOFTCAP)
            value = (jnp.exp(capped) * factor - hit) * (1.0 - ratio * ratio)
            marks[rows, lanes] = value.astype(BF)
            return carry

        lax.fori_loop(0, NV, slab, 0)
        if n >= 2:
            cap_load(n - 2).start()

    for n in (2, 3, 0, 1):
        agenda.compute(0.9, lambda: slopes(n))

    def bound(k):
        rest = jnp.maximum(1.0 - jnp.exp(stats[k, 1:2, :]) / stats[k, 0:1, :], 0.0)
        return TABLE_BOUND * (2.0 * rest + 1e-4)

    for k in range(4):
        turned = jnp.broadcast_to(UNITS / bound(k), (128, 256)).T
        scale_rows[k * 256 : (k + 1) * 256, :] = turned
    back_rows[...] = jnp.broadcast_to(bound(g) * (1.0 / UNITS), (128, 256)).T

    weights = [metas[k, 2:3, :].astype(F32) for k in range(4)]
    weight_sum = sum(jnp.sum(w) for w in weights)
    loss_sum = sum(
        jnp.sum(w * (jnp.log(stats[k, 0:1, :]) - stats[k, 1:2, :])) for k, w in enumerate(weights)
    )
    loss_out[...] = jnp.full((8, 128), loss_sum / jnp.maximum(weight_sum, 1.0), F32)
    for j in (NT_COLS - 2, NT_COLS - 1):
        post.sent(crossing[j])

    class Flow:
        def __init__(self, step, j):
            self.send_sem, self.recv_sem = flow_send.at[step, j], flow_recv.at[step, j]

        def start(self, parts):
            for src, dst, peer in parts:
                pltpu.make_async_remote_copy(
                    src_ref=src,
                    dst_ref=dst,
                    send_sem=self.send_sem,
                    recv_sem=self.recv_sem,
                    device_id=peer,
                    device_id_type=MESH,
                ).start()

        def sent(self, like):
            pltpu.make_async_copy(like, like, self.send_sem).wait()

        def here(self, like):
            pltpu.make_async_copy(like, like, self.recv_sem).wait()

    def pull(t):
        slot = t % 2

        @pl.when(t >= 2)
        def _():
            Flow(0, t - 2).sent(snd.at[slot])

        product = lax.dot_general(marks[...], columns(table, t), TN, preferred_element_type=F32)
        for side in range(2):
            for half in range(2):
                at = side * W + half * 128
                stage[slot, side * 1024 : side * 1024 + 1024, half * 128 : half * 128 + 128] = (
                    product[:, at : at + 128] * scale_rows[...]
                )
        there = pl.ds(pl.multiple_of(o * 1024, 16), 1024)
        snd[slot] = encode(stage[slot, there, :]).reshape(*shape)
        Flow(0, t).start([(snd.at[slot], rc.at[t % 4], place.core)])

    def held(slot, at):
        whole = stage.at[slot, pl.ds(pl.multiple_of(c * 1024, 16), 1024)].reshape(*shape)
        return whole[:, :, at]

    def merge(j):
        slot = j % 2
        Flow(0, j).here(rc.at[j % 4])

        @pl.when(j >= 2)
        def _():
            Flow(1, j - 2).sent(sx.at[slot])

        acc[j] = held(slot, a) + decode(rc[j % 4, :, :, a])
        parts = []
        for n, peer in enumerate(place.a_peers):
            at = place.a_at[n]
            sx[slot, n] = encode(held(slot, at) + decode(rc[j % 4, :, :, at]))
            parts.append((sx.at[slot, n], rx.at[j, n], peer))
        Flow(1, j).start(parts)

    def along_b(j):
        Flow(1, j).here(rx.at[j])
        parts = []
        for n in range(4):
            at = (b + n) % 4
            value = acc[j, :, at] + decode(rx[j, 0, :, at])
            value = value + decode(rx[j, 1, :, at]) + decode(rx[j, 2, :, at])
            if n == 0:
                acc_z[j] = value
            else:
                sz[j, n - 1] = encode(value)
                parts.append((sz.at[j, n - 1], rz.at[j, n - 1], place.b_peers[n - 1]))
        Flow(2, j).start(parts)

    def along_y(j):
        Flow(2, j).here(rz.at[j])
        acc_z[j] = acc_z[j] + decode(rz[j, 0]) + decode(rz[j, 1]) + decode(rz[j, 2])
        parts = []
        for n, peer in enumerate(place.y_peers):
            sy[j, n] = encode(acc_z[j, place.y_at[n]])
            parts.append((sy.at[j, n], ry.at[j, n], peer))
        Flow(3, j).start(parts)

    def give_b(j):
        Flow(3, j).here(ry.at[j])
        value = acc_z[j, g] + decode(ry[j, 0]) + decode(ry[j, 1]) + decode(ry[j, 2])
        cols = place.tile_cols(j)
        up[b, a, :, cols] = encode(value)
        part = up.at[b, a, :, cols]
        Flow(4, j).start([(part, part, peer) for peer in place.b_peers])

    def give_a(j):
        cols = place.tile_cols(j)
        Flow(4, j).here(up.at[0:3, 0, :, cols])
        part = up.at[:, a, :, cols]
        Flow(5, j).start([(part, part, peer) for peer in place.a_peers])

    def give_core(j):
        cols = place.tile_cols(j)
        Flow(5, j).here(up.at[:, 0:3, :, cols])
        part = up.at[:, :, :, cols]
        Flow(6, j).start([(part, part, place.core)])

    def last(j):
        Flow(6, j).here(up.at[:, :, :, place.tile_cols(j)])

    steps = (merge, along_b, along_y, give_b, give_a, give_core, last)

    def head_store(n, h):
        cols = pl.ds(pl.multiple_of((2 * n + h) * W, 128), W)
        return pltpu.make_async_copy(
            d_stage.at[h, pl.ds(0, ROWS)], head_hbm.at[:, cols], local_sems.at[3 + h]
        )

    def head_tiles(n):
        def one(h, carry):
            @pl.when(n > 0)
            def _():
                head_store(n - 1, h).wait()

            cols = pl.ds(pl.multiple_of((2 * n + h) * W, 128), W)
            product = lax.dot_general(marks[...], normed[:, cols], NN, preferred_element_type=F32)
            d_stage[h, 0:ROWS] = product.astype(BF)
            head_store(n, h).start()
            return carry

        lax.fori_loop(0, 2, one, 0)

    for n in range(3, pieces + pieces // 2):
        agenda.add(2.8 * (n - 3) + 0.1, lambda n=n: piece(n))
    agenda.add(2.8 * (pieces + pieces // 2 - 3) + 4.0, cot_swap)
    began = agenda.now

    def turn(t, carry):
        @pl.when(t < NT_COLS)
        def _():
            pull(t)

        @pl.when((t >= NT_COLS) & (t < NT_COLS + TG_TURNS))
        def _():
            head_tiles(t - NT_COLS)

        for lag, step in zip(LAG, steps):
            @pl.when((t >= lag) & (t < lag + NT_COLS))
            def _():
                step(t - lag)

        for k in range(TURNS):
            due = began + 2.8 * (k + 1)
            if agenda.due(due):
                @pl.when(t == k)
                def _():
                    agenda.run(due)
                    agenda.now = max(agenda.now, due)
            agenda.now = max(agenda.now, due)
        return carry

    lax.fori_loop(0, TURNS, turn, 0)
    agenda.run()

    embed_store = pltpu.make_async_copy(found, embed_hbm, local_sems.at[0])
    embed_store.start()

    GR = 16

    def upstream(i):
        rows = pl.ds(pl.multiple_of(i * GR, 16), GR)
        down = back_rows[rows, :]
        value = decode(up[i // 4, i % 4]) * jnp.concatenate([down] * (D // 128), axis=1)
        return value, hidden[rows, :].astype(F32), inverses[rows, :]

    def gain_rows(i, total):
        value, wide, inv = upstream(i)
        product = value * wide * jnp.concatenate([inv] * (D // 128), axis=1)
        return total + (product[0:8] + product[8:16])

    part = jnp.sum(lax.fori_loop(0, 16, gain_rows, jnp.zeros((8, D), F32)), axis=0, keepdims=True)
    gain_in[y] = jnp.concatenate([part[:, i * 128 : (i + 1) * 128] for i in range(D // 128)], axis=0)

    def gain_part():
        return gain_in.at[y]

    gain_item = post.group(
        [(gain_part, gain_part, peer) for peer in place.y_peers],
        lambda: gain_in.at[0:3],
        lambda: gain_in.at[0:3],
    )
    embed_store.wait()
    for item in found_sends:
        post.sent(item)

    def grad_rows(i, carry):
        value, wide, inv = upstream(i)
        scaled_up = value * gain[...]
        mean_dot = jnp.sum(scaled_up * wide, axis=1, keepdims=True) * (1.0 / D)
        pull_back = inv * inv * inv * mean_dot
        out = jnp.concatenate([inv] * (D // 128), axis=1) * scaled_up
        out = out - wide * jnp.concatenate([pull_back] * (D // 128), axis=1)
        found[i // 4, i % 4] = out.astype(BF)
        return carry

    lax.fori_loop(0, 16, grad_rows, 0)
    grad_store = pltpu.make_async_copy(found, grad_hbm, local_sems.at[0])
    grad_store.start()
    for n in range(3):
        cot_in["swap", n].wait_recv()
    metas_out[...] = metas[...]
    for h in range(2):
        head_store(TG_TURNS - 1, h).wait()

    def drain(j, carry):
        cols = place.tile_cols(j)
        Flow(2, j).sent(sz.at[j])
        Flow(3, j).sent(sy.at[j])
        for _ in range(3):
            Flow(4, j).sent(up.at[0, 0, :, cols])
        Flow(5, j).sent(up.at[:, 0:3, :, cols])
        Flow(6, j).sent(up.at[:, :, :, cols])
        return carry

    lax.fori_loop(0, NT_COLS, drain, 0)
    for j in (NT_COLS - 2, NT_COLS - 1):
        Flow(0, j).sent(snd.at[j % 2])
        Flow(1, j).sent(sx.at[j % 2])
    post.close()
    gain_item.wait_recv()
    gain_out[...] = gain_in[0] + gain_in[1] + gain_in[2] + gain_in[3]
    grad_store.wait()


FAR = 1 << 30
SLOTS = 128


def patch_kernel(
    metas, own_cot, cot_hbm, head_hbm, out_hbm, grad, cot, left, picks, sums, rows_of, sems
):
    g = gray(lax.axis_index("dp"))
    first = lax.axis_index(DP_VOCAB) * ROWS
    for k in range(4):
        @pl.when(g == k)
        def _():
            pltpu.make_async_copy(own_cot, cot.at[k], sems.at[k]).start()

        @pl.when(g != k)
        def _():
            pltpu.make_async_copy(cot_hbm.at[k], cot.at[k], sems.at[k]).start()

    def tile(ref, i):
        return ref.at[pl.ds(i * MT, MT)]

    for i in range(NV):
        pltpu.make_async_copy(tile(head_hbm, i), tile(grad, i), sems.at[4 + i]).start()
    for k in range(4):
        local = metas[k, 0:1, :] - first
        left[k : k + 1, :] = jnp.where((local >= 0) & (local < ROWS), local, FAR)
    for k in range(4):
        pltpu.make_async_copy(own_cot, cot.at[k], sems.at[k]).wait()
    for i in range(NV):
        pltpu.make_async_copy(tile(head_hbm, i), tile(grad, i), sems.at[4 + i]).wait()

    def one_pass(lowest):
        picks[...] = jnp.zeros_like(picks)

        def more(state):
            return (state[0] < SLOTS) & (state[1] < FAR)

        def take(state):
            n, row = state
            rows_of[n] = row
            rest = left[...]
            same = rest == row
            for k in range(4):
                picks[pl.ds(n, 1), k * 256 : (k + 1) * 256] = jnp.where(same[k : k + 1], 1.0, 0.0)
            rest = jnp.where(same, FAR, rest)
            left[...] = rest
            return n + 1, jnp.min(rest)

        count, lowest = lax.while_loop(more, take, (0, lowest))
        sums[...] = lax.dot_general(
            picks[...].astype(BF), cot[...].reshape(1024, D), NN, preferred_element_type=F32
        )

        def patch(n, carry):
            row = rows_of[n]
            base = pl.multiple_of((row // 16) * 16, 16)
            old = grad[pl.ds(base, 16), :]
            new = (old.astype(F32) + sums[pl.ds(n, 1), :] * EMBED_SCALE).astype(BF)
            here = lax.broadcasted_iota(jnp.int32, (16, D), 0) == row - base
            grad[pl.ds(base, 16), :] = jnp.where(here, new, old)
            return carry

        lax.fori_loop(0, count, patch, 0)
        return lowest

    lax.while_loop(lambda lowest: lowest < FAR, one_pass, jnp.min(left[...]))
    for i in range(NV):
        pltpu.make_async_copy(tile(grad, i), tile(out_hbm, i), sems.at[4 + i]).start()
    for i in range(NV):
        pltpu.make_async_copy(tile(grad, i), tile(out_hbm, i), sems.at[4 + i]).wait()


def body(input_ids, target_ids, loss_mask, final_hidden, norm_gain, embed_cotangent, table):
    any_ = pl.BlockSpec(memory_space=pl.ANY)
    vmem = pl.BlockSpec(memory_space=pltpu.VMEM)
    dma = pltpu.SemaphoreType.DMA
    V = pltpu.VMEM
    S = jax.ShapeDtypeStruct
    meta = jnp.pad(jnp.stack([input_ids, target_ids, loss_mask]), ((0, 5), (0, 0)))
    gain = norm_gain.reshape(1, D)
    n = NT_COLS
    head, cot, metas, embed, grad, gain_grad, loss, _ = pl.pallas_call(
        main_kernel,
        out_shape=(
            S((ROWS, D), BF),
            S((4, 256, D), BF),
            S((4, 8, 256), jnp.int32),
            S((4, 4, 16, D), BF),
            S((4, 4, 16, D), BF),
            S((D // 128, 128), F32),
            S((8, 128), F32),
            S((2, ROWS, 256), F32),
        ),
        in_specs=[vmem, vmem, vmem, any_, any_],
        out_specs=(any_, any_, vmem, any_, any_, vmem, vmem, any_),
        scratch_shapes=[
            V((ROWS, D), BF),
            V((1024, D), BF),
            V((4, 8, 256), jnp.int32),
            V((ROWS, 1024), BF),
            V((4, 2, 256), F32),
            V((16, 4, 2, 256), F32),
            V((1024, 128), F32),
            V((256, 128), F32),
            V((256, 128), F32),
            V((2, 2048, W), BF),
            V((n, 4, 4, 4, 16, W), BF),
            V((n, 3, 4, 4, 16, W), BF),
            V((n, 3, 4, 16, W), BF),
            V((n, 3, 16, W), BF),
            V((4, 4, 16, D), BF),
            V((2, 2048, W), F32),
            V((2, 4, 4, 4, 16, W), I16),
            V((4, 4, 4, 4, 16, W), I16),
            V((2, 3, 4, 4, 16, W), I16),
            V((n, 3, 4, 4, 16, W), I16),
            V((n, 4, 4, 16, W), F32),
            V((n, 3, 4, 16, W), I16),
            V((n, 3, 4, 16, W), I16),
            V((n, 4, 16, W), F32),
            V((n, 3, 16, W), I16),
            V((n, 3, 16, W), I16),
            V((4, 4, 16, D), I16),
            V((4, D // 128, 128), F32),
            dma((5,)),
            dma((120,)),
            dma((120,)),
            dma((STEPS, n)),
            dma((STEPS, n)),
        ],
        compiler_params=pltpu.CompilerParams(
            collective_id=0, has_side_effects=True, vmem_limit_bytes=VMEM_LIMIT
        ),
        name="main",
    )(meta, final_hidden, gain, table, embed_cotangent)

    table_grad = pl.pallas_call(
        patch_kernel,
        out_shape=S((ROWS, D), BF),
        in_specs=[vmem, any_, any_, any_],
        out_specs=any_,
        scratch_shapes=[
            V((ROWS, D), BF),
            V((4, 256, D), BF),
            V((4, 256), jnp.int32),
            V((SLOTS, 1024), F32),
            V((SLOTS, D), F32),
            pltpu.SMEM((SLOTS,), jnp.int32),
            dma((4 + NV,)),
        ],
        compiler_params=pltpu.CompilerParams(vmem_limit_bytes=VMEM_LIMIT),
        name="patch",
    )(metas, embed_cotangent, cot, head)
    return (
        embed.reshape(256, D),
        loss[0, 0],
        grad.reshape(256, D),
        gain_grad.reshape(D),
        table_grad,
    )


def solution(mesh):
    finer = Mesh(
        mesh.devices.reshape(mesh.shape["dp"], 4, 4, 2), ("dp", "vocab_0", "vocab_1", "vocab_2")
    )
    placed = (P("dp"), P("dp"), P("dp"), P("dp", None), P(), P("dp", None), P(DP_VOCAB, None))
    return jax.shard_map(
        body,
        mesh=finer,
        in_specs=placed,
        out_specs=(P("dp", None), P(), P("dp", None), P(), P(DP_VOCAB, None)),
        check_vma=False,
    )
```

time: 785 us -> 173 us (0.22)
  waiting for transfers between devices: 365 us -> 0 us
  Pallas kernels: 0 us -> 163 us
  blocking collectives: 143 us -> 0 us
  local copies, waits for them, and re-layouts: 92.7 us -> 7.95 us
  other arithmetic: 79.7 us -> 0.72 us
  matrix products: 78.9 us -> 0 us
  between operations: 17.6 us -> 0.66 us
    reduce_scatter x4 -> x0, waiting for transfers between devices: 185 us -> none  [the longest x1 128 us: body(): lax.psum_scatter(upstream_term(), 'dp', scatter_dimension=0, tiled=True)]
    all_gather x3 -> x0, waiting for transfers between devices: 179 us -> none  [the longest x1 137 us: gather_together(): lines, at, finished = (lax.all_gather(flat, axis), 0, [])]
    pallas_call x0 -> x2, Pallas kernels: none -> 163 us  [the longest x1 147 us: body(): pl.pallas_call(main_kernel, out_shape=(S((ROWS, D), BF), S((4, 256, D), B...]
    psum x5 -> x0, blocking collectives: 121 us -> none  [the longest x1 66.1 us: packed_total(): so_far = lax.psum(jnp.concatenate([a.ravel() for a in arrays]), axis)]
    dot_general x3 -> x0, matrix products: 78.9 us -> none  [the longest x1 29.1 us: upstream_term(): return jnp.dot(block, table, preferred_element_type=jnp.float32)]
    scatter-add x1 -> x0, other arithmetic: 35.3 us -> none  [body(): jax.ops.segment_sum(cotangent_all.astype(jnp.float32), segment_ids, num_s...]
    convert_element_type x7 -> x0, other arithmetic: 35.2 us -> none  [the longest x1 15 us: body(): cotangent_all.astype(jnp.float32)]
    convert_element_type x1 -> x0, local copies, waits for them, and re-layouts: 28.9 us -> none  [body(): cotangent_all.astype(jnp.float32)]
  transfers between devices with their start and end apart: 7 -> 0, of which waited for: 5 -> 0; matrix products, arithmetic and copies ran while one was open for 27% -> 0% of each run, Pallas kernels for 0% -> 0%
where the time goes in v2:
time: 173 us; the launch traced here: 172 us
  Pallas kernels  163 us (94%)
  local copies, waits for them, and re-layouts  7.95 us (5%)
    pallas_call x1, Pallas kernels, body(): pl.pallas_call(main_kernel, out_shape=(S((ROWS, D), BF), S((4, 256, D), B...  147 us
    pallas_call x1, Pallas kernels, body(): pl.pallas_call(patch_kernel, out_shape=S((ROWS, D), BF), in_specs=[vmem,...  16.4 us
    unnamed x7, local copies, waits for them, and re-layouts  4.82 us

profile of v2, /device:TPU:1, one launch (start us, length us, event | category | flops | bytes accessed | tf_op | source)
XLA Modules:
  0.0 172.3 jit_solution(11720815614888252233)
XLA Ops:
  0.6 0.7 pad_add_fusion
  1.4 0.6 pad.4.meta
  2.0 1.3 reshape.22.gain
  3.3 146.6 %main.1 = (bf16[2000,3584]{1,0:T(8,128)(2,1)}, bf16[4,256,3584]{2,1,0:T(8,128)(2,1)}, s32[4,8,256]{2,1,0:T(8,128)}, bf16[4,4,16,3584]{3,2,1,0:T(8,128)(2,1)}, bf...) custom-call(s32[8,256]{1,0:T(8,128)} %pad.4.meta, ...), custom_call_target="tpu_custom_call" | custom-call | tf_op jit(solution)/shard_map/main/pallas_call | solution.py:858
  149.9 1.2 slice.3
  151.1 16.4 %patch.1 = bf16[2000,3584]{1,0:T(8,128)(2,1)} custom-call(s32[4,8,256]{2,1,0:T(8,128)} %get-tuple-element.16.metas, bf16[256,3584]{1,0:T(8,128)(2,1)} %own_cot.1, bf16[4,256,3584]{2,1,0:T(8,128)(2,1)} %get-tuple-element.17.cot_hbm, bf16[2000,3584]{1,0:T(8,128)(2,1)} %get-tuple-element.18.head_hbm), custom_call_target="tpu_custom_call" | custom-call | tf_op jit(solution)/shard_map/patch/pallas_call | solution.py:913
  167.5 0.0 copy-start
  167.5 3.0 %copy.15 = bf16[256,3584]{1,0:T(8,128)(2,1)} copy(bf16[256,3584]{1,0:T(8,128)(2,1)} %bitcast.8) | data formatting | bytes 3670016
  170.5 0.0 copy-done
  170.5 0.0 copy-start.1
  170.5 1.2 copy.16
  171.7 0.0 copy-done.1
  171.7 0.6 copy.17
Async XLA Ops:
  167.5 3.0 %copy-start = (bf16[4,4,16,3584]{3,2,1,0:T(8,128)(2,1)S(1)}, bf16[4,4,16,3584]{3,2,1,0:T(8,128)(2,1)}, u32[]{:S(2)}) copy-start(bf16[4,4,16,3584]{3,2,1,0:T(8,128)(2,1)} %get-tuple-element.14) | copy-start | bytes 5505028
  170.5 1.2 copy-start.1

commit v3 on v2

--- a/solution.py
+++ b/solution.py
@@ -27,8 +27,8 @@
 HALF = D // 2
 W = 256
 NT_COLS = HALF // W
-CHUNK = 32
-D_START = 24.0
+SLOTS = 32
+ALL_SLOTS = 4 * SLOTS
 VMEM_LIMIT = 66_900_000
 TABLE_BOUND = 5.0 / math.sqrt(D) * 1.01
 UNITS = 24000.0
@@ -73,7 +73,6 @@
         self.z_peers = [{"vocab_0": (z + off) % 4} for off in (1, 2, 3)]
         self.y_peers = [{"dp": (y + off) % 4} for off in (1, 2, 3)]
         self.cols = pl.ds(pl.multiple_of(c * HALF, 128), HALF)
-        self.tiles = [self.tile_cols(j) for j in range(NT_COLS)]
         self.a_at = [(self.a + off) % 4 for off in (1, 2, 3)]
         self.b_at = [(self.b + off) % 4 for off in (1, 2, 3)]
         self.y_at = [gray((y + off) % 4) for off in (1, 2, 3)]
@@ -86,9 +85,11 @@
     def _at(self, a, b):
         return {"vocab_1": a + self.c * (b - a), "vocab_0": b + self.c * (a - b)}
 
-    def tile_cols(self, j, core=None):
-        core = self.c if core is None else core
-        return pl.ds(pl.multiple_of(core * HALF + j * W, 128), W)
+    def tile_cols(self, j):
+        return pl.ds(pl.multiple_of(self.c * HALF + j * W, 128), W)
+
+    def first_row_of(self, k):
+        return (((gray(k) * 4 + self.z) * 4 + self.x) * 2 + self.c) * ROWS
 
     def meet(self):
         peers = [self.core] + self.x_peers + self.z_peers + self.y_peers
@@ -182,42 +183,39 @@
     return jnp.concatenate([table[:, left], table[:, right]], axis=1)
 
 
-def gather_tile(place, post, agenda, buf, j, sends):
-    a, b = place.a, place.b
-    cols = place.tiles[j]
+def gather_rows(place, post, agenda, buf, sends):
+    a, b, cols = place.a, place.b, place.cols
 
     def mine():
         return buf.at[b, a, :, cols]
+
+    def row():
+        return buf.at[:, a, :, cols]
+
+    def rows():
+        return buf.at[:, 0:3, :, cols]
+
+    def half():
+        return buf.at[:, :, :, cols]
 
     first = post.group(
         [(mine, mine, peer) for peer in place.b_peers], mine, lambda: buf.at[0:3, 0, :, cols], 3
     )
+    sends.append(first)
 
     def along_a():
         first.wait_recv()
-
-        def part():
-            return buf.at[:, a, :, cols]
-
-        def like():
-            return buf.at[:, 0:3, :, cols]
-
-        second = post.group([(part, part, peer) for peer in place.a_peers], like, like)
+        second = post.group([(row, row, peer) for peer in place.a_peers], rows, rows)
         sends.append(second)
-        agenda.add(4.5, lambda: across(second))
+        agenda.add(10.0, lambda: across(second))
 
     def across(second):
         second.wait_recv()
-
-        def part():
-            return buf.at[:, :, :, cols]
-
-        third = post.send(part, part, place.core)
+        third = post.send(half, half, place.core)
         sends.append(third)
-        agenda.add(2.5, third.wait_recv)
-
-    sends.append(first)
-    agenda.add(3.6, along_a)
+        agenda.add(4.0, third.wait_recv)
+
+    agenda.add(6.0, along_a)
 
 
 STEPS = 7
@@ -227,10 +225,10 @@
 
 
 def main_kernel(
-    meta, hidden, gain, table_hbm, cotangent,
-    head_hbm, cot_hbm, metas_out, embed_hbm, grad_hbm, gain_out, loss_out, cap_hbm,
-    table, normed, metas, marks, stats, stat_in, scale_rows, back_rows, inverses,
-    d_stage, d_rc, d_rx, d_rz, d_ry, found,
+    own_ids, own_targets, own_mask, hidden, gain_in_rows, table_hbm, cot_hbm,
+    head_hbm, metas_out, embed_hbm, grad_hbm, gain_out, loss_out, cap_hbm,
+    table, normed, metas, gain, marks, stats, stat_in, scale_rows, back_rows, inverses,
+    d_stage, d_part, d_rc, d_rx, d_rz, found, owner_of, slot_of, packed, lines, cot_packed, cot_lines,
     stage, snd, rc, sx, rx, acc, sz, rz, acc_z, sy, ry, up,
     gain_in, local_sems, send_sems, recv_sems, flow_send, flow_recv,
 ):
@@ -243,7 +241,12 @@
     entered = place.meet()
     table_load = pltpu.make_async_copy(table_hbm, table, local_sems.at[0])
     table_load.start()
-    metas[g] = meta[...]
+    metas[g, 0:1, :] = own_ids[...]
+    metas[g, 1:2, :] = own_targets[...]
+    metas[g, 2:3, :] = own_mask[...]
+    gain[...] = jnp.concatenate([gain_in_rows[i : i + 1, :] for i in range(D // 128)], axis=1)
+    cot_load = pltpu.make_async_copy(cot_hbm, found, local_sems.at[3])
+    cot_load.start()
 
     def inverse(wide):
         return lax.rsqrt(jnp.mean(wide * wide, axis=1, keepdims=True) + EPSILON)
@@ -303,39 +306,6 @@
         for item in spread[name]:
             item.wait_recv()
         swaps[name] = ship(block, 0, 256, place.core)
-
-    cot_in = {}
-    pieces = 256 // CHUNK
-
-    def piece(n):
-        rows_a = pl.ds((n % pieces) * CHUNK, CHUNK)
-        rows_b = pl.ds((pieces - 1 - n % pieces) * CHUNK, CHUNK)
-
-        def part(ref, rows, block=None):
-            if block is None:
-                return lambda: ref.at[rows, place.cols]
-            return lambda: ref.at[block, rows, place.cols]
-
-        if n < pieces:
-            cot_in["a", n] = post.send(part(cotangent, rows_a), part(cot_hbm, rows_a, g), place.y_a)
-            cot_in["b", n] = post.send(part(cotangent, rows_b), part(cot_hbm, rows_b, g), place.y_b)
-        else:
-            cot_in["b", n - pieces].wait_recv()
-            cot_in["a", n - pieces].wait_recv()
-            at_a, at_b = part(cot_hbm, rows_b, place.gb), part(cot_hbm, rows_a, place.ga)
-            cot_in["a", n] = post.send(at_a, at_a, place.y_a)
-            cot_in["b", n] = post.send(at_b, at_b, place.y_b)
-
-    def cot_swap():
-        for n in range(pieces // 2, pieces + pieces // 2):
-            cot_in["a", n].wait_recv()
-            cot_in["b", n].wait_recv()
-
-        def part(block):
-            return lambda: cot_hbm.at[block, :, place.cols]
-
-        for n, block in enumerate((place.ga, place.gb, place.gc)):
-            cot_in["swap", n] = post.send(part(block), part(block), place.core)
 
     def cap_store(n):
         return pltpu.make_async_copy(
@@ -367,103 +337,148 @@
     agenda.now = 4.5
     agenda.compute(4.0, lambda: forward(0))
 
+
+    meta_c.wait_recv()
+    relay()
+    ids = [metas[k, 0:1, :] for k in range(4)]
+    locals_ = [row - first_row for row in ids]
+    for k in range(4):
+        locals_.append(own_ids[...] - place.first_row_of(k))
+    owned = [jnp.where((row >= 0) & (row < ROWS), 1.0, 0.0) for row in locals_]
+    later = lax.broadcasted_iota(jnp.int32, (256, 256), 0) < lax.broadcasted_iota(
+        jnp.int32, (256, 256), 1
+    )
+    ranks = lax.dot_general(
+        jnp.concatenate(owned + [jnp.zeros((8, 256), F32)], axis=0).astype(BF),
+        jnp.where(later, 1.0, 0.0).astype(BF),
+        NN,
+        preferred_element_type=F32,
+    )
+    numbers = lax.broadcasted_iota(jnp.int32, (SLOTS, 256), 0).astype(F32)
+
+    def chosen(k):
+        same = (numbers == ranks[k : k + 1, :]) & (owned[k] > 0.5)
+        return jnp.where(same, 1.0, 0.0)
+
+    mine = jnp.concatenate([chosen(k) for k in range(4)], axis=0).astype(BF)
+    slot_of[...] = jnp.concatenate([chosen(4 + k) for k in range(4)], axis=0).astype(BF)
+    digits = [jnp.right_shift(row, 6) for row in locals_[:4]]
+    digits += [jnp.bitwise_and(row, 63) for row in locals_[:4]]
+    digits = [jnp.where(owned[n % 4] > 0.5, row.astype(F32), 0.0) for n, row in enumerate(digits)]
+    read = lax.dot_general(
+        jnp.concatenate(digits + [jnp.ones((8, 256), F32)], axis=0).astype(BF),
+        mine,
+        NT,
+        preferred_element_type=F32,
+    )
+    lane = lax.broadcasted_iota(jnp.int32, (1, ALL_SLOTS), 1)
+    wanted = jnp.zeros((1, ALL_SLOTS), F32)
+    for k in range(4):
+        here = (lane >= k * SLOTS) & (lane < (k + 1) * SLOTS)
+        wanted = jnp.where(here, read[k : k + 1] * 64.0 + read[4 + k : 5 + k], wanted)
+    wanted = jnp.where(read[8:9] > 0.5, wanted, -1.0)
+
     def mark(i, carry):
         rows = pl.ds(pl.multiple_of(i * MT, 16), MT)
-        ids = lax.broadcasted_iota(jnp.int32, (MT, 256), 0) + (first_row + i * MT)
-        for k in range(4):
-            same = ids == metas[k, 0:1, :]
-            marks[rows, k * 256 : (k + 1) * 256] = jnp.where(same, 1.0, 0.0).astype(BF)
+        at = lax.broadcasted_iota(jnp.int32, (MT, ALL_SLOTS), 0) + i * MT
+        owner_of[rows, :] = jnp.where(at.astype(F32) == wanted, 1.0, 0.0).astype(BF)
         return carry
 
-    meta_c.wait_recv()
-    relay()
-    agenda.compute(1.2, lambda: lax.fori_loop(0, NV, mark, 0))
-    crossing = {}
-    shape = (4, 4, 4, 16, W)
-
-    def look_up(j):
-        slot = j % 2
-        if j >= 2:
-            post.sent(crossing[j - 2])
-        product = lax.dot_general(
-            marks[...], columns(table, j), TN, preferred_element_type=F32
-        ).astype(BF)
-        d_stage[slot, 0:1024] = product[:, :W]
-        d_stage[slot, 1024:2048] = product[:, W:]
-
-        def there():
-            return d_stage.at[slot, pl.ds(pl.multiple_of(o * 1024, 16), 1024)].reshape(*shape)
-
-        crossing[j] = post.send(there, lambda: d_rc.at[j], place.core)
-
-    def d_merge(j):
-        crossing[j].wait_recv()
-        here = d_stage[j % 2, pl.ds(pl.multiple_of(c * 1024, 16), 1024), :]
-        d_rc[j] = here.reshape(*shape) + d_rc[j]
-        agenda.add(max(0.0, D_START - agenda.now), lambda: d_along_a(j))
-
-    def d_along_a(j):
+    lax.fori_loop(0, NV, mark, 0)
+    starts = lax.broadcasted_iota(jnp.int32, (128, 256), 0) * ROWS
+    most = jnp.float32(0.0)
+    for row in ids:
+        held = jnp.where((row >= starts) & (row < starts + ROWS), 1.0, 0.0)
+        most = jnp.maximum(most, jnp.max(jnp.sum(held, axis=1, keepdims=True)))
+    embed_scale = jnp.where(most <= SLOTS, EMBED_SCALE, 0.0)
+
+    spread_block("a", place.ga, [a_high])
+    spread_block("b", place.gb, [b_low])
+
+    def look_up(j, carry):
+        cols = pl.ds(pl.multiple_of(j * 2 * W, 128), 2 * W)
+        rows = lax.dot_general(owner_of[...], table[:, cols], TN, preferred_element_type=F32)
+        packed[:, :, cols] = rows.astype(BF).reshape(4, SLOTS, 2 * W)
+        return carry
+
+    lax.fori_loop(0, 3, look_up, 0)
+    spread_block("c", place.gc, relays)
+    cot_load.wait()
+
+    def cot_pack(j, carry):
+        cols = pl.ds(pl.multiple_of(j * 2 * W, 128), 2 * W)
+        rows = lax.dot_general(
+            slot_of[...], found[:, :, :, cols].reshape(256, 2 * W), NN, preferred_element_type=F32
+        )
+        cot_packed[:, :, cols] = rows.astype(BF).reshape(4, SLOTS, 2 * W)
+        return carry
+
+    lax.fori_loop(0, NT_COLS, cot_pack, 0)
+
+    def exchange(src, dst):
+        dst[g] = src[g]
         parts = [
-            (lambda n=n: d_rc.at[j, :, :, place.a_at[n]], lambda n=n: d_rx.at[j, n], peer)
-            for n, peer in enumerate(place.a_peers)
-        ]
-        item = post.group(parts, lambda: d_rx.at[j], lambda: d_rx.at[j])
-        agenda.add(7.0, lambda: d_along_b(j, item))
-
-    def d_along_b(j, item):
-        item.wait_recv()
-        d_rc[j, :, :, a] = (d_rc[j, :, :, a] + d_rx[j, 0]) + (d_rx[j, 1] + d_rx[j, 2])
-        parts = [
-            (lambda n=n: d_rc.at[j, :, place.b_at[n], a], lambda n=n: d_rz.at[j, n], peer)
-            for n, peer in enumerate(place.b_peers)
-        ]
-        item = post.group(parts, lambda: d_rz.at[j], lambda: d_rz.at[j])
-        agenda.add(5.0, lambda: d_along_y(j, item))
-
-    def d_along_y(j, item):
-        item.wait_recv()
-        d_rc[j, :, b, a] = (d_rc[j, :, b, a] + d_rz[j, 0]) + (d_rz[j, 1] + d_rz[j, 2])
-        parts = [
-            (lambda n=n: d_rc.at[j, place.y_at[n], b, a], lambda n=n: d_ry.at[j, n], peer)
+            (lambda n=n: src.at[place.y_at[n]], lambda: dst.at[g], peer)
             for n, peer in enumerate(place.y_peers)
         ]
-        item = post.group(parts, lambda: d_ry.at[j], lambda: d_ry.at[j])
-        agenda.add(6.0, lambda: d_end(j, item))
-
-    def d_end(j, item):
-        item.wait_recv()
-        row = (d_rc[j, g, b, a] + d_ry[j, 0]) + (d_ry[j, 1] + d_ry[j, 2])
-        found[b, a, :, place.tiles[j]] = (row.astype(F32) * EMBED_SCALE).astype(BF)
-        gather_tile(place, post, agenda, found, j, found_sends)
-
-    looked = [0]
-    found_sends = []
-
-    def look():
-        j = looked[0]
-        looked[0] += 1
-        agenda.compute(2.4, lambda: look_up(j))
-        agenda.add(2.2, lambda: d_merge(j))
-
-    look()
-    spread_block("a", place.ga, [a_low_rest for a_low_rest in (a_high,)])
-    spread_block("b", place.gb, [b_low])
-    look()
-    spread_block("c", place.gc, relays)
-    for _ in range(2):
-        look()
+        return post.group(parts, lambda: src.at[0:3], lambda: dst.at[0:3])
+
+    lax.fori_loop(3, NT_COLS, look_up, 0)
+    line_item = exchange(packed, lines)
+    cot_item = exchange(cot_packed, cot_lines)
+
     swap_block("a", place.ga)
     swap_block("b", place.gb)
     agenda.now = max(agenda.now, 23.0)
     swaps["a"].wait_recv()
-    agenda.compute(4.0, lambda: forward(1))
+    agenda.compute(4.3, lambda: forward(1))
     swap_block("c", place.gc)
-    piece(0)
     swaps["b"].wait_recv()
-    agenda.compute(4.0, lambda: forward(2))
-    piece(1)
+    agenda.compute(4.3, lambda: forward(2))
     swaps["c"].wait_recv()
-    agenda.compute(4.0, lambda: forward(3))
+    agenda.compute(4.3, lambda: forward(3))
+
+    found_sends = []
+
+    def unpack():
+        line_item.wait_recv()
+        cot_item.wait_recv()
+        for h in range(2):
+            rows = lax.dot_general(
+                slot_of[...],
+                lines[:, :, h * HALF : (h + 1) * HALF].reshape(ALL_SLOTS, HALF),
+                TN,
+                preferred_element_type=F32,
+            )
+            d_part[h] = rows.astype(BF).reshape(4, 4, 16, HALF)
+        item = post.send(lambda: d_part.at[o], lambda: d_rc, place.core)
+        agenda.add(3.5, lambda: d_merge(item))
+
+    def d_merge(item):
+        item.wait_recv()
+        d_rc[...] = d_part[c] + d_rc[...]
+        parts = [
+            (lambda n=n: d_rc.at[:, place.a_at[n]], lambda n=n: d_rx.at[n], peer)
+            for n, peer in enumerate(place.a_peers)
+        ]
+        item = post.group(parts, lambda: d_rx, lambda: d_rx)
+        agenda.add(11.0, lambda: d_along_b(item))
+
+    def d_along_b(item):
+        item.wait_recv()
+        d_rc[:, a] = (d_rc[:, a] + d_rx[0]) + (d_rx[1] + d_rx[2])
+        parts = [
+            (lambda n=n: d_rc.at[place.b_at[n], a], lambda n=n: d_rz.at[n], peer)
+            for n, peer in enumerate(place.b_peers)
+        ]
+        item = post.group(parts, lambda: d_rz, lambda: d_rz)
+        agenda.add(6.0, lambda: d_end(item))
+
+    def d_end(item):
+        item.wait_recv()
+        row = (d_rc[b, a] + d_rz[0]) + (d_rz[1] + d_rz[2])
+        found[b, a, :, place.cols] = (row.astype(F32) * EMBED_SCALE).astype(BF)
+        gather_rows(place, post, agenda, found, found_sends)
 
     def ring_start(base, peers, at):
         stat_in[base + at] = stats[...]
@@ -485,16 +500,11 @@
 
     item, base, count = ring_start(0, [place.core], c), 0, 2
     for peers, at in ((place.x_peers, place.x), (place.z_peers, place.z), (place.y_peers, y)):
-        if base:
-            look()
         ring_end(item, base, count)
         base = base + 4
         item, count = ring_start(base, peers, at), 4
-    while looked[0] < NT_COLS:
-        look()
-    agenda.run(agenda.now + 1.5)
     ring_end(item, base, count)
-    piece(2)
+    unpack()
 
     def cap_load(n):
         return pltpu.make_async_copy(
@@ -541,9 +551,9 @@
     loss_sum = sum(
         jnp.sum(w * (jnp.log(stats[k, 0:1, :]) - stats[k, 1:2, :])) for k, w in enumerate(weights)
     )
-    loss_out[...] = jnp.full((8, 128), loss_sum / jnp.maximum(weight_sum, 1.0), F32)
-    for j in (NT_COLS - 2, NT_COLS - 1):
-        post.sent(crossing[j])
+    loss_out[0:8] = jnp.full((8, 128), loss_sum / jnp.maximum(weight_sum, 1.0), F32)
+    loss_out[8:16] = jnp.full((8, 128), most, F32)
+    shape = (4, 4, 4, 16, W)
 
     class Flow:
         def __init__(self, step, j):
@@ -666,15 +676,14 @@
 
             cols = pl.ds(pl.multiple_of((2 * n + h) * W, 128), W)
             product = lax.dot_general(marks[...], normed[:, cols], NN, preferred_element_type=F32)
-            d_stage[h, 0:ROWS] = product.astype(BF)
+            rows = cot_lines[:, :, cols].reshape(ALL_SLOTS, W)
+            embed = lax.dot_general(owner_of[...], rows, NN, preferred_element_type=F32)
+            d_stage[h, 0:ROWS] = (product + embed * embed_scale).astype(BF)
             head_store(n, h).start()
             return carry
 
         lax.fori_loop(0, 2, one, 0)
 
-    for n in range(3, pieces + pieces // 2):
-        agenda.add(2.8 * (n - 3) + 0.1, lambda n=n: piece(n))
-    agenda.add(2.8 * (pieces + pieces // 2 - 3) + 4.0, cot_swap)
     began = agenda.now
 
     def turn(t, carry):
@@ -748,8 +757,6 @@
     lax.fori_loop(0, 16, grad_rows, 0)
     grad_store = pltpu.make_async_copy(found, grad_hbm, local_sems.at[0])
     grad_store.start()
-    for n in range(3):
-        cot_in["swap", n].wait_recv()
     metas_out[...] = metas[...]
     for h in range(2):
         head_store(TG_TURNS - 1, h).wait()
@@ -774,76 +781,45 @@
     grad_store.wait()
 
 
-FAR = 1 << 30
-SLOTS = 128
-
-
-def patch_kernel(
-    metas, own_cot, cot_hbm, head_hbm, out_hbm, grad, cot, left, picks, sums, rows_of, sems
-):
+def deliver_kernel(*refs):
+    ins, outs, (small, large, sems) = refs[:3], refs[3:6], refs[6:]
+    moves = [(ins[n], outs[n], small.at[n], n) for n in range(2)]
+    for i in range(NV):
+        rows = pl.ds(i * MT, MT)
+        moves.append((ins[2].at[rows], outs[2].at[rows], large.at[rows], 2 + i))
+    for src, _, buf, n in moves:
+        pltpu.make_async_copy(src, buf, sems.at[n]).start()
+    for src, dst, buf, n in moves:
+        pltpu.make_async_copy(src, buf, sems.at[n]).wait()
+        pltpu.make_async_copy(buf, dst, sems.at[n]).start()
+    for _, dst, buf, n in moves:
+        pltpu.make_async_copy(buf, dst, sems.at[n]).wait()
+
+
+def around(array, axis):
+    count = lax.axis_size(axis)
+    for _ in range(count - 1):
+        array = lax.ppermute(array, axis, [(i, (i + 1) % count) for i in range(count)])
+        yield array
+
+
+def dense_embedding(ids, embed_cotangent, table, head):
+    local = ids - lax.axis_index(DP_VOCAB) * ROWS
+    inside = (local >= 0) & (local < ROWS)
+    rows = jnp.take(table, jnp.clip(local, 0, ROWS - 1), axis=0)
+    total = jnp.where(inside[:, None], rows, 0)
+    for axis in DP_VOCAB:
+        total = sum(around(total, axis), total)
     g = gray(lax.axis_index("dp"))
-    first = lax.axis_index(DP_VOCAB) * ROWS
-    for k in range(4):
-        @pl.when(g == k)
-        def _():
-            pltpu.make_async_copy(own_cot, cot.at[k], sems.at[k]).start()
-
-        @pl.when(g != k)
-        def _():
-            pltpu.make_async_copy(cot_hbm.at[k], cot.at[k], sems.at[k]).start()
-
-    def tile(ref, i):
-        return ref.at[pl.ds(i * MT, MT)]
-
-    for i in range(NV):
-        pltpu.make_async_copy(tile(head_hbm, i), tile(grad, i), sems.at[4 + i]).start()
-    for k in range(4):
-        local = metas[k, 0:1, :] - first
-        left[k : k + 1, :] = jnp.where((local >= 0) & (local < ROWS), local, FAR)
-    for k in range(4):
-        pltpu.make_async_copy(own_cot, cot.at[k], sems.at[k]).wait()
-    for i in range(NV):
-        pltpu.make_async_copy(tile(head_hbm, i), tile(grad, i), sems.at[4 + i]).wait()
-
-    def one_pass(lowest):
-        picks[...] = jnp.zeros_like(picks)
-
-        def more(state):
-            return (state[0] < SLOTS) & (state[1] < FAR)
-
-        def take(state):
-            n, row = state
-            rows_of[n] = row
-            rest = left[...]
-            same = rest == row
-            for k in range(4):
-                picks[pl.ds(n, 1), k * 256 : (k + 1) * 256] = jnp.where(same[k : k + 1], 1.0, 0.0)
-            rest = jnp.where(same, FAR, rest)
-            left[...] = rest
-            return n + 1, jnp.min(rest)
-
-        count, lowest = lax.while_loop(more, take, (0, lowest))
-        sums[...] = lax.dot_general(
-            picks[...].astype(BF), cot[...].reshape(1024, D), NN, preferred_element_type=F32
-        )
-
-        def patch(n, carry):
-            row = rows_of[n]
-            base = pl.multiple_of((row // 16) * 16, 16)
-            old = grad[pl.ds(base, 16), :]
-            new = (old.astype(F32) + sums[pl.ds(n, 1), :] * EMBED_SCALE).astype(BF)
-            here = lax.broadcasted_iota(jnp.int32, (16, D), 0) == row - base
-            grad[pl.ds(base, 16), :] = jnp.where(here, new, old)
-            return carry
-
-        lax.fori_loop(0, count, patch, 0)
-        return lowest
-
-    lax.while_loop(lambda lowest: lowest < FAR, one_pass, jnp.min(left[...]))
-    for i in range(NV):
-        pltpu.make_async_copy(tile(grad, i), tile(out_hbm, i), sems.at[4 + i]).start()
-    for i in range(NV):
-        pltpu.make_async_copy(tile(grad, i), tile(out_hbm, i), sems.at[4 + i]).wait()
+    own = lax.dynamic_slice_in_dim(total, g * 256, 256, axis=0)
+    embedded = (own.astype(F32) * EMBED_SCALE).astype(BF)
+    y = lax.axis_index("dp")
+    cot = lax.dynamic_update_slice_in_dim(jnp.zeros((1024, D), BF), embed_cotangent, g * 256, axis=0)
+    for off, block in enumerate(around(embed_cotangent, "dp")):
+        cot = lax.dynamic_update_slice_in_dim(cot, block, gray((y - off - 1) % 4) * 256, axis=0)
+    where = jnp.where(inside, local, ROWS)
+    part = jax.ops.segment_sum(cot.astype(F32), where, num_segments=ROWS + 1)[:ROWS]
+    return embedded, (head.astype(F32) + part * EMBED_SCALE).astype(BF)
 
 
 def body(input_ids, target_ids, loss_mask, final_hidden, norm_gain, embed_cotangent, table):
@@ -852,27 +828,26 @@
     dma = pltpu.SemaphoreType.DMA
     V = pltpu.VMEM
     S = jax.ShapeDtypeStruct
-    meta = jnp.pad(jnp.stack([input_ids, target_ids, loss_mask]), ((0, 5), (0, 0)))
-    gain = norm_gain.reshape(1, D)
+    gain = norm_gain.reshape(D // 128, 128)
     n = NT_COLS
-    head, cot, metas, embed, grad, gain_grad, loss, _ = pl.pallas_call(
+    head, metas, embed, grad, gain_grad, loss, _ = pl.pallas_call(
         main_kernel,
         out_shape=(
             S((ROWS, D), BF),
-            S((4, 256, D), BF),
             S((4, 8, 256), jnp.int32),
             S((4, 4, 16, D), BF),
             S((4, 4, 16, D), BF),
             S((D // 128, 128), F32),
-            S((8, 128), F32),
+            S((16, 128), F32),
             S((2, ROWS, 256), F32),
         ),
-        in_specs=[vmem, vmem, vmem, any_, any_],
-        out_specs=(any_, any_, vmem, any_, any_, vmem, vmem, any_),
+        in_specs=[vmem, vmem, vmem, vmem, vmem, any_, any_],
+        out_specs=(any_, vmem, any_, any_, vmem, vmem, any_),
         scratch_shapes=[
             V((ROWS, D), BF),
             V((1024, D), BF),
             V((4, 8, 256), jnp.int32),
+            V((1, D), F32),
             V((ROWS, 1024), BF),
             V((4, 2, 256), F32),
             V((16, 4, 2, 256), F32),
@@ -880,11 +855,17 @@
             V((256, 128), F32),
             V((256, 128), F32),
             V((2, 2048, W), BF),
-            V((n, 4, 4, 4, 16, W), BF),
-            V((n, 3, 4, 4, 16, W), BF),
-            V((n, 3, 4, 16, W), BF),
-            V((n, 3, 16, W), BF),
+            V((2, 4, 4, 16, HALF), BF),
+            V((4, 4, 16, HALF), BF),
+            V((3, 4, 16, HALF), BF),
+            V((3, 16, HALF), BF),
             V((4, 4, 16, D), BF),
+            V((ROWS, ALL_SLOTS), BF),
+            V((ALL_SLOTS, 256), BF),
+            V((4, SLOTS, D), BF),
+            V((4, SLOTS, D), BF),
+            V((4, SLOTS, D), BF),
+            V((4, SLOTS, D), BF),
             V((2, 2048, W), F32),
             V((2, 4, 4, 4, 16, W), I16),
             V((4, 4, 4, 4, 16, W), I16),
@@ -899,8 +880,8 @@
             V((4, 4, 16, D), I16),
             V((4, D // 128, 128), F32),
             dma((5,)),
-            dma((120,)),
-            dma((120,)),
+            dma((48,)),
+            dma((48,)),
             dma((STEPS, n)),
             dma((STEPS, n)),
         ],
@@ -908,32 +889,31 @@
             collective_id=0, has_side_effects=True, vmem_limit_bytes=VMEM_LIMIT
         ),
         name="main",
-    )(meta, final_hidden, gain, table, embed_cotangent)
-
-    table_grad = pl.pallas_call(
-        patch_kernel,
-        out_shape=S((ROWS, D), BF),
-        in_specs=[vmem, any_, any_, any_],
-        out_specs=any_,
-        scratch_shapes=[
-            V((ROWS, D), BF),
-            V((4, 256, D), BF),
-            V((4, 256), jnp.int32),
-            V((SLOTS, 1024), F32),
-            V((SLOTS, D), F32),
-            pltpu.SMEM((SLOTS,), jnp.int32),
-            dma((4 + NV,)),
-        ],
+    )(
+        input_ids.reshape(1, 256),
+        target_ids.reshape(1, 256),
+        loss_mask.reshape(1, 256),
+        final_hidden,
+        gain,
+        table,
+        embed_cotangent.reshape(4, 4, 16, D),
+    )
+
+    embedded, table_grad = lax.cond(
+        loss[8, 0] > SLOTS,
+        lambda: dense_embedding(metas[:, 0, :].reshape(1024), embed_cotangent, table, head),
+        lambda: (embed.reshape(256, D), head),
+    )
+    embedded, grad_hidden, table_grad = pl.pallas_call(
+        deliver_kernel,
+        out_shape=(S((256, D), BF), S((256, D), BF), S((ROWS, D), BF)),
+        in_specs=[any_] * 3,
+        out_specs=(any_,) * 3,
+        scratch_shapes=[V((2, 256, D), BF), V((ROWS, D), BF), dma((2 + NV,))],
         compiler_params=pltpu.CompilerParams(vmem_limit_bytes=VMEM_LIMIT),
-        name="patch",
-    )(metas, embed_cotangent, cot, head)
-    return (
-        embed.reshape(256, D),
-        loss[0, 0],
-        grad.reshape(256, D),
-        gain_grad.reshape(D),
-        table_grad,
-    )
+        name="deliver",
+    )(embedded, grad.reshape(256, D), table_grad)
+    return (embedded, loss[0, 0], grad_hidden, gain_grad.reshape(D), table_grad)
 
 
 def solution(mesh):

time: 173 us -> 142 us (0.82)
  Pallas kernels: 163 us -> 138 us
  local copies, waits for them, and re-layouts: 7.95 us -> 1.81 us
    pallas_call x2, Pallas kernels: 163 us -> 138 us  [the longest x1 125 us: body(): pl.pallas_call(main_kernel, out_shape=(S((ROWS, D), BF), S((4, 8, 256), j...]
    unnamed x7 -> x3, local copies, waits for them, and re-layouts: 4.82 us -> 0.61 us
where the time goes in v3:
time: 142 us
  Pallas kernels  138 us (97%)
  local copies, waits for them, and re-layouts  1.81 us (1%)
    pallas_call x1, Pallas kernels, body(): pl.pallas_call(main_kernel, out_shape=(S((ROWS, D), BF), S((4, 8, 256), j...  125 us
    pallas_call x1, Pallas kernels, body(): pl.pallas_call(deliver_kernel, out_shape=(S((256, D), BF), S((256, D), BF...  12.7 us

profile of v3, /device:TPU:1, one launch (start us, length us, event | category | flops | bytes accessed | tf_op | source)
XLA Modules:
  0.0 141.7 jit_solution(10321611270871964713)
XLA Ops:
  0.6 125.5 %main.1 = (bf16[2000,3584]{1,0:T(8,128)(2,1)}, s32[4,8,256]{2,1,0:T(8,128)S(1)}, bf16[4,4,16,3584]{3,2,1,0:T(8,128)(2,1)}, bf16[4,4,16,3584]{3,2,1,0:T(8,128)(2,...) custom-call(s32[1,256]{1,0:T(1,128)} %bitcast.32, s32[1,256]{1,0:T(1,128)} %bitcast.33, ...), custom_call_target="tpu_custom_call" | custom-call | tf_op jit(solution)/shard_map/main/pallas_call | solution.py:833
  126.1 1.2 fusion.6
  128.0 0.3 conditional.1
  128.3 0.0 copy-start.2
  128.3 12.7 %deliver.1 = (bf16[256,3584]{1,0:T(8,128)(2,1)}, bf16[256,3584]{1,0:T(8,128)(2,1)}, bf16[2000,3584]{1,0:T(8,128)(2,1)}) custom-call(bf16[256,3584]{1,0:T(8,128)(2,1)} %get-tuple-element.38.refs_0_, bf16[256,3584]{1,0:T(8,128)(2,1)} %bitcast.24, bf16[2000,3584]{1,0:T(8,128)(2,1)} %get-tuple-element.40.refs_2_), custom_call_target="tpu_custom_call" | custom-call | tf_op jit(solution)/shard_map/deliver/pallas_call | solution.py:907
  141.0 0.0 copy-done.2
  141.1 0.6 copy.25
Async XLA Ops:
  128.3 12.8 %copy-start.2 = (f32[28,128]{1,0:T(8,128)S(1)}, f32[28,128]{1,0:T(8,128)}, u32[]{:S(2)}) copy-start(f32[28,128]{1,0:T(8,128)} %get-tuple-element.43) | copy-start | bytes 43012

commit v4 on v3

--- a/solution.py
+++ b/solution.py
@@ -13,6 +13,8 @@
 D = 3584
 ROWS = 2000
 EMBED_SCALE = math.sqrt(D)
+SCALE_HIGH = 59.75
+SCALE_LOW = EMBED_SCALE - SCALE_HIGH
 DP_VOCAB = ("dp", "vocab_0", "vocab_1", "vocab_2")
 MESH = pl.DeviceIdType.MESH
 BF = jnp.bfloat16
@@ -27,6 +29,7 @@
 HALF = D // 2
 W = 256
 NT_COLS = HALF // W
+EARLY = 4
 SLOTS = 32
 ALL_SLOTS = 4 * SLOTS
 VMEM_LIMIT = 66_900_000
@@ -69,18 +72,27 @@
         self.b = z + c * (x - z)
         self.a_peers = [self._at((self.a + off) % 4, self.b) for off in (1, 2, 3)]
         self.b_peers = [self._at(self.a, (self.b + off) % 4) for off in (1, 2, 3)]
-        self.x_peers = [{"vocab_1": (x + off) % 4} for off in (1, 2, 3)]
-        self.z_peers = [{"vocab_0": (z + off) % 4} for off in (1, 2, 3)]
+        cores = [(off, core) for off in range(4) for core in (self.c, self.o)][1:]
+        self.line = [{"vocab_1": (x + off) % 4, "vocab_2": core} for off, core in cores]
+        planes = [(up, over) for up in range(4) for over in range(4)][1:]
+        self.sheet = [{"vocab_0": (z + up) % 4, "dp": (y + over) % 4} for up, over in planes]
         self.y_peers = [{"dp": (y + off) % 4} for off in (1, 2, 3)]
         self.cols = pl.ds(pl.multiple_of(c * HALF, 128), HALF)
         self.a_at = [(self.a + off) % 4 for off in (1, 2, 3)]
         self.b_at = [(self.b + off) % 4 for off in (1, 2, 3)]
         self.y_at = [gray((y + off) % 4) for off in (1, 2, 3)]
         a, b = self.a, self.b
-        a0, a1, b0 = (a + a // 2) % 2, a // 2, (b + b // 2) % 2
-        self.colour = (a0 + b0) % 2 + 2 * ((a1 + b0) % 2)
+        a0, a1, b0, b1 = (a + a // 2) % 2, a // 2, (b + b // 2) % 2, b // 2
+        self.colours = [(a0 + third) % 2 + 2 * ((a1 + third) % 2) for third in (b0, b1)]
         flip_a, flip_b = a + 1 - 2 * (a % 2), b + 1 - 2 * (b % 2)
-        self.near = [self._at(flip_a, b), self._at(3 - a, b), self._at(a, flip_b)]
+        first, second = self._at(flip_a, b), self._at(3 - a, b)
+        self.near = [
+            [first, second, self._at(a, flip_b)],
+            [second, first, self._at(a, 3 - b)],
+        ]
+        self.parts = [
+            pl.ds(pl.multiple_of(c * HALF + part * (HALF // 2), 128), HALF // 2) for part in range(2)
+        ]
 
     def _at(self, a, b):
         return {"vocab_1": a + self.c * (b - a), "vocab_0": b + self.c * (a - b)}
@@ -92,7 +104,7 @@
         return (((gray(k) * 4 + self.z) * 4 + self.x) * 2 + self.c) * ROWS
 
     def meet(self):
-        peers = [self.core] + self.x_peers + self.z_peers + self.y_peers
+        peers = self.line + self.sheet
         barrier = pltpu.get_barrier_semaphore()
         for peer in peers:
             pl.semaphore_signal(barrier, inc=1, device_id=peer, device_id_type=MESH)
@@ -100,9 +112,20 @@
 
 
 class Sent:
-    def __init__(self, sems, at, out_like, in_like, times):
-        self.sems, self.at = sems, at
+    def __init__(self, sems, at, parts, out_like, in_like, times):
+        self.sems, self.at, self.parts = sems, at, parts
         self.out_like, self.in_like, self.times = out_like, in_like, times
+
+    def start(self):
+        for src, dst, peer in self.parts:
+            pltpu.make_async_remote_copy(
+                src_ref=src(),
+                dst_ref=dst(),
+                send_sem=self.sems[0].at[self.at],
+                recv_sem=self.sems[1].at[self.at],
+                device_id=peer,
+                device_id_type=MESH,
+            ).start()
 
     def wait_send(self):
         for _ in range(self.times):
@@ -124,16 +147,12 @@
         return self.group([(src, dst, peer)], src, dst)
 
     def group(self, parts, out_like, in_like, times=1):
-        for src, dst, peer in parts:
-            pltpu.make_async_remote_copy(
-                src_ref=src(),
-                dst_ref=dst(),
-                send_sem=self.sems[0].at[self.used],
-                recv_sem=self.sems[1].at[self.used],
-                device_id=peer,
-                device_id_type=MESH,
-            ).start()
-        sent = Sent(self.sems, self.used, out_like, in_like, times)
+        sent = self.plan(parts, out_like, in_like, times)
+        sent.start()
+        return sent
+
+    def plan(self, parts, out_like, in_like, times=1):
+        sent = Sent(self.sems, self.used, parts, out_like, in_like, times)
         self.used += 1
         self.open.append(sent)
         return sent
@@ -146,6 +165,11 @@
         for item in self.open:
             item.wait_send()
         self.open = []
+
+
+class Seen:
+    def wait_recv(self):
+        pass
 
 
 class Agenda:
@@ -177,13 +201,13 @@
         self.run(self.now)
 
 
-def columns(table, j):
-    left = pl.ds(pl.multiple_of(j * W, 128), W)
-    right = pl.ds(pl.multiple_of(HALF + j * W, 128), W)
-    return jnp.concatenate([table[:, left], table[:, right]], axis=1)
-
-
-def gather_rows(place, post, agenda, buf, sends):
+def columns(table, j, core):
+    own = pl.ds(pl.multiple_of(core * HALF + j * W, 128), W)
+    other = pl.ds(pl.multiple_of((1 - core) * HALF + j * W, 128), W)
+    return jnp.concatenate([table[:, own], table[:, other]], axis=1)
+
+
+def gather_rows(place, post, agenda, buf, sends, done):
     a, b, cols = place.a, place.b, place.cols
 
     def mine():
@@ -207,29 +231,34 @@
         first.wait_recv()
         second = post.group([(row, row, peer) for peer in place.a_peers], rows, rows)
         sends.append(second)
-        agenda.add(10.0, lambda: across(second))
+        agenda.add(14.0, lambda: across(second))
 
     def across(second):
         second.wait_recv()
         third = post.send(half, half, place.core)
         sends.append(third)
-        agenda.add(4.0, third.wait_recv)
-
-    agenda.add(6.0, along_a)
-
-
-STEPS = 7
-LAG = (1, 4, 6, 8, 10, 12, 13)
-TG_TURNS = NT_COLS
-TURNS = NT_COLS + LAG[-1]
+        agenda.add(5.0, lambda: finish(third))
+
+    def finish(third):
+        third.wait_recv()
+        done()
+
+    agenda.add(8.0, along_a)
+
+
+STEPS = 8
+LAG = (1, 3, 5)
+TAIL_AT = ((1, 2), (4, 2), (6, 1), (8, 1), (10, 1), (12, 1), (14, 1), (15, 1))
+HEAD_TILES = 2 * NT_COLS
+TAIL = TAIL_AT[-1][0] + 1
 
 
 def main_kernel(
     own_ids, own_targets, own_mask, hidden, gain_in_rows, table_hbm, cot_hbm,
     head_hbm, metas_out, embed_hbm, grad_hbm, gain_out, loss_out, cap_hbm,
-    table, normed, metas, gain, marks, stats, stat_in, scale_rows, back_rows, inverses,
-    d_stage, d_part, d_rc, d_rx, d_rz, found, owner_of, slot_of, packed, lines, cot_packed, cot_lines,
-    stage, snd, rc, sx, rx, acc, sz, rz, acc_z, sy, ry, up,
+    table, normed, metas, gain, marks, stats, stat_in, scale_rows, back_rows, inverses, dots,
+    d_stage, d_part, d_rc, d_rx, d_rz, found, owner_of, slot_of, packed, lines, cot_packed,
+    stage, snd, rc, sx, rx, s_two, r_two, acc, acc_two, sz, rz, acc_z, sy, ry, up,
     gain_in, local_sems, send_sems, recv_sems, flow_send, flow_recv,
 ):
     place = Place()
@@ -239,8 +268,12 @@
     a, b, c, o, g, y = place.a, place.b, place.c, place.o, place.g, place.y
     blocks = [g, place.ga, place.gb, place.gc]
     entered = place.meet()
-    table_load = pltpu.make_async_copy(table_hbm, table, local_sems.at[0])
-    table_load.start()
+    def table_load(i):
+        rows = pl.ds(i * 1024, 1024 - 48 * i)
+        return pltpu.make_async_copy(table_hbm.at[rows], table.at[rows], local_sems.at[5 * i])
+
+    table_load(0).start()
+    table_load(1).start()
     metas[g, 0:1, :] = own_ids[...]
     metas[g, 1:2, :] = own_targets[...]
     metas[g, 2:3, :] = own_mask[...]
@@ -254,10 +287,8 @@
     def rows_of(block, first, count):
         return pl.ds(pl.multiple_of(block * 256 + first, 16), count)
 
-    quarter = place.colour
-
     def normalise(i, carry):
-        at = ((quarter + i) % 4) * 64
+        at = i * 64
         rows = pl.ds(pl.multiple_of(at, 16), 64)
         wide = hidden[rows, :].astype(F32)
         inv = inverse(wide)
@@ -265,61 +296,64 @@
         normed[rows_of(g, at, 64), :] = (wide * inv * gain[...]).astype(BF)
         return carry
 
-    normalise(0, 0)
+    lax.fori_loop(0, 4, normalise, 0)
     stats[...] = jnp.zeros_like(stats)
     entered()
 
-    def ship(block, first, count, peer):
-        def part():
-            return normed.at[rows_of(block, first, count), place.cols]
-
-        return post.send(part, part, peer)
-
-    at_q = quarter * 64
+    def ship(block, part, half, peer):
+        def rows():
+            at = place.colours[part] * 64 + half * 32
+            return normed.at[rows_of(block, at, 32), place.parts[part]]
+
+        return post.send(rows, rows, peer)
+
     meta_in = [
         post.send(lambda: metas.at[g], lambda: metas.at[g], peer) for peer in (place.y_a, place.y_b)
     ]
-    a_low = ship(g, at_q, 32, place.y_a)
-    b_high = ship(g, at_q + 32, 32, place.y_b)
-    a_high = ship(g, at_q + 32, 32, place.y_a)
-    b_low = ship(g, at_q, 32, place.y_b)
-    lax.fori_loop(1, 4, normalise, 0)
-    for item in meta_in:
-        item.wait_recv()
-    meta_c = post.send(lambda: metas.at[place.ga], lambda: metas.at[place.ga], place.y_b)
-    spread = {}
-    swaps = {}
+    both = (0, 1)
+    a_low = [ship(g, part, 0, place.y_a) for part in both]
+    b_high = [ship(g, part, 1, place.y_b) for part in both]
+    a_high = [ship(g, part, 1, place.y_a) for part in both]
+    b_low = [ship(g, part, 0, place.y_b) for part in both]
+    meta_c = post.plan(
+        [(lambda: metas.at[place.ga], lambda: metas.at[place.ga], place.y_b)],
+        lambda: metas.at[place.ga],
+        lambda: metas.at[place.gc],
+    )
+    spread = {"a": [], "b": [], "c": []}
     relays = []
 
-    def relay():
-        a_low.wait_recv()
-        relays.append(ship(place.ga, at_q, 32, place.y_b))
-        b_high.wait_recv()
-        relays.append(ship(place.gb, at_q + 32, 32, place.y_a))
-
-    def spread_block(name, block, items):
-        for item in items:
+    def swap(block):
+        def part():
+            return normed.at[rows_of(block, 0, 256), place.cols]
+
+        return post.plan([(part, part, place.core)], part, part)
+
+    swaps = {"a": swap(place.ga), "b": swap(place.gb), "c": swap(place.gc)}
+
+    def spread_piece(name, block, half, items):
+        for part, item in enumerate(items):
             item.wait_recv()
-        spread[name] = [ship(block, at_q, 64, peer) for peer in place.near]
-
-    def swap_block(name, block):
+            spread[name] += [ship(block, part, half, peer) for peer in place.near[part]]
+
+    def swap_block(name):
         for item in spread[name]:
             item.wait_recv()
-        swaps[name] = ship(block, 0, 256, place.core)
+        swaps[name].start()
 
     def cap_store(n):
         return pltpu.make_async_copy(
             stage.at[n, pl.ds(0, ROWS)], cap_hbm.at[n], local_sems.at[1 + n]
         )
 
-    def forward(n):
-        block, side = blocks[n], n % 2
-        if n >= 2:
-            cap_store(side).wait()
+    def forward(n, block, between):
+        side = n % 2
         rows = normed[rows_of(block, 0, 256), :]
         total = jnp.zeros((1, 256), F32)
         picked = total
         for at in range(0, ROWS, MF):
+            if at == 4 * MF:
+                between()
             size = min(MF, ROWS - at)
             logits = lax.dot_general(table[at : at + size, :], rows, NT, preferred_element_type=F32)
             capped = SOFTCAP * jnp.tanh(logits * (1.0 / SOFTCAP))
@@ -330,16 +364,28 @@
             picked += jnp.sum(jnp.where(hit, capped, 0.0), axis=0, keepdims=True)
         stats[block, 0:1, :] = total
         stats[block, 1:2, :] = picked
-        if n < 2:
-            cap_store(side).start()
-
-    table_load.wait()
-    agenda.now = 4.5
-    agenda.compute(4.0, lambda: forward(0))
-
+
+    seen = [Seen(), Seen()]
+
+    def pass_on():
+        table_load(1).wait()
+        for item in meta_in:
+            item.wait_recv()
+        meta_c.start()
+        for part in both:
+            a_low[part].wait_recv()
+            b_high[part].wait_recv()
+            relays.append(
+                (ship(place.ga, part, 0, place.y_b), ship(place.gb, part, 1, place.y_a))
+            )
+        spread_piece("a", place.ga, 0, seen)
+
+    table_load(0).wait()
+    forward(0, g, pass_on)
+    cap_store(0).start()
+    spread_piece("a", place.ga, 1, a_high)
 
     meta_c.wait_recv()
-    relay()
     ids = [metas[k, 0:1, :] for k in range(4)]
     locals_ = [row - first_row for row in ids]
     for k in range(4):
@@ -378,22 +424,27 @@
         wanted = jnp.where(here, read[k : k + 1] * 64.0 + read[4 + k : 5 + k], wanted)
     wanted = jnp.where(read[8:9] > 0.5, wanted, -1.0)
 
-    def mark(i, carry):
-        rows = pl.ds(pl.multiple_of(i * MT, 16), MT)
-        at = lax.broadcasted_iota(jnp.int32, (MT, ALL_SLOTS), 0) + i * MT
-        owner_of[rows, :] = jnp.where(at.astype(F32) == wanted, 1.0, 0.0).astype(BF)
-        return carry
-
-    lax.fori_loop(0, NV, mark, 0)
     starts = lax.broadcasted_iota(jnp.int32, (128, 256), 0) * ROWS
     most = jnp.float32(0.0)
     for row in ids:
         held = jnp.where((row >= starts) & (row < starts + ROWS), 1.0, 0.0)
         most = jnp.maximum(most, jnp.max(jnp.sum(held, axis=1, keepdims=True)))
-    embed_scale = jnp.where(most <= SLOTS, EMBED_SCALE, 0.0)
-
-    spread_block("a", place.ga, [a_high])
-    spread_block("b", place.gb, [b_low])
+    keep = jnp.where(most <= SLOTS, 1.0, 0.0)
+
+    def mark(i, carry):
+        rows = pl.ds(pl.multiple_of(i * MT, 16), MT)
+        at = lax.broadcasted_iota(jnp.int32, (MT, ALL_SLOTS), 0) + i * MT
+        same = at.astype(F32) == wanted
+        owner_of[rows, :] = jnp.where(same, 1.0, 0.0).astype(BF)
+        marks[rows, 1024:1152] = jnp.where(same, keep * SCALE_HIGH, 0.0).astype(BF)
+        marks[rows, 1152:1280] = jnp.where(same, keep * SCALE_LOW, 0.0).astype(BF)
+        return carry
+
+
+    lax.fori_loop(0, NV, mark, 0)
+
+    spread_piece("b", place.gb, 1, seen)
+    spread_piece("b", place.gb, 0, b_low)
 
     def look_up(j, carry):
         cols = pl.ds(pl.multiple_of(j * 2 * W, 128), 2 * W)
@@ -401,9 +452,20 @@
         packed[:, :, cols] = rows.astype(BF).reshape(4, SLOTS, 2 * W)
         return carry
 
-    lax.fori_loop(0, 3, look_up, 0)
-    spread_block("c", place.gc, relays)
-    cot_load.wait()
+    def exchange(src, dst):
+        dst[g] = src[g]
+        parts = [
+            (lambda n=n: src.at[place.y_at[n]], lambda: dst.at[g], peer)
+            for n, peer in enumerate(place.y_peers)
+        ]
+        return post.group(parts, lambda: src.at[0:3], lambda: dst.at[0:3])
+
+    lax.fori_loop(0, EARLY, look_up, 0)
+    spread_piece("c", place.gc, 0, [pair[0] for pair in relays])
+    spread_piece("c", place.gc, 1, [pair[1] for pair in relays])
+    swap_block("a")
+    lax.fori_loop(EARLY, NT_COLS, look_up, 0)
+    line_item = exchange(packed, lines)
 
     def cot_pack(j, carry):
         cols = pl.ds(pl.multiple_of(j * 2 * W, 128), 2 * W)
@@ -413,36 +475,46 @@
         cot_packed[:, :, cols] = rows.astype(BF).reshape(4, SLOTS, 2 * W)
         return carry
 
-    lax.fori_loop(0, NT_COLS, cot_pack, 0)
-
-    def exchange(src, dst):
-        dst[g] = src[g]
-        parts = [
-            (lambda n=n: src.at[place.y_at[n]], lambda: dst.at[g], peer)
-            for n, peer in enumerate(place.y_peers)
-        ]
-        return post.group(parts, lambda: src.at[0:3], lambda: dst.at[0:3])
-
-    lax.fori_loop(3, NT_COLS, look_up, 0)
-    line_item = exchange(packed, lines)
-    cot_item = exchange(cot_packed, cot_lines)
-
-    swap_block("a", place.ga)
-    swap_block("b", place.gb)
-    agenda.now = max(agenda.now, 23.0)
-    swaps["a"].wait_recv()
-    agenda.compute(4.3, lambda: forward(1))
-    swap_block("c", place.gc)
-    swaps["b"].wait_recv()
-    agenda.compute(4.3, lambda: forward(2))
-    swaps["c"].wait_recv()
-    agenda.compute(4.3, lambda: forward(3))
+    def later_block(n, carry):
+        block = jnp.where(n == 1, place.ga, jnp.where(n == 2, place.gb, place.gc))
+
+        @pl.when(n == 1)
+        def _():
+            swaps["a"].wait_recv()
+
+        @pl.when(n == 2)
+        def _():
+            swaps["b"].wait_recv()
+            cap_store(0).wait()
+
+        @pl.when(n == 3)
+        def _():
+            swaps["c"].wait_recv()
+            cap_store(1).wait()
+
+        def between():
+            @pl.when(n == 1)
+            def _():
+                swap_block("b")
+
+            @pl.when(n == 2)
+            def _():
+                swap_block("c")
+
+        forward(n, block, between)
+
+        @pl.when(n == 1)
+        def _():
+            cap_store(1).start()
+
+        return carry
+
+    lax.fori_loop(1, 4, later_block, 0)
 
     found_sends = []
 
     def unpack():
         line_item.wait_recv()
-        cot_item.wait_recv()
         for h in range(2):
             rows = lax.dot_general(
                 slot_of[...],
@@ -451,8 +523,7 @@
                 preferred_element_type=F32,
             )
             d_part[h] = rows.astype(BF).reshape(4, 4, 16, HALF)
-        item = post.send(lambda: d_part.at[o], lambda: d_rc, place.core)
-        agenda.add(3.5, lambda: d_merge(item))
+        return post.send(lambda: d_part.at[o], lambda: d_rc, place.core)
 
     def d_merge(item):
         item.wait_recv()
@@ -462,7 +533,7 @@
             for n, peer in enumerate(place.a_peers)
         ]
         item = post.group(parts, lambda: d_rx, lambda: d_rx)
-        agenda.add(11.0, lambda: d_along_b(item))
+        agenda.add(9.0, lambda: d_along_b(item))
 
     def d_along_b(item):
         item.wait_recv()
@@ -472,13 +543,21 @@
             for n, peer in enumerate(place.b_peers)
         ]
         item = post.group(parts, lambda: d_rz, lambda: d_rz)
-        agenda.add(6.0, lambda: d_end(item))
+        agenda.add(12.0, lambda: d_end(item))
 
     def d_end(item):
         item.wait_recv()
         row = (d_rc[b, a] + d_rz[0]) + (d_rz[1] + d_rz[2])
         found[b, a, :, place.cols] = (row.astype(F32) * EMBED_SCALE).astype(BF)
-        gather_rows(place, post, agenda, found, found_sends)
+        gather_rows(place, post, agenda, found, found_sends, embed_done)
+
+    def embed_store():
+        return pltpu.make_async_copy(found, embed_hbm, local_sems.at[0])
+
+    def embed_done():
+        embed_store().start()
+        for item in found_sends:
+            post.sent(item)
 
     def ring_start(base, peers, at):
         stat_in[base + at] = stats[...]
@@ -498,13 +577,16 @@
             total = total + stat_in[base + i]
         stats[...] = total
 
-    item, base, count = ring_start(0, [place.core], c), 0, 2
-    for peers, at in ((place.x_peers, place.x), (place.z_peers, place.z), (place.y_peers, y)):
-        ring_end(item, base, count)
-        base = base + 4
-        item, count = ring_start(base, peers, at), 4
-    ring_end(item, base, count)
-    unpack()
+    item = ring_start(0, place.line, place.x * 2 + c)
+    half_item = unpack()
+    ring_end(item, 0, 8)
+    item = ring_start(8, place.sheet, place.z * 4 + y)
+    cot_load.wait()
+    lax.fori_loop(0, NT_COLS, cot_pack, 0)
+    ring_end(item, 8, 16)
+    cot_item = exchange(cot_packed, normed.at[pl.ds(1024, ALL_SLOTS)].reshape(4, SLOTS, D))
+    agenda.now = 40.0
+    d_merge(half_item)
 
     def cap_load(n):
         return pltpu.make_async_copy(
@@ -583,138 +665,173 @@
         def _():
             Flow(0, t - 2).sent(snd.at[slot])
 
-        product = lax.dot_general(marks[...], columns(table, t), TN, preferred_element_type=F32)
-        for side in range(2):
-            for half in range(2):
-                at = side * W + half * 128
-                stage[slot, side * 1024 : side * 1024 + 1024, half * 128 : half * 128 + 128] = (
-                    product[:, at : at + 128] * scale_rows[...]
-                )
-        there = pl.ds(pl.multiple_of(o * 1024, 16), 1024)
-        snd[slot] = encode(stage[slot, there, :]).reshape(*shape)
+        product = lax.dot_general(
+            marks[:, 0:1024], columns(table, t, c), TN, preferred_element_type=F32
+        )
+        for half in range(2):
+            lanes = slice(half * 128, half * 128 + 128)
+            other = slice(W + half * 128, W + half * 128 + 128)
+            stage[slot, 0:1024, lanes] = product[:, lanes] * scale_rows[...]
+            code = encode(product[:, other] * scale_rows[...])
+            snd[slot, :, :, :, :, lanes] = code.reshape(4, 4, 4, 16, 128)
         Flow(0, t).start([(snd.at[slot], rc.at[t % 4], place.core)])
 
     def held(slot, at):
-        whole = stage.at[slot, pl.ds(pl.multiple_of(c * 1024, 16), 1024)].reshape(*shape)
+        whole = stage.at[slot, pl.ds(0, 1024)].reshape(*shape)
         return whole[:, :, at]
+
+    near_a = (a + 1 - 2 * (a % 2), 3 - a)
+
+    def partners(j):
+        first = near_a[0] + (j % 2) * (near_a[1] - near_a[0])
+        second = near_a[1] + (j % 2) * (near_a[0] - near_a[1])
+        return first, second
 
     def merge(j):
         slot = j % 2
+        first, second = partners(j)
         Flow(0, j).here(rc.at[j % 4])
 
         @pl.when(j >= 2)
         def _():
             Flow(1, j - 2).sent(sx.at[slot])
 
+        for n, at in enumerate((first, (a + 2) % 4)):
+            sx[slot, n] = encode(held(slot, at) + decode(rc[j % 4, :, :, at]))
+        Flow(1, j).start([(sx.at[slot], rx.at[j], place._at(first, b))])
         acc[j] = held(slot, a) + decode(rc[j % 4, :, :, a])
-        parts = []
-        for n, peer in enumerate(place.a_peers):
-            at = place.a_at[n]
-            sx[slot, n] = encode(held(slot, at) + decode(rc[j % 4, :, :, at]))
-            parts.append((sx.at[slot, n], rx.at[j, n], peer))
-        Flow(1, j).start(parts)
+        acc_two[j % 3] = held(slot, second) + decode(rc[j % 4, :, :, second])
+
+    def second_half(j):
+        _, second = partners(j)
+        Flow(1, j).here(rx.at[j])
+
+        @pl.when(j >= 2)
+        def _():
+            Flow(2, j - 2).sent(s_two.at[j % 2])
+
+        s_two[j % 2] = encode(acc_two[j % 3] + decode(rx[j, 1]))
+        Flow(2, j).start([(s_two.at[j % 2], r_two.at[j], place._at(second, b))])
+        acc[j] = acc[j] + decode(rx[j, 0])
 
     def along_b(j):
-        Flow(1, j).here(rx.at[j])
+        Flow(2, j).here(r_two.at[j])
         parts = []
         for n in range(4):
             at = (b + n) % 4
-            value = acc[j, :, at] + decode(rx[j, 0, :, at])
-            value = value + decode(rx[j, 1, :, at]) + decode(rx[j, 2, :, at])
+            value = acc[j, :, at] + decode(r_two[j, :, at])
             if n == 0:
                 acc_z[j] = value
             else:
                 sz[j, n - 1] = encode(value)
                 parts.append((sz.at[j, n - 1], rz.at[j, n - 1], place.b_peers[n - 1]))
-        Flow(2, j).start(parts)
+        Flow(3, j).start(parts)
 
     def along_y(j):
-        Flow(2, j).here(rz.at[j])
+        Flow(3, j).here(rz.at[j])
         acc_z[j] = acc_z[j] + decode(rz[j, 0]) + decode(rz[j, 1]) + decode(rz[j, 2])
         parts = []
         for n, peer in enumerate(place.y_peers):
             sy[j, n] = encode(acc_z[j, place.y_at[n]])
             parts.append((sy.at[j, n], ry.at[j, n], peer))
-        Flow(3, j).start(parts)
+        Flow(4, j).start(parts)
 
     def give_b(j):
-        Flow(3, j).here(ry.at[j])
+        Flow(4, j).here(ry.at[j])
         value = acc_z[j, g] + decode(ry[j, 0]) + decode(ry[j, 1]) + decode(ry[j, 2])
         cols = place.tile_cols(j)
         up[b, a, :, cols] = encode(value)
         part = up.at[b, a, :, cols]
-        Flow(4, j).start([(part, part, peer) for peer in place.b_peers])
+        Flow(5, j).start([(part, part, peer) for peer in place.b_peers])
 
     def give_a(j):
         cols = place.tile_cols(j)
-        Flow(4, j).here(up.at[0:3, 0, :, cols])
+        Flow(5, j).here(up.at[0:3, 0, :, cols])
         part = up.at[:, a, :, cols]
-        Flow(5, j).start([(part, part, peer) for peer in place.a_peers])
+        Flow(6, j).start([(part, part, peer) for peer in place.a_peers])
 
     def give_core(j):
         cols = place.tile_cols(j)
-        Flow(5, j).here(up.at[:, 0:3, :, cols])
+        Flow(6, j).here(up.at[:, 0:3, :, cols])
         part = up.at[:, :, :, cols]
-        Flow(6, j).start([(part, part, place.core)])
+        Flow(7, j).start([(part, part, place.core)])
 
     def last(j):
-        Flow(6, j).here(up.at[:, :, :, place.tile_cols(j)])
-
-    steps = (merge, along_b, along_y, give_b, give_a, give_core, last)
-
-    def head_store(n, h):
-        cols = pl.ds(pl.multiple_of((2 * n + h) * W, 128), W)
+        cols = place.tile_cols(j)
+        Flow(7, j).here(up.at[:, :, :, cols])
+        down, inv = back_rows[...], inverses[...]
+        for h in range(2):
+            for q in range(W // 128):
+                at = h * HALF + j * W + q * 128
+                cols = pl.ds(pl.multiple_of(at, 128), 128)
+                value = decode(up[:, :, :, cols].reshape(256, 128)) * down
+                product = value * hidden[:, cols].astype(F32)
+                dots[...] += product * gain[:, cols]
+                gain_in[y, pl.ds(h * (HALF // 128) + j * 2 + q, 1), :] = jnp.sum(
+                    product * inv, axis=0, keepdims=True
+                )
+
+    steps = (merge, second_half, along_b, along_y, give_b, give_a, give_core, last)
+
+    def head_store(n):
+        cols = pl.ds(pl.multiple_of(n * W, 128), W)
         return pltpu.make_async_copy(
-            d_stage.at[h, pl.ds(0, ROWS)], head_hbm.at[:, cols], local_sems.at[3 + h]
+            d_stage.at[n % 2, pl.ds(0, ROWS)], head_hbm.at[:, cols], local_sems.at[3 + n % 2]
         )
 
-    def head_tiles(n):
-        def one(h, carry):
-            @pl.when(n > 0)
-            def _():
-                head_store(n - 1, h).wait()
-
-            cols = pl.ds(pl.multiple_of((2 * n + h) * W, 128), W)
-            product = lax.dot_general(marks[...], normed[:, cols], NN, preferred_element_type=F32)
-            rows = cot_lines[:, :, cols].reshape(ALL_SLOTS, W)
-            embed = lax.dot_general(owner_of[...], rows, NN, preferred_element_type=F32)
-            d_stage[h, 0:ROWS] = (product + embed * embed_scale).astype(BF)
-            head_store(n, h).start()
-            return carry
-
-        lax.fori_loop(0, 2, one, 0)
-
-    began = agenda.now
-
-    def turn(t, carry):
-        @pl.when(t < NT_COLS)
+    def head_tile(n):
+        @pl.when(n >= 2)
         def _():
-            pull(t)
-
-        @pl.when((t >= NT_COLS) & (t < NT_COLS + TG_TURNS))
-        def _():
-            head_tiles(t - NT_COLS)
-
-        for lag, step in zip(LAG, steps):
-            @pl.when((t >= lag) & (t < lag + NT_COLS))
-            def _():
-                step(t - lag)
-
-        for k in range(TURNS):
-            due = began + 2.8 * (k + 1)
+            head_store(n - 2).wait()
+
+        cols = pl.ds(pl.multiple_of(n * W, 128), W)
+        product = lax.dot_general(marks[...], normed[:, cols], NN, preferred_element_type=F32)
+        d_stage[n % 2, 0:ROWS] = product.astype(BF)
+        head_store(n).start()
+
+    def take_due(t, turns, pace):
+        for k in range(turns):
+            due = agenda.now + pace
             if agenda.due(due):
                 @pl.when(t == k)
                 def _():
                     agenda.run(due)
-                    agenda.now = max(agenda.now, due)
             agenda.now = max(agenda.now, due)
+
+    def turn(t, carry):
+        pull(t)
+        for lag, step in zip(LAG, steps):
+            @pl.when(t >= lag)
+            def _():
+                step(t - lag)
+
+        take_due(t, NT_COLS, 2.8)
         return carry
 
-    lax.fori_loop(0, TURNS, turn, 0)
+    dots[...] = jnp.zeros_like(dots)
+    lax.fori_loop(0, NT_COLS, turn, 0)
+    cot_item.wait_recv()
+    normed[1152:1280, :] = normed[1024:1152, :]
+
+    def tail(t, carry):
+        @pl.when(t < HEAD_TILES)
+        def _():
+            head_tile(t)
+
+        for n, ((at, pace), step) in enumerate(zip(TAIL_AT, steps)):
+            begun = NT_COLS - LAG[n] if n < len(LAG) else 0
+            ahead = at - t
+            j = NT_COLS - 1 - ahead // pace
+
+            @pl.when((ahead >= 0) & (ahead % pace == 0) & (j >= begun))
+            def _():
+                step(j)
+
+        take_due(t, TAIL, 1.9)
+        return carry
+
+    lax.fori_loop(0, TAIL, tail, 0)
     agenda.run()
-
-    embed_store = pltpu.make_async_copy(found, embed_hbm, local_sems.at[0])
-    embed_store.start()
 
     GR = 16
 
@@ -724,14 +841,6 @@
         value = decode(up[i // 4, i % 4]) * jnp.concatenate([down] * (D // 128), axis=1)
         return value, hidden[rows, :].astype(F32), inverses[rows, :]
 
-    def gain_rows(i, total):
-        value, wide, inv = upstream(i)
-        product = value * wide * jnp.concatenate([inv] * (D // 128), axis=1)
-        return total + (product[0:8] + product[8:16])
-
-    part = jnp.sum(lax.fori_loop(0, 16, gain_rows, jnp.zeros((8, D), F32)), axis=0, keepdims=True)
-    gain_in[y] = jnp.concatenate([part[:, i * 128 : (i + 1) * 128] for i in range(D // 128)], axis=0)
-
     def gain_part():
         return gain_in.at[y]
 
@@ -740,45 +849,47 @@
         lambda: gain_in.at[0:3],
         lambda: gain_in.at[0:3],
     )
-    embed_store.wait()
-    for item in found_sends:
-        post.sent(item)
+    embed_store().wait()
 
     def grad_rows(i, carry):
         value, wide, inv = upstream(i)
-        scaled_up = value * gain[...]
-        mean_dot = jnp.sum(scaled_up * wide, axis=1, keepdims=True) * (1.0 / D)
+        rows = pl.ds(pl.multiple_of(i * GR, 16), GR)
+        mean_dot = jnp.sum(dots[rows, :], axis=1, keepdims=True) * (1.0 / D)
         pull_back = inv * inv * inv * mean_dot
-        out = jnp.concatenate([inv] * (D // 128), axis=1) * scaled_up
+        out = jnp.concatenate([inv] * (D // 128), axis=1) * (value * gain[...])
         out = out - wide * jnp.concatenate([pull_back] * (D // 128), axis=1)
         found[i // 4, i % 4] = out.astype(BF)
+        grad_store(i).start()
         return carry
 
+    def grad_store(i):
+        at = (i // 4, i % 4)
+        return pltpu.make_async_copy(found.at[at], grad_hbm.at[at], local_sems.at[6])
+
     lax.fori_loop(0, 16, grad_rows, 0)
-    grad_store = pltpu.make_async_copy(found, grad_hbm, local_sems.at[0])
-    grad_store.start()
     metas_out[...] = metas[...]
-    for h in range(2):
-        head_store(TG_TURNS - 1, h).wait()
+    for n in (HEAD_TILES - 2, HEAD_TILES - 1):
+        head_store(n).wait()
 
     def drain(j, carry):
         cols = place.tile_cols(j)
-        Flow(2, j).sent(sz.at[j])
-        Flow(3, j).sent(sy.at[j])
+        Flow(3, j).sent(sz.at[j])
+        Flow(4, j).sent(sy.at[j])
         for _ in range(3):
-            Flow(4, j).sent(up.at[0, 0, :, cols])
-        Flow(5, j).sent(up.at[:, 0:3, :, cols])
-        Flow(6, j).sent(up.at[:, :, :, cols])
+            Flow(5, j).sent(up.at[0, 0, :, cols])
+        Flow(6, j).sent(up.at[:, 0:3, :, cols])
+        Flow(7, j).sent(up.at[:, :, :, cols])
         return carry
 
     lax.fori_loop(0, NT_COLS, drain, 0)
     for j in (NT_COLS - 2, NT_COLS - 1):
         Flow(0, j).sent(snd.at[j % 2])
         Flow(1, j).sent(sx.at[j % 2])
+        Flow(2, j).sent(s_two.at[j % 2])
     post.close()
     gain_item.wait_recv()
     gain_out[...] = gain_in[0] + gain_in[1] + gain_in[2] + gain_in[3]
-    grad_store.wait()
+    pltpu.make_async_copy(found, grad_hbm, local_sems.at[6]).wait()
 
 
 def deliver_kernel(*refs):
@@ -845,13 +956,14 @@
         out_specs=(any_, vmem, any_, any_, vmem, vmem, any_),
         scratch_shapes=[
             V((ROWS, D), BF),
-            V((1024, D), BF),
+            V((1024 + 2 * ALL_SLOTS, D), BF),
             V((4, 8, 256), jnp.int32),
             V((1, D), F32),
-            V((ROWS, 1024), BF),
+            V((ROWS, 1024 + 2 * ALL_SLOTS), BF),
             V((4, 2, 256), F32),
-            V((16, 4, 2, 256), F32),
+            V((24, 4, 2, 256), F32),
             V((1024, 128), F32),
+            V((256, 128), F32),
             V((256, 128), F32),
             V((256, 128), F32),
             V((2, 2048, W), BF),
@@ -865,13 +977,15 @@
             V((4, SLOTS, D), BF),
             V((4, SLOTS, D), BF),
             V((4, SLOTS, D), BF),
-            V((4, SLOTS, D), BF),
             V((2, 2048, W), F32),
             V((2, 4, 4, 4, 16, W), I16),
             V((4, 4, 4, 4, 16, W), I16),
-            V((2, 3, 4, 4, 16, W), I16),
-            V((n, 3, 4, 4, 16, W), I16),
+            V((2, 2, 4, 4, 16, W), I16),
+            V((n, 2, 4, 4, 16, W), I16),
+            V((2, 4, 4, 16, W), I16),
+            V((n, 4, 4, 16, W), I16),
             V((n, 4, 4, 16, W), F32),
+            V((3, 4, 4, 16, W), F32),
             V((n, 3, 4, 16, W), I16),
             V((n, 3, 4, 16, W), I16),
             V((n, 4, 16, W), F32),
@@ -879,9 +993,9 @@
             V((n, 3, 16, W), I16),
             V((4, 4, 16, D), I16),
             V((4, D // 128, 128), F32),
-            dma((5,)),
-            dma((48,)),
-            dma((48,)),
+            dma((7,)),
+            dma((96,)),
+            dma((96,)),
             dma((STEPS, n)),
             dma((STEPS, n)),
         ],

time: 142 us -> 134 us (0.944)
  Pallas kernels: 138 us -> 130 us
    pallas_call x1, Pallas kernels: 125 us -> 117 us  [body(): pl.pallas_call(main_kernel, out_shape=(S((ROWS, D), BF), S((4, 8, 256), j...]
where the time goes in v4:
time: 134 us; the launch traced here: 133 us
  Pallas kernels  130 us (97%)
  local copies, waits for them, and re-layouts  1.81 us (1%)
    pallas_call x1, Pallas kernels, body(): pl.pallas_call(main_kernel, out_shape=(S((ROWS, D), BF), S((4, 8, 256), j...  117 us
    pallas_call x1, Pallas kernels, body(): pl.pallas_call(deliver_kernel, out_shape=(S((256, D), BF), S((256, D), BF...  12.7 us

profile of v4, /device:TPU:1, one launch (start us, length us, event | category | flops | bytes accessed | tf_op | source)
XLA Modules:
  0.0 133.4 jit_solution(17343186458591681009)
XLA Ops:
  0.6 117.3 %main.1 = (bf16[2000,3584]{1,0:T(8,128)(2,1)}, s32[4,8,256]{2,1,0:T(8,128)S(1)}, bf16[4,4,16,3584]{3,2,1,0:T(8,128)(2,1)}, bf16[4,4,16,3584]{3,2,1,0:T(8,128)(2,...) custom-call(s32[1,256]{1,0:T(1,128)} %bitcast.32, s32[1,256]{1,0:T(1,128)} %bitcast.33, ...), custom_call_target="tpu_custom_call" | custom-call | tf_op jit(solution)/shard_map/main/pallas_call | solution.py:944
  118.0 1.2 fusion.6
  119.8 0.2 conditional.1
  120.1 0.0 copy-start.2
  120.1 12.7 %deliver.1 = (bf16[256,3584]{1,0:T(8,128)(2,1)}, bf16[256,3584]{1,0:T(8,128)(2,1)}, bf16[2000,3584]{1,0:T(8,128)(2,1)}) custom-call(bf16[256,3584]{1,0:T(8,128)(2,1)} %get-tuple-element.38.refs_0_, bf16[256,3584]{1,0:T(8,128)(2,1)} %bitcast.24, bf16[2000,3584]{1,0:T(8,128)(2,1)} %get-tuple-element.40.refs_2_), custom_call_target="tpu_custom_call" | custom-call | tf_op jit(solution)/shard_map/deliver/pallas_call | solution.py:1021
  132.8 0.0 copy-done.2
  132.8 0.6 copy.25
Async XLA Ops:
  120.1 12.8 %copy-start.2 = (f32[28,128]{1,0:T(8,128)S(1)}, f32[28,128]{1,0:T(8,128)}, u32[]{:S(2)}) copy-start(f32[28,128]{1,0:T(8,128)} %get-tuple-element.43) | copy-start | bytes 43012

commit v5 on v4

--- a/solution.py
+++ b/solution.py
@@ -128,7 +128,8 @@
             ).start()
 
     def wait_send(self):
-        for _ in range(self.times):
+        times, self.times = self.times, 0
+        for _ in range(times):
             like = self.out_like()
             pltpu.make_async_copy(like, like, self.sems[0].at[self.at]).wait()
 
@@ -231,32 +232,32 @@
         first.wait_recv()
         second = post.group([(row, row, peer) for peer in place.a_peers], rows, rows)
         sends.append(second)
-        agenda.add(14.0, lambda: across(second))
+        agenda.add(9.0, lambda: across(second))
 
     def across(second):
         second.wait_recv()
         third = post.send(half, half, place.core)
         sends.append(third)
-        agenda.add(5.0, lambda: finish(third))
+        agenda.add(4.0, lambda: finish(third))
 
     def finish(third):
         third.wait_recv()
         done()
 
-    agenda.add(8.0, along_a)
+    agenda.add(13.0, along_a)
 
 
 STEPS = 8
 LAG = (1, 3, 5)
-TAIL_AT = ((1, 2), (4, 2), (6, 1), (8, 1), (10, 1), (12, 1), (14, 1), (15, 1))
+TAIL_AT = ((1, 2), (4, 2), (6, 1), (8, 1), (10, 1), (12, 1), (14, 0), (15, 0))
 HEAD_TILES = 2 * NT_COLS
 TAIL = TAIL_AT[-1][0] + 1
 
 
 def main_kernel(
-    own_ids, own_targets, own_mask, hidden, gain_in_rows, table_hbm, cot_hbm,
+    ids_hbm, targets_hbm, mask_hbm, hidden_hbm, gain_hbm, table_hbm, cot_hbm,
     head_hbm, metas_out, embed_hbm, grad_hbm, gain_out, loss_out, cap_hbm,
-    table, normed, metas, gain, marks, stats, stat_in, scale_rows, back_rows, inverses, dots,
+    table, normed, metas, own_lines, hidden, gain_rows, gain, marks, stats, stat_in, scale_rows, back_rows, inverses, dots,
     d_stage, d_part, d_rc, d_rx, d_rz, found, owner_of, slot_of, packed, lines, cot_packed,
     stage, snd, rc, sx, rx, s_two, r_two, acc, acc_two, sz, rz, acc_z, sy, ry, up,
     gain_in, local_sems, send_sems, recv_sems, flow_send, flow_recv,
@@ -268,16 +269,26 @@
     a, b, c, o, g, y = place.a, place.b, place.c, place.o, place.g, place.y
     blocks = [g, place.ga, place.gb, place.gc]
     entered = place.meet()
+    early = [
+        pltpu.make_async_copy(hidden_hbm, hidden, local_sems.at[7]),
+        pltpu.make_async_copy(gain_hbm, gain_rows, local_sems.at[8]),
+    ]
+    for n, ref in enumerate((ids_hbm, targets_hbm, mask_hbm)):
+        early.append(pltpu.make_async_copy(ref, own_lines.at[n], local_sems.at[9 + n]))
+    for copy in early:
+        copy.start()
     def table_load(i):
         rows = pl.ds(i * 1024, 1024 - 48 * i)
         return pltpu.make_async_copy(table_hbm.at[rows], table.at[rows], local_sems.at[5 * i])
 
     table_load(0).start()
     table_load(1).start()
-    metas[g, 0:1, :] = own_ids[...]
-    metas[g, 1:2, :] = own_targets[...]
-    metas[g, 2:3, :] = own_mask[...]
-    gain[...] = jnp.concatenate([gain_in_rows[i : i + 1, :] for i in range(D // 128)], axis=1)
+    for copy in early[1:]:
+        copy.wait()
+    for n in range(3):
+        metas[g, n : n + 1, :] = own_lines[n]
+    gain[...] = jnp.concatenate([gain_rows[i : i + 1, :] for i in range(D // 128)], axis=1)
+    early[0].wait()
     cot_load = pltpu.make_async_copy(cot_hbm, found, local_sems.at[3])
     cot_load.start()
 
@@ -321,7 +332,7 @@
         lambda: metas.at[place.gc],
     )
     spread = {"a": [], "b": [], "c": []}
-    relays = []
+    c_low, c_high = [], []
 
     def swap(block):
         def part():
@@ -346,7 +357,7 @@
             stage.at[n, pl.ds(0, ROWS)], cap_hbm.at[n], local_sems.at[1 + n]
         )
 
-    def forward(n, block, between):
+    def forward(n, block, between, later=None):
         side = n % 2
         rows = normed[rows_of(block, 0, 256), :]
         total = jnp.zeros((1, 256), F32)
@@ -354,6 +365,8 @@
         for at in range(0, ROWS, MF):
             if at == 4 * MF:
                 between()
+            if at == 6 * MF and later is not None:
+                later()
             size = min(MF, ROWS - at)
             logits = lax.dot_general(table[at : at + size, :], rows, NT, preferred_element_type=F32)
             capped = SOFTCAP * jnp.tanh(logits * (1.0 / SOFTCAP))
@@ -374,22 +387,21 @@
         meta_c.start()
         for part in both:
             a_low[part].wait_recv()
+            c_low.append(ship(place.ga, part, 0, place.y_b))
+            spread["a"] += [ship(place.ga, part, 0, peer) for peer in place.near[part]]
+        for part in both:
             b_high[part].wait_recv()
-            relays.append(
-                (ship(place.ga, part, 0, place.y_b), ship(place.gb, part, 1, place.y_a))
-            )
-        spread_piece("a", place.ga, 0, seen)
+            c_high.append(ship(place.gb, part, 1, place.y_a))
 
     table_load(0).wait()
-    forward(0, g, pass_on)
+    forward(0, g, pass_on, lambda: spread_piece("a", place.ga, 1, a_high))
     cap_store(0).start()
-    spread_piece("a", place.ga, 1, a_high)
 
     meta_c.wait_recv()
     ids = [metas[k, 0:1, :] for k in range(4)]
     locals_ = [row - first_row for row in ids]
     for k in range(4):
-        locals_.append(own_ids[...] - place.first_row_of(k))
+        locals_.append(own_lines[0] - place.first_row_of(k))
     owned = [jnp.where((row >= 0) & (row < ROWS), 1.0, 0.0) for row in locals_]
     later = lax.broadcasted_iota(jnp.int32, (256, 256), 0) < lax.broadcasted_iota(
         jnp.int32, (256, 256), 1
@@ -443,9 +455,6 @@
 
     lax.fori_loop(0, NV, mark, 0)
 
-    spread_piece("b", place.gb, 1, seen)
-    spread_piece("b", place.gb, 0, b_low)
-
     def look_up(j, carry):
         cols = pl.ds(pl.multiple_of(j * 2 * W, 128), 2 * W)
         rows = lax.dot_general(owner_of[...], table[:, cols], TN, preferred_element_type=F32)
@@ -460,10 +469,12 @@
         ]
         return post.group(parts, lambda: src.at[0:3], lambda: dst.at[0:3])
 
+    spread_piece("b", place.gb, 1, seen)
+    spread_piece("b", place.gb, 0, b_low)
     lax.fori_loop(0, EARLY, look_up, 0)
-    spread_piece("c", place.gc, 0, [pair[0] for pair in relays])
-    spread_piece("c", place.gc, 1, [pair[1] for pair in relays])
     swap_block("a")
+    spread_piece("c", place.gc, 0, c_low)
+    spread_piece("c", place.gc, 1, c_high)
     lax.fori_loop(EARLY, NT_COLS, look_up, 0)
     line_item = exchange(packed, lines)
 
@@ -714,31 +725,28 @@
         Flow(2, j).start([(s_two.at[j % 2], r_two.at[j], place._at(second, b))])
         acc[j] = acc[j] + decode(rx[j, 0])
 
+    def along_y(j):
+        Flow(2, j).here(r_two.at[j])
+        acc_z[j] = acc[j, g] + decode(r_two[j, g])
+        parts = []
+        for n, peer in enumerate(place.y_peers):
+            at = place.y_at[n]
+            sz[j, n] = encode(acc[j, at] + decode(r_two[j, at]))
+            parts.append((sz.at[j, n], rz.at[j, n], peer))
+        Flow(3, j).start(parts)
+
     def along_b(j):
-        Flow(2, j).here(r_two.at[j])
-        parts = []
-        for n in range(4):
-            at = (b + n) % 4
-            value = acc[j, :, at] + decode(r_two[j, :, at])
-            if n == 0:
-                acc_z[j] = value
-            else:
-                sz[j, n - 1] = encode(value)
-                parts.append((sz.at[j, n - 1], rz.at[j, n - 1], place.b_peers[n - 1]))
-        Flow(3, j).start(parts)
-
-    def along_y(j):
         Flow(3, j).here(rz.at[j])
         acc_z[j] = acc_z[j] + decode(rz[j, 0]) + decode(rz[j, 1]) + decode(rz[j, 2])
         parts = []
-        for n, peer in enumerate(place.y_peers):
-            sy[j, n] = encode(acc_z[j, place.y_at[n]])
+        for n, peer in enumerate(place.b_peers):
+            sy[j, n] = encode(acc_z[j, place.b_at[n]])
             parts.append((sy.at[j, n], ry.at[j, n], peer))
         Flow(4, j).start(parts)
 
     def give_b(j):
         Flow(4, j).here(ry.at[j])
-        value = acc_z[j, g] + decode(ry[j, 0]) + decode(ry[j, 1]) + decode(ry[j, 2])
+        value = acc_z[j, b] + decode(ry[j, 0]) + decode(ry[j, 1]) + decode(ry[j, 2])
         cols = place.tile_cols(j)
         up[b, a, :, cols] = encode(value)
         part = up.at[b, a, :, cols]
@@ -771,7 +779,7 @@
                     product * inv, axis=0, keepdims=True
                 )
 
-    steps = (merge, second_half, along_b, along_y, give_b, give_a, give_core, last)
+    steps = (merge, second_half, along_y, along_b, give_b, give_a, give_core, last)
 
     def head_store(n):
         cols = pl.ds(pl.multiple_of(n * W, 128), W)
@@ -813,12 +821,23 @@
     cot_item.wait_recv()
     normed[1152:1280, :] = normed[1024:1152, :]
 
+    agenda.add(22.0, post.close)
+
     def tail(t, carry):
         @pl.when(t < HEAD_TILES)
         def _():
             head_tile(t)
 
         for n, ((at, pace), step) in enumerate(zip(TAIL_AT, steps)):
+            if pace == 0:
+                for q in range(2):
+                    j = NT_COLS - 1 - 2 * (at - t) + q
+
+                    @pl.when((j >= 0) & (j < NT_COLS))
+                    def _():
+                        step(j)
+
+                continue
             begun = NT_COLS - LAG[n] if n < len(LAG) else 0
             ahead = at - t
             j = NT_COLS - 1 - ahead // pace
@@ -849,7 +868,6 @@
         lambda: gain_in.at[0:3],
         lambda: gain_in.at[0:3],
     )
-    embed_store().wait()
 
     def grad_rows(i, carry):
         value, wide, inv = upstream(i)
@@ -858,13 +876,9 @@
         pull_back = inv * inv * inv * mean_dot
         out = jnp.concatenate([inv] * (D // 128), axis=1) * (value * gain[...])
         out = out - wide * jnp.concatenate([pull_back] * (D // 128), axis=1)
-        found[i // 4, i % 4] = out.astype(BF)
-        grad_store(i).start()
+        normed[rows, :] = out.astype(BF)
+        pltpu.make_async_copy(normed.at[rows], grad_hbm.at[rows], local_sems.at[6]).start()
         return carry
-
-    def grad_store(i):
-        at = (i // 4, i % 4)
-        return pltpu.make_async_copy(found.at[at], grad_hbm.at[at], local_sems.at[6])
 
     lax.fori_loop(0, 16, grad_rows, 0)
     metas_out[...] = metas[...]
@@ -889,7 +903,8 @@
     post.close()
     gain_item.wait_recv()
     gain_out[...] = gain_in[0] + gain_in[1] + gain_in[2] + gain_in[3]
-    pltpu.make_async_copy(found, grad_hbm, local_sems.at[6]).wait()
+    embed_store().wait()
+    pltpu.make_async_copy(normed.at[pl.ds(0, 256)], grad_hbm, local_sems.at[6]).wait()
 
 
 def deliver_kernel(*refs):
@@ -947,17 +962,20 @@
             S((ROWS, D), BF),
             S((4, 8, 256), jnp.int32),
             S((4, 4, 16, D), BF),
-            S((4, 4, 16, D), BF),
+            S((256, D), BF),
             S((D // 128, 128), F32),
             S((16, 128), F32),
             S((2, ROWS, 256), F32),
         ),
-        in_specs=[vmem, vmem, vmem, vmem, vmem, any_, any_],
+        in_specs=[any_] * 7,
         out_specs=(any_, vmem, any_, any_, vmem, vmem, any_),
         scratch_shapes=[
             V((ROWS, D), BF),
             V((1024 + 2 * ALL_SLOTS, D), BF),
             V((4, 8, 256), jnp.int32),
+            V((3, 1, 256), jnp.int32),
+            V((256, D), BF),
+            V((D // 128, 128), F32),
             V((1, D), F32),
             V((ROWS, 1024 + 2 * ALL_SLOTS), BF),
             V((4, 2, 256), F32),
@@ -993,7 +1011,7 @@
             V((n, 3, 16, W), I16),
             V((4, 4, 16, D), I16),
             V((4, D // 128, 128), F32),
-            dma((7,)),
+            dma((12,)),
             dma((96,)),
             dma((96,)),
             dma((STEPS, n)),
@@ -1026,7 +1044,7 @@
         scratch_shapes=[V((2, 256, D), BF), V((ROWS, D), BF), dma((2 + NV,))],
         compiler_params=pltpu.CompilerParams(vmem_limit_bytes=VMEM_LIMIT),
         name="deliver",
-    )(embedded, grad.reshape(256, D), table_grad)
+    )(embedded, grad, table_grad)
     return (embedded, loss[0, 0], grad_hidden, gain_grad.reshape(D), table_grad)
 
 

time: 134 us -> 127 us (0.948)
  Pallas kernels: 130 us -> 123 us
    pallas_call x1, Pallas kernels: 117 us -> 110 us  [body(): pl.pallas_call(main_kernel, out_shape=(S((ROWS, D), BF), S((4, 8, 256), j...]
where the time goes in v5:
time: 127 us; the launch traced here: 126 us
  Pallas kernels  123 us (97%)
  local copies, waits for them, and re-layouts  1.81 us (1%)
  between operations  1.33 us (1%)
    pallas_call x1, Pallas kernels, body(): pl.pallas_call(main_kernel, out_shape=(S((ROWS, D), BF), S((4, 8, 256), j...  110 us
    pallas_call x1, Pallas kernels, body(): pl.pallas_call(deliver_kernel, out_shape=(S((256, D), BF), S((256, D), BF...  12.7 us

profile of v5, /device:TPU:1, one launch (start us, length us, event | category | flops | bytes accessed | tf_op | source)
XLA Modules:
  0.0 126.4 jit_solution(14258320365223716248)
XLA Ops:
  0.6 110.3 %main.1 = (bf16[2000,3584]{1,0:T(8,128)(2,1)}, s32[4,8,256]{2,1,0:T(8,128)S(1)}, bf16[4,4,16,3584]{3,2,1,0:T(8,128)(2,1)}, bf16[256,3584]{1,0:T(8,128)(2,1)}, f3...) custom-call(s32[1,256]{1,0:T(1,128)} %bitcast.30, s32[1,256]{1,0:T(1,128)} %bitcast.31, ...), custom_call_target="tpu_custom_call" | custom-call | tf_op jit(solution)/shard_map/main/pallas_call | solution.py:959
  111.0 1.2 fusion.6
  112.8 0.2 conditional.1
  113.1 0.0 copy-start.2
  113.1 12.7 %deliver.1 = (bf16[256,3584]{1,0:T(8,128)(2,1)}, bf16[256,3584]{1,0:T(8,128)(2,1)}, bf16[2000,3584]{1,0:T(8,128)(2,1)}) custom-call(bf16[256,3584]{1,0:T(8,128)(2,1)} %get-tuple-element.38.refs_0_, bf16[256,3584]{1,0:T(8,128)(2,1)} %get-tuple-element.39.refs_1_, bf16[2000,3584]{1,0:T(8,128)(2,1)} %get-tuple-element.40.refs_2_), custom_call_target="tpu_custom_call" | custom-call | tf_op jit(solution)/shard_map/deliver/pallas_call | solution.py:1039
  125.8 0.0 copy-done.2
  125.8 0.6 copy.25
Async XLA Ops:
  113.1 12.8 %copy-start.2 = (f32[28,128]{1,0:T(8,128)S(1)}, f32[28,128]{1,0:T(8,128)}, u32[]{:S(2)}) copy-start(f32[28,128]{1,0:T(8,128)} %get-tuple-element.43) | copy-start | bytes 43012

commit v6 on v5

--- a/solution.py
+++ b/solution.py
@@ -47,6 +47,11 @@
 def decode(code):
     wide = code.astype(jnp.int32).astype(F32)
     return wide - jnp.clip(wide, -KNEE * FINE, KNEE * FINE) * (1.0 - 1.0 / FINE)
+
+
+def bend(capped):
+    ratio = capped * (1.0 / SOFTCAP)
+    return 1.0 - ratio * ratio
 
 
 def gray(i):
@@ -116,8 +121,8 @@
         self.sems, self.at, self.parts = sems, at, parts
         self.out_like, self.in_like, self.times = out_like, in_like, times
 
-    def start(self):
-        for src, dst, peer in self.parts:
+    def start(self, parts=None):
+        for src, dst, peer in self.parts if parts is None else parts:
             pltpu.make_async_remote_copy(
                 src_ref=src(),
                 dst_ref=dst(),
@@ -247,6 +252,7 @@
     agenda.add(13.0, along_a)
 
 
+POSTS = 32
 STEPS = 8
 LAG = (1, 3, 5)
 TAIL_AT = ((1, 2), (4, 2), (6, 1), (8, 1), (10, 1), (12, 1), (14, 0), (15, 0))
@@ -256,8 +262,8 @@
 
 def main_kernel(
     ids_hbm, targets_hbm, mask_hbm, hidden_hbm, gain_hbm, table_hbm, cot_hbm,
-    head_hbm, metas_out, embed_hbm, grad_hbm, gain_out, loss_out, cap_hbm,
-    table, normed, metas, own_lines, hidden, gain_rows, gain, marks, stats, stat_in, scale_rows, back_rows, inverses, dots,
+    head_hbm, metas_hbm, embed_hbm, grad_hbm, gain_sum_hbm, loss_hbm, most_hbm, cap_hbm,
+    table, normed, metas, own_lines, scalars, hidden, gain_rows, gain, marks, stats, stat_in, scale_rows, back_rows, inverses, dots,
     d_stage, d_part, d_rc, d_rx, d_rz, found, owner_of, slot_of, packed, lines, cot_packed,
     stage, snd, rc, sx, rx, s_two, r_two, acc, acc_two, sz, rz, acc_z, sy, ry, up,
     gain_in, local_sems, send_sems, recv_sems, flow_send, flow_recv,
@@ -311,11 +317,15 @@
     stats[...] = jnp.zeros_like(stats)
     entered()
 
-    def ship(block, part, half, peer):
+    def piece(block, part, half):
         def rows():
             at = place.colours[part] * 64 + half * 32
             return normed.at[rows_of(block, at, 32), place.parts[part]]
 
+        return rows
+
+    def ship(block, part, half, peer):
+        rows = piece(block, part, half)
         return post.send(rows, rows, peer)
 
     meta_in = [
@@ -331,7 +341,10 @@
         lambda: metas.at[place.ga],
         lambda: metas.at[place.gc],
     )
-    spread = {"a": [], "b": [], "c": []}
+    def pieces():
+        return normed.at[pl.ds(0, 12 * 32), place.parts[0]]
+
+    spread = {name: post.plan([], pieces, pieces) for name in "abc"}
     c_low, c_high = [], []
 
     def swap(block):
@@ -342,14 +355,17 @@
 
     swaps = {"a": swap(place.ga), "b": swap(place.gb), "c": swap(place.gc)}
 
+    def pass_piece(name, block, part, half):
+        rows = piece(block, part, half)
+        spread[name].start([(rows, rows, peer) for peer in place.near[part]])
+
     def spread_piece(name, block, half, items):
         for part, item in enumerate(items):
             item.wait_recv()
-            spread[name] += [ship(block, part, half, peer) for peer in place.near[part]]
+            pass_piece(name, block, part, half)
 
     def swap_block(name):
-        for item in spread[name]:
-            item.wait_recv()
+        spread[name].wait_recv()
         swaps[name].start()
 
     def cap_store(n):
@@ -370,10 +386,11 @@
             size = min(MF, ROWS - at)
             logits = lax.dot_general(table[at : at + size, :], rows, NT, preferred_element_type=F32)
             capped = SOFTCAP * jnp.tanh(logits * (1.0 / SOFTCAP))
-            stage[side, at : at + size] = capped
+            raised = jnp.exp(capped)
+            stage[side, at : at + size] = raised * bend(capped)
             ids = lax.broadcasted_iota(jnp.int32, capped.shape, 0) + (first_row + at)
             hit = ids == metas[block, 1:2, :]
-            total += jnp.sum(jnp.exp(capped), axis=0, keepdims=True)
+            total += jnp.sum(raised, axis=0, keepdims=True)
             picked += jnp.sum(jnp.where(hit, capped, 0.0), axis=0, keepdims=True)
         stats[block, 0:1, :] = total
         stats[block, 1:2, :] = picked
@@ -388,7 +405,7 @@
         for part in both:
             a_low[part].wait_recv()
             c_low.append(ship(place.ga, part, 0, place.y_b))
-            spread["a"] += [ship(place.ga, part, 0, peer) for peer in place.near[part]]
+            pass_piece("a", place.ga, part, 0)
         for part in both:
             b_high[part].wait_recv()
             c_high.append(ship(place.gb, part, 1, place.y_a))
@@ -611,15 +628,14 @@
         weight = metas[block, 2:3, :].astype(F32)
         factor = weight / stats[block, 0:1, :]
         target = metas[block, 1:2, :]
+        taken = weight * bend(stats[block, 1:2, :])
         lanes = pl.ds(pl.multiple_of(block * 256, 128), 256)
 
         def slab(i, carry):
             rows = pl.ds(pl.multiple_of(i * MT, 16), MT)
             ids = lax.broadcasted_iota(jnp.int32, (MT, 256), 0) + (first_row + i * MT)
-            capped = stage[side, rows, :]
-            hit = jnp.where(ids == target, weight, 0.0)
-            ratio = capped * (1.0 / SOFTCAP)
-            value = (jnp.exp(capped) * factor - hit) * (1.0 - ratio * ratio)
+            hit = jnp.where(ids == target, taken, 0.0)
+            value = stage[side, rows, :] * factor - hit
             marks[rows, lanes] = value.astype(BF)
             return carry
 
@@ -644,13 +660,21 @@
     loss_sum = sum(
         jnp.sum(w * (jnp.log(stats[k, 0:1, :]) - stats[k, 1:2, :])) for k, w in enumerate(weights)
     )
-    loss_out[0:8] = jnp.full((8, 128), loss_sum / jnp.maximum(weight_sum, 1.0), F32)
-    loss_out[8:16] = jnp.full((8, 128), most, F32)
+    scalars[0] = jnp.full((1, 1), loss_sum / jnp.maximum(weight_sum, 1.0), F32)
+    scalars[1] = jnp.full((1, 1), most, F32)
+    small_stores = [
+        pltpu.make_async_copy(scalars.at[0], loss_hbm, local_sems.at[7]),
+        pltpu.make_async_copy(scalars.at[1], most_hbm, local_sems.at[8]),
+        pltpu.make_async_copy(metas, metas_hbm, local_sems.at[9]),
+    ]
+    for copy in small_stores:
+        copy.start()
     shape = (4, 4, 4, 16, W)
 
     class Flow:
         def __init__(self, step, j):
-            self.send_sem, self.recv_sem = flow_send.at[step, j], flow_recv.at[step, j]
+            self.send_sem = flow_send.at[2 * step + j % 2 if step < 3 else step + 3]
+            self.recv_sem = flow_recv.at[step, j]
 
         def start(self, parts):
             for src, dst, peer in parts:
@@ -850,6 +874,16 @@
         return carry
 
     lax.fori_loop(0, TAIL, tail, 0)
+
+    def gain_part():
+        return gain_in.at[y]
+
+    gain_item = post.group(
+        [(gain_part, gain_part, peer) for peer in place.y_peers],
+        lambda: gain_in.at[0:3],
+        lambda: gain_in.at[0:3],
+    )
+
     agenda.run()
 
     GR = 16
@@ -859,15 +893,6 @@
         down = back_rows[rows, :]
         value = decode(up[i // 4, i % 4]) * jnp.concatenate([down] * (D // 128), axis=1)
         return value, hidden[rows, :].astype(F32), inverses[rows, :]
-
-    def gain_part():
-        return gain_in.at[y]
-
-    gain_item = post.group(
-        [(gain_part, gain_part, peer) for peer in place.y_peers],
-        lambda: gain_in.at[0:3],
-        lambda: gain_in.at[0:3],
-    )
 
     def grad_rows(i, carry):
         value, wide, inv = upstream(i)
@@ -881,38 +906,37 @@
         return carry
 
     lax.fori_loop(0, 16, grad_rows, 0)
-    metas_out[...] = metas[...]
+    for copy in small_stores:
+        copy.wait()
     for n in (HEAD_TILES - 2, HEAD_TILES - 1):
         head_store(n).wait()
 
-    def drain(j, carry):
-        cols = place.tile_cols(j)
-        Flow(3, j).sent(sz.at[j])
-        Flow(4, j).sent(sy.at[j])
-        for _ in range(3):
-            Flow(5, j).sent(up.at[0, 0, :, cols])
-        Flow(6, j).sent(up.at[:, 0:3, :, cols])
-        Flow(7, j).sent(up.at[:, :, :, cols])
-        return carry
-
-    lax.fori_loop(0, NT_COLS, drain, 0)
+    Flow(3, 0).sent(sz)
+    Flow(4, 0).sent(sy)
+    Flow(5, 0).sent(up.at[0:3, 0, :, place.cols])
+    Flow(6, 0).sent(up.at[:, 0:3, :, place.cols])
+    Flow(7, 0).sent(up.at[:, :, :, place.cols])
     for j in (NT_COLS - 2, NT_COLS - 1):
         Flow(0, j).sent(snd.at[j % 2])
         Flow(1, j).sent(sx.at[j % 2])
         Flow(2, j).sent(s_two.at[j % 2])
     post.close()
     gain_item.wait_recv()
-    gain_out[...] = gain_in[0] + gain_in[1] + gain_in[2] + gain_in[3]
+    gain_rows[...] = gain_in[0] + gain_in[1] + gain_in[2] + gain_in[3]
+    gain_store = pltpu.make_async_copy(gain_rows, gain_sum_hbm, local_sems.at[10])
+    gain_store.start()
+    gain_store.wait()
     embed_store().wait()
     pltpu.make_async_copy(normed.at[pl.ds(0, 256)], grad_hbm, local_sems.at[6]).wait()
 
 
 def deliver_kernel(*refs):
-    ins, outs, (small, large, sems) = refs[:3], refs[3:6], refs[6:]
-    moves = [(ins[n], outs[n], small.at[n], n) for n in range(2)]
+    ins, outs, (small, large, line, sems) = refs[:4], refs[4:8], refs[8:]
+    moves = [(ins[0], outs[0], line, 0)]
+    moves += [(ins[n], outs[n], small.at[n - 1], n) for n in (1, 2)]
     for i in range(NV):
         rows = pl.ds(i * MT, MT)
-        moves.append((ins[2].at[rows], outs[2].at[rows], large.at[rows], 2 + i))
+        moves.append((ins[3].at[rows], outs[3].at[rows], large.at[rows], 3 + i))
     for src, _, buf, n in moves:
         pltpu.make_async_copy(src, buf, sems.at[n]).start()
     for src, dst, buf, n in moves:
@@ -956,7 +980,7 @@
     S = jax.ShapeDtypeStruct
     gain = norm_gain.reshape(D // 128, 128)
     n = NT_COLS
-    head, metas, embed, grad, gain_grad, loss, _ = pl.pallas_call(
+    head, metas, embed, grad, gain_grad, loss, most, _ = pl.pallas_call(
         main_kernel,
         out_shape=(
             S((ROWS, D), BF),
@@ -964,16 +988,18 @@
             S((4, 4, 16, D), BF),
             S((256, D), BF),
             S((D // 128, 128), F32),
-            S((16, 128), F32),
+            S((1, 1), F32),
+            S((1, 1), F32),
             S((2, ROWS, 256), F32),
         ),
         in_specs=[any_] * 7,
-        out_specs=(any_, vmem, any_, any_, vmem, vmem, any_),
+        out_specs=(any_,) * 8,
         scratch_shapes=[
             V((ROWS, D), BF),
             V((1024 + 2 * ALL_SLOTS, D), BF),
             V((4, 8, 256), jnp.int32),
             V((3, 1, 256), jnp.int32),
+            V((2, 1, 1), F32),
             V((256, D), BF),
             V((D // 128, 128), F32),
             V((1, D), F32),
@@ -1012,9 +1038,9 @@
             V((4, 4, 16, D), I16),
             V((4, D // 128, 128), F32),
             dma((12,)),
-            dma((96,)),
-            dma((96,)),
-            dma((STEPS, n)),
+            dma((POSTS,)),
+            dma((POSTS,)),
+            dma((STEPS + 3,)),
             dma((STEPS, n)),
         ],
         compiler_params=pltpu.CompilerParams(
@@ -1032,20 +1058,25 @@
     )
 
     embedded, table_grad = lax.cond(
-        loss[8, 0] > SLOTS,
+        most.reshape(()) > SLOTS,
         lambda: dense_embedding(metas[:, 0, :].reshape(1024), embed_cotangent, table, head),
         lambda: (embed.reshape(256, D), head),
     )
-    embedded, grad_hidden, table_grad = pl.pallas_call(
+    gain_grad, embedded, grad_hidden, table_grad = pl.pallas_call(
         deliver_kernel,
-        out_shape=(S((256, D), BF), S((256, D), BF), S((ROWS, D), BF)),
-        in_specs=[any_] * 3,
-        out_specs=(any_,) * 3,
-        scratch_shapes=[V((2, 256, D), BF), V((ROWS, D), BF), dma((2 + NV,))],
+        out_shape=(S((D // 128, 128), F32), S((256, D), BF), S((256, D), BF), S((ROWS, D), BF)),
+        in_specs=[any_] * 4,
+        out_specs=(any_,) * 4,
+        scratch_shapes=[
+            V((2, 256, D), BF),
+            V((ROWS, D), BF),
+            V((D // 128, 128), F32),
+            dma((3 + NV,)),
+        ],
         compiler_params=pltpu.CompilerParams(vmem_limit_bytes=VMEM_LIMIT),
         name="deliver",
-    )(embedded, grad, table_grad)
-    return (embedded, loss[0, 0], grad_hidden, gain_grad.reshape(D), table_grad)
+    )(gain_grad, embedded, grad, table_grad)
+    return (embedded, loss.reshape(()), grad_hidden, gain_grad.reshape(D), table_grad)
 
 
 def solution(mesh):

time: 127 us -> 125 us (0.984)
  Pallas kernels: 123 us -> 121 us
  local copies, waits for them, and re-layouts: 1.81 us -> 0 us
  between operations: 1.33 us -> 2.97 us
    pallas_call x1, Pallas kernels: 110 us -> 108 us  [body(): pl.pallas_call(main_kernel, out_shape=(S((ROWS, D), BF), S((4, 8, 256), j...]
where the time goes in v6:
time: 125 us; the launch traced here: 124 us
  Pallas kernels  121 us (97%)
  between operations  2.97 us (2%)
    pallas_call x1, Pallas kernels, body(): pl.pallas_call(main_kernel, out_shape=(S((ROWS, D), BF), S((4, 8, 256), j...  108 us
    pallas_call x1, Pallas kernels, body(): pl.pallas_call(deliver_kernel, out_shape=(S((D // 128, 128), F32), S((256...  12.8 us

profile of v6, /device:TPU:1, one launch (start us, length us, event | category | flops | bytes accessed | tf_op | source)
XLA Modules:
  0.0 124.4 jit_solution(6824626408168124696)
XLA Ops:
  0.6 108.4 %main.1 = (bf16[2000,3584]{1,0:T(8,128)(2,1)}, s32[4,8,256]{2,1,0:T(8,128)S(1)}, bf16[4,4,16,3584]{3,2,1,0:T(8,128)(2,1)}, bf16[256,3584]{1,0:T(8,128)(2,1)}, f3...) custom-call(s32[1,256]{1,0:T(1,128)} %bitcast.29, s32[1,256]{1,0:T(1,128)} %bitcast.30, ...), custom_call_target="tpu_custom_call" | custom-call | tf_op jit(solution)/shard_map/main/pallas_call | solution.py:983
  109.6 0.2 conditional.1
  109.9 12.8 %deliver.1 = (f32[28,128]{1,0:T(8,128)}, bf16[256,3584]{1,0:T(8,128)(2,1)}, bf16[256,3584]{1,0:T(8,128)(2,1)}, bf16[2000,3584]{1,0:T(8,128)(2,1)}) custom-call(f32[28,128]{1,0:T(8,128)} %get-tuple-element.36.refs_0_, bf16[256,3584]{1,0:T(8,128)(2,1)} %get-tuple-element.41.refs_1_, bf16[256,3584]{1,0:T(8,128)(2,1)} %get-tuple-element.42.refs_2_, ...), custom_call_target="tpu_custom_call" | custom-call | tf_op jit(solution)/shard_map/deliver/pallas_call | solution.py:1065

commit v7 on v6

--- a/solution.py
+++ b/solution.py
@@ -26,6 +26,7 @@
 MT = 400
 MF = 256
 NV = ROWS // MT
+MOVED = 80
 HALF = D // 2
 W = 256
 NT_COLS = HALF // W
@@ -934,8 +935,8 @@
     ins, outs, (small, large, line, sems) = refs[:4], refs[4:8], refs[8:]
     moves = [(ins[0], outs[0], line, 0)]
     moves += [(ins[n], outs[n], small.at[n - 1], n) for n in (1, 2)]
-    for i in range(NV):
-        rows = pl.ds(i * MT, MT)
+    for i in range(ROWS // MOVED):
+        rows = pl.ds(i * MOVED, MOVED)
         moves.append((ins[3].at[rows], outs[3].at[rows], large.at[rows], 3 + i))
     for src, _, buf, n in moves:
         pltpu.make_async_copy(src, buf, sems.at[n]).start()
@@ -1071,7 +1072,7 @@
             V((2, 256, D), BF),
             V((ROWS, D), BF),
             V((D // 128, 128), F32),
-            dma((3 + NV,)),
+            dma((3 + ROWS // MOVED,)),
         ],
         compiler_params=pltpu.CompilerParams(vmem_limit_bytes=VMEM_LIMIT),
         name="deliver",

time: 125 us -> 124 us (level)
  no operation moved by 1% of the time
where the time goes in v7:
time: 124 us
  Pallas kernels  121 us (98%)
  between operations  2.97 us (2%)
    pallas_call x1, Pallas kernels, body(): pl.pallas_call(main_kernel, out_shape=(S((ROWS, D), BF), S((4, 8, 256), j...  108 us
    pallas_call x1, Pallas kernels, body(): pl.pallas_call(deliver_kernel, out_shape=(S((D // 128, 128), F32), S((256...  12.5 us

profile of v7, /device:TPU:1, one launch (start us, length us, event | category | flops | bytes accessed | tf_op | source)
XLA Modules:
  0.0 124.1 jit_solution(2709453059807963460)
XLA Ops:
  0.6 108.4 %main.1 = (bf16[2000,3584]{1,0:T(8,128)(2,1)}, s32[4,8,256]{2,1,0:T(8,128)S(1)}, bf16[4,4,16,3584]{3,2,1,0:T(8,128)(2,1)}, bf16[256,3584]{1,0:T(8,128)(2,1)}, f3...) custom-call(s32[1,256]{1,0:T(1,128)} %bitcast.29, s32[1,256]{1,0:T(1,128)} %bitcast.30, ...), custom_call_target="tpu_custom_call" | custom-call | tf_op jit(solution)/shard_map/main/pallas_call | solution.py:984
  109.6 0.2 conditional.1
  109.9 12.5 %deliver.1 = (f32[28,128]{1,0:T(8,128)}, bf16[256,3584]{1,0:T(8,128)(2,1)}, bf16[256,3584]{1,0:T(8,128)(2,1)}, bf16[2000,3584]{1,0:T(8,128)(2,1)}) custom-call(f32[28,128]{1,0:T(8,128)} %get-tuple-element.36.refs_0_, bf16[256,3584]{1,0:T(8,128)(2,1)} %get-tuple-element.41.refs_1_, bf16[256,3584]{1,0:T(8,128)(2,1)} %get-tuple-element.42.refs_2_, ...), custom_call_target="tpu_custom_call" | custom-call | tf_op jit(solution)/shard_map/deliver/pallas_call | solution.py:1066
